TPU v7x, 128 devices: a whole 4x4x4 slice. The times are simulated.
128 devices in a mesh: lev: 4 (over y), col: 32 (over z, x, core).
Axes of the slice: x: 4, y: 4, z: 4, core: 2. Of those that a mesh axis runs over, the one named last changes fastest.
Arguments:
- control_field: float32 [96, 16, 768, 128], P('lev', None, 'col'), may hold values from -24 to 24
- decay_rate: float32 [96, 768, 128], P('lev', 'col'), may hold values from 0.5 to 0.999
- diffusivity: float32 [768, 128], P('col'), may hold values from 0.08 to 0.24
Outputs:
- localized: float32 [96, 16, 768, 128], P('lev', None, 'col')
All inputs are finite; a program needn't handle non-finite values.
Results may differ from a plain program's by a relative error of at most 0.00002.
Values sent between devices are 32-bit elements; how exact they have to be, the bound alone decides.
No kernel may reach another device: no remote copies, remote signals or barrier semaphores. Data moves between devices by JAX's collectives and lax.ppermute only.
A program may use at most 64 MiB of HBM per device.

v0:
```python
import jax
import jax.numpy as jnp
from jax import lax
from jax.sharding import PartitionSpec as P

SMOOTH = 4


def sent_to_all(x, axis):
    peers = lax.axis_size(axis)
    return lax.all_to_all(jnp.broadcast_to(x[None], (peers, *x.shape)), axis, 0, 0, tiled=True)


def combined_pairwise(pieces, combine):
    while len(jax.tree.leaves(pieces)[0]) > 1:
        pieces = jax.vmap(combine)(
            *(jax.tree.map(lambda part: part[side::2], pieces) for side in (0, 1))
        )
    return jax.tree.map(lambda part: part[0], pieces)


def prefix(x, axis, combine, identity, reverse):
    peers, here = (lax.axis_size(axis), lax.axis_index(axis))
    passed = jnp.arange(peers) > here if reverse else jnp.arange(peers) < here

    def kept(part, zero, own):
        part = jnp.where(
            passed.reshape(-1, *(1 for _ in own.shape)), part, jnp.asarray(zero, own.dtype)
        )
        return part[::-1] if reverse else part

    pieces = jax.tree.map(lambda part: sent_to_all(part, axis), x)
    return combined_pairwise(jax.tree.map(kept, pieces, identity, x), combine)


def with_halo(block, sides, width):
    for axis, dim in sides:
        count = lax.axis_size(axis)
        forward = [(i, i + 1) for i in range(count - 1)]
        backward = [(target, source) for source, target in forward]
        low = lax.ppermute(
            lax.slice_in_dim(block, block.shape[dim] - width, None, axis=dim), axis, forward
        )
        high = lax.ppermute(lax.slice_in_dim(block, 0, width, axis=dim), axis, backward)
        block = jnp.concatenate([low, block, high], axis=dim)
    return block


def sweep_levels(decay_rates, field, backward):
    blocks = field.shape[0] // 8
    rate_blocks = decay_rates.reshape((blocks, 8) + decay_rates.shape[1:])
    field_blocks = field.reshape((blocks, 8) + field.shape[1:])

    def run_block(state, inputs):
        rate_block, values_block = inputs
        results = [None] * 8
        order = range(7, -1, -1) if backward else range(8)
        for position in order:
            weight = rate_block[position]
            state = weight * state + (1.0 - weight) * values_block[position]
            results[position] = state
        return (state, jnp.stack(results))

    start = jnp.zeros(field.shape[1:], jnp.float32)
    unused, swept = lax.scan(run_block, start, (rate_blocks, field_blocks), reverse=backward)
    return swept.reshape(field.shape)


def combine_maps(earlier, later):
    return (later[0] * earlier[0], later[0][None] * earlier[1] + later[1])


def forward_pass(decay_rates, field):
    within = sweep_levels(decay_rates, field, False)
    through = jnp.prod(decay_rates, axis=0)
    identity = (jnp.ones_like(through), jnp.zeros_like(within[-1]))
    entering = prefix((through, within[-1]), "lev", combine_maps, identity, False)
    growth = jnp.cumprod(decay_rates, axis=0)
    return within + growth[:, None] * entering[1][None]


def backward_pass(decay_rates, field):
    within = sweep_levels(decay_rates, field, True)
    through = jnp.prod(decay_rates, axis=0)
    identity = (jnp.ones_like(through), jnp.zeros_like(within[0]))
    entering = prefix((through, within[0]), "lev", combine_maps, identity, True)
    growth = jnp.flip(jnp.cumprod(jnp.flip(decay_rates, 0), axis=0), 0)
    return within + growth[:, None] * entering[1][None]


def lat_sum(field):
    padded = jnp.pad(field, ((0, 0), (0, 0), (0, 0), (1, 1)))
    return padded[..., 2:] + padded[..., :-2]


def per_device(control_field, decay_rate, diffusivity):
    filtered = control_field
    for repeat in range(2):
        filtered = forward_pass(decay_rate, filtered)
        filtered = backward_pass(decay_rate, filtered)
    current = with_halo(filtered, (("col", 2),), SMOOTH)
    kappa_wide = with_halo(diffusivity, (("col", 0),), SMOOTH)
    for position in range(SMOOTH):
        center = current[:, :, 1:-1]
        kappa_part = kappa_wide[position + 1 : kappa_wide.shape[0] - position - 1]
        current = center + kappa_part[None, None] * (
            current[:, :, 2:] + current[:, :, :-2] + lat_sum(center) - 4.0 * center
        )
    return current


def solution(mesh):
    in_specs = (P("lev", None, "col", None), P("lev", "col", None), P("col", None))
    out_specs = P("lev", None, "col", None)
    return jax.shard_map(
        per_device, mesh=mesh, in_specs=in_specs, out_specs=out_specs, check_vma=False
    )
```

profile of v0, /device:TPU:7, one launch (start us, length us, event | category | flops | bytes accessed | tf_op | source)
XLA Modules:
  0.0 229.9 jit_solution(5336159888158184857)
XLA Ops:
  1.7 4.2 %all-to-all-start = ((f32[4,24,128]{2,1,0:T(8,128)}), f32[4,24,128]{2,1,0:T(8,128)S(1)}, u32[]{:S(2)}, u32[]{:S(2)}) async-start(f32[4,24,128]{2,1,0:T(8,128)} %broadcast_in_dim.172), calls=%async_computation | async-start | bytes 98304 | tf_op jit(solution)/shard_map/all_to_all | solution.py:11
  6.9 2.7 %broadcast.243.clone.2 = f32[3,8,16,24,128]{4,3,2,1,0:T(8,128)} broadcast(f32[]{:T(128)} %constant.132.clone.1), dimensions={} | broadcast | bytes 4718596 | tf_op jit(solution)/shard_map/broadcast.12
  9.6 28.4 %while.60 = (s32[]{:T(128)}, f32[16,24,128]{2,1,0:T(8,128)S(1)}, f32[3,8,16,24,128]{4,3,2,1,0:T(8,128)}, f32[3,8,24,128]{3,2,1,0:T(8,128)S(1)}, f32[3,8,16,24,12...) while((s32[]{:T(128)}, f32[16,24,128]{2,1,0:T(8,128)S(1)}, ...), condition=%wide.region_1.2_spmd.clone, body=%wide.region_0.1_spmd.clone.sunk | while | flops 1695753 | bytes 10003275 | solution.py:65
  13.6 1.1 bitcast_dynamic-update-slice_fusion.74
  15.7 1.1 bitcast_dynamic-update-slice_fusion.76
  17.8 1.3 bitcast_dynamic-update-slice_fusion.78
  21.0 1.1 bitcast_dynamic-update-slice_fusion.72
  23.1 1.1 bitcast_dynamic-update-slice_fusion.74
  25.2 1.1 bitcast_dynamic-update-slice_fusion.76
  27.2 1.3 bitcast_dynamic-update-slice_fusion.78
  32.5 1.1 bitcast_dynamic-update-slice_fusion.74
  36.7 1.3 bitcast_dynamic-update-slice_fusion.78
  40.0 4.2 %all-to-all-start.1 = ((f32[4,16,24,128]{3,1,2,0:T(8,128)}), f32[4,16,24,128]{3,1,2,0:T(8,128)S(1)}, u32[]{:S(2)}, u32[]{:S(2)}) async-start(f32[4,16,24,128]{3,1,2,0:T(8,128)} %broadcast_in_dim.176), calls=%async_computation.1 | async-start | bytes 1572864 | tf_op jit(solution)/shard_map/all_to_all | solution.py:11
  44.3 10.8 %all-to-all-done.1 = f32[4,16,24,128]{3,1,2,0:T(8,128)S(1)} async-done(((f32[4,16,24,128]{3,1,2,0:T(8,128)}), f32[4,16,24,128]{3,1,2,0:T(8,128)S(1)}, u32[]{:S(2)}, u32[]{:S(2)}) %all-to-all-start.1) | async-done | bytes 786464 | tf_op jit(solution)/shard_map/all_to_all | solution.py:11
  55.4 5.2 %multiply_add_fusion.3 = f32[3,8,16,24,128]{4,3,2,1,0:T(8,128)} fusion(f32[3,8,16,24,128]{4,3,2,1,0:T(8,128)} %get-tuple-element.265, f32[16,24,128]{2,1,0:T(8,128)S(1)} %copy.7, f32[3,8,24,128]{3,2,1,0:T(8,128)S(1)} %bitcast.578), kind=kLoop, calls=%fused_computation.236 | loop fusion | flops 2359296 | bytes 9928704 | tf_op jit(solution)/shard_map/add | solution.py:79
  60.6 2.7 %broadcast.243.clone.1 = f32[3,8,16,24,128]{4,3,2,1,0:T(8,128)} broadcast(f32[]{:T(128)} %constant.132.clone.1), dimensions={} | broadcast | bytes 4718596 | tf_op jit(solution)/shard_map/broadcast.12
  63.3 18.0 %while.61 = (s32[]{:T(128)}, f32[16,24,128]{2,1,0:T(8,128)S(1)}, f32[3,8,16,24,128]{4,3,2,1,0:T(8,128)}, f32[3,8,24,128]{3,2,1,0:T(8,128)S(1)}, f32[3,8,16,24,12...) while((s32[]{:T(128)}, f32[16,24,128]{2,1,0:T(8,128)S(1)}, ...), condition=%wide.region_5.6_spmd.clone, body=%wide.region_4.5_spmd.clone.sunk | while | flops 1695754 | bytes 10002771 | solution.py:65
  63.3 1.7 bitcast_dynamic-update-slice_fusion.79
  68.0 1.3 bitcast_dynamic-update-slice_fusion.87
  69.3 1.7 bitcast_dynamic-update-slice_fusion.79
  74.0 1.3 bitcast_dynamic-update-slice_fusion.87
  75.3 1.7 bitcast_dynamic-update-slice_fusion.79
  80.0 1.3 bitcast_dynamic-update-slice_fusion.87
  83.2 3.5 %all-to-all-start.2 = ((f32[4,16,24,128]{3,1,2,0:T(8,128)}), f32[4,16,24,128]{3,1,2,0:T(8,128)S(1)}, u32[]{:S(2)}, u32[]{:S(2)}) async-start(f32[4,16,24,128]{3,1,2,0:T(8,128)} %broadcast_in_dim.181), calls=%async_computation.2 | async-start | bytes 1572864 | tf_op jit(solution)/shard_map/all_to_all | solution.py:11
  86.7 1.3 fusion.118
  88.1 8.3 %all-to-all-done.2 = f32[4,16,24,128]{3,1,2,0:T(8,128)S(1)} async-done(((f32[4,16,24,128]{3,1,2,0:T(8,128)}), f32[4,16,24,128]{3,1,2,0:T(8,128)S(1)}, u32[]{:S(2)}, u32[]{:S(2)}) %all-to-all-start.2) | async-done | bytes 786464 | tf_op jit(solution)/shard_map/all_to_all | solution.py:11
  96.8 2.0 copy-done.2
  98.7 2.7 %multiply_add_fusion.2 = f32[3,8,16,24,128]{4,3,2,1,0:T(8,128)} fusion(f32[3,8,16,24,128]{4,3,2,1,0:T(8,128)S(1)} %copy-done.2, f32[16,24,128]{2,1,0:T(8,128)S(1)} %copy.9, f32[3,8,24,128]{3,2,1,0:T(8,128)S(1)} %bitcast.580), kind=kLoop, calls=%fused_computation.235 | loop fusion | flops 2359296 | bytes 9928704 | tf_op jit(solution)/shard_map/add | solution.py:88
  101.4 2.7 %broadcast.243 = f32[3,8,16,24,128]{4,3,2,1,0:T(8,128)} broadcast(f32[]{:T(128)} %constant.132.clone.1), dimensions={} | broadcast | bytes 4718596 | tf_op jit(solution)/shard_map/broadcast.12
  104.2 28.4 %while.62 = (s32[]{:T(128)}, f32[16,24,128]{2,1,0:T(8,128)S(1)}, f32[3,8,16,24,128]{4,3,2,1,0:T(8,128)}, f32[3,8,24,128]{3,2,1,0:T(8,128)S(1)}, f32[3,8,16,24,12...) while((s32[]{:T(128)}, f32[16,24,128]{2,1,0:T(8,128)S(1)}, ...), condition=%wide.region_8.9_spmd.clone, body=%wide.region_7.8_spmd.clone.sunk | while | flops 1695753 | bytes 10003275 | solution.py:65
  106.1 1.1 bitcast_dynamic-update-slice_fusion.90
  108.2 1.1 bitcast_dynamic-update-slice_fusion.92
  110.3 1.1 bitcast_dynamic-update-slice_fusion.94
  112.4 1.3 bitcast_dynamic-update-slice_fusion.96
  115.6 1.1 bitcast_dynamic-update-slice_fusion.90
  117.7 1.1 bitcast_dynamic-update-slice_fusion.92
  119.7 1.1 bitcast_dynamic-update-slice_fusion.94
  121.8 1.3 bitcast_dynamic-update-slice_fusion.96
  125.0 1.1 bitcast_dynamic-update-slice_fusion.90
  127.1 1.1 bitcast_dynamic-update-slice_fusion.92
  129.2 1.1 bitcast_dynamic-update-slice_fusion.94
  131.3 1.3 bitcast_dynamic-update-slice_fusion.96
  134.5 3.5 %all-to-all-start.3 = ((f32[4,16,24,128]{3,1,2,0:T(8,128)}), f32[4,16,24,128]{3,1,2,0:T(8,128)S(1)}, u32[]{:S(2)}, u32[]{:S(2)}) async-start(f32[4,16,24,128]{3,1,2,0:T(8,128)} %broadcast_in_dim.183), calls=%async_computation.3 | async-start | bytes 1572864 | tf_op jit(solution)/shard_map/all_to_all | solution.py:11
  138.0 8.5 %all-to-all-done.3 = f32[4,16,24,128]{3,1,2,0:T(8,128)S(1)} async-done(((f32[4,16,24,128]{3,1,2,0:T(8,128)}), f32[4,16,24,128]{3,1,2,0:T(8,128)S(1)}, u32[]{:S(2)}, u32[]{:S(2)}) %all-to-all-start.3) | async-done | bytes 786464 | tf_op jit(solution)/shard_map/all_to_all | solution.py:11
  146.8 5.2 %multiply_add_fusion.1 = f32[3,8,16,24,128]{4,3,2,1,0:T(8,128)} fusion(f32[3,8,16,24,128]{4,3,2,1,0:T(8,128)} %get-tuple-element.267, f32[16,24,128]{2,1,0:T(8,128)S(1)} %copy.11, f32[3,8,24,128]{3,2,1,0:T(8,128)S(1)} %bitcast.579), kind=kLoop, calls=%fused_computation.234 | loop fusion | flops 2359296 | bytes 9928704 | tf_op jit(solution)/shard_map/add | solution.py:79
  152.0 2.7 %broadcast.243.clone = f32[3,8,16,24,128]{4,2,3,1,0:T(8,128)} broadcast(f32[]{:T(128)} %constant.132.clone.1), dimensions={} | broadcast | bytes 4718596 | tf_op jit(solution)/shard_map/broadcast.12
  154.7 18.5 %while.63 = (s32[]{:T(128)}, f32[16,24,128]{2,1,0:T(8,128)S(1)}, f32[3,8,16,24,128]{4,2,3,1,0:T(8,128)}, f32[3,8,24,128]{3,2,1,0:T(8,128)S(1)}, f32[3,8,16,24,12...) while((s32[]{:T(128)}, f32[16,24,128]{2,1,0:T(8,128)S(1)}, ...), condition=%wide.region_10.11_spmd.clone, body=%wide.region_9.10_spmd.clone.sunk | while | flops 1695754 | bytes 10002771 | solution.py:65
  154.7 1.7 bitcast_dynamic-update-slice_fusion.97
  159.4 1.4 copy_dynamic-update-slice_fusion.2
  160.9 1.7 bitcast_dynamic-update-slice_fusion.97
  165.6 1.4 copy_dynamic-update-slice_fusion.2
  167.0 1.7 bitcast_dynamic-update-slice_fusion.97
  171.7 1.4 copy_dynamic-update-slice_fusion.2
  174.3 10.9 %all_to_all.28 = f32[4,16,24,128]{3,1,2,0:T(8,128)S(1)} all-to-all(f32[4,16,24,128]{3,1,2,0:T(8,128)S(1)} %broadcast_in_dim.185), channel_id=1, replica_groups=mesh['lev'=4,'col'=32] {'lev'}, dimensions={0} | all-to-all | bytes 1572864 | tf_op jit(solution)/shard_map/all_to_all | solution.py:11
  186.5 9.2 %collective-permute-start = (f32[24,16,4,128]{3,1,2,0:T(8,128)S(1)}, f32[24,16,4,128]{3,1,2,0:T(8,128)S(1)}, u32[]{:S(2)}, u32[]{:S(2)}) collective-permute-start(f32[24,16,4,128]{3,1,2,0:T(8,128)S(1)} %get-tuple-element.533), channel_id=1, source_target_pairs={{0,1},{1,2},{2,3},{3,4},{4,5},{5,6},{6,7},{7,8},{8,9},{9,10},{10,1... | collective-permute-start | bytes 2359304 | tf_op jit(solution)/shard_map/ppermute | solution.py:41
  195.7 1.9 collective-permute-start.1
  197.7 5.8 %collective-permute-start.2 = (f32[4,128]{1,0:T(4,128)S(1)}, f32[4,128]{1,0:T(4,128)S(1)}, u32[]{:S(2)}, u32[]{:S(2)}) collective-permute-start(f32[4,128]{1,0:T(4,128)S(1)} %get-tuple-element.545), channel_id=1, source_target_pairs={{0,1},{1,2},{2,3},{3,4},{4,5},{5,6},{6,7},{7,8},{8,9},{9,10},{10,1... | collective-permute-start | bytes 6152 | tf_op jit(solution)/shard_map/ppermute | solution.py:41
  203.4 2.1 collective-permute-start.3
  205.5 5.6 %collective-permute-done.3 = f32[4,128]{1,0:T(4,128)S(1)} collective-permute-done((f32[4,128]{1,0:T(4,128)S(1)}, f32[4,128]{1,0:T(4,128)S(1)}, u32[]{:S(2)}, u32[]{:S(2)}) %collective-permute-start.3) | collective-permute-done | bytes 2080 | tf_op jit(solution)/shard_map/ppermute | solution.py:44
  212.4 3.2 %fusion.68 = f32[24,16,30,128]{3,1,2,0:T(8,128)S(1)} fusion(f32[24,16,30,128]{3,1,2,0:T(8,128)S(1)} %slice.782, f32[24,16,32,128]{3,1,2,0:T(8,128)S(1)} %pad_maximum_fusion, f32[30,128]{1,0:T(8,128)S(1)} %slice.783), kind=kLoop, calls=%fused_computation.213 | loop fusion | flops 10321920 | bytes 23608320 | tf_op jit(solution)/shard_map/add | solution.py:106
  216.1 3.0 %fusion.73 = f32[24,16,28,128]{3,1,2,0:T(8,128)S(1)} fusion(f32[24,16,28,128]{3,1,2,0:T(8,128)S(1)} %slice.786, f32[24,16,30,128]{3,1,2,0:T(8,128)S(1)} %fusion.68, f32[28,128]{1,0:T(8,128)S(1)} %slice.787), kind=kLoop, calls=%fused_computation.219 | loop fusion | flops 9633792 | bytes 22034432 | tf_op jit(solution)/shard_map/add | solution.py:106
  219.6 3.2 %fusion.78 = f32[24,16,26,128]{3,1,2,0:T(8,128)S(1)} fusion(f32[24,16,26,128]{3,1,2,0:T(8,128)S(1)} %slice.790, f32[24,16,28,128]{3,1,2,0:T(8,128)S(1)} %fusion.73, f32[26,128]{1,0:T(8,128)S(1)} %slice.791), kind=kLoop, calls=%fused_computation.225 | loop fusion | flops 8945664 | bytes 20460544 | tf_op jit(solution)/shard_map/add | solution.py:106
  223.3 2.6 %fusion.83 = f32[24,16,24,128]{3,1,2,0:T(8,128)S(1)} fusion(f32[24,16,24,128]{3,1,2,0:T(8,128)S(1)} %slice.794, f32[24,16,26,128]{3,1,2,0:T(8,128)S(1)} %fusion.78, f32[24,128]{1,0:T(8,128)S(1)} %copy-done.3), kind=kLoop, calls=%fused_computation.231 | loop fusion | flops 8257536 | bytes 18886656 | tf_op jit(solution)/shard_map/add | solution.py:106
  225.9 4.0 %copy.13 = f32[24,16,24,128]{3,2,1,0:T(8,128)} copy(f32[24,16,24,128]{3,1,2,0:T(8,128)S(1)} %fusion.83) | data formatting | bytes 9437184 | tf_op jit(solution)/shard_map/add | solution.py:106
  (156 shorter events, 65.0 us)
Async XLA Ops:
  0.0 9.6 %copy-start = (f32[24,24,128]{2,1,0:T(8,128)S(1)}, f32[24,24,128]{2,1,0:T(8,128)}, u32[]{:S(2)}) copy-start(f32[24,24,128]{2,1,0:T(8,128)} %param.12) | copy-start | bytes 884740
  1.7 37.3 %all-to-all-start = ((f32[4,24,128]{2,1,0:T(8,128)}), f32[4,24,128]{2,1,0:T(8,128)S(1)}, u32[]{:S(2)}, u32[]{:S(2)}) async-start(f32[4,24,128]{2,1,0:T(8,128)} %broadcast_in_dim.172), calls=%async_computation | async-start | bytes 98304 | tf_op jit(solution)/shard_map/all_to_all | solution.py:11
  40.0 15.1 %all-to-all-start.1 = ((f32[4,16,24,128]{3,1,2,0:T(8,128)}), f32[4,16,24,128]{3,1,2,0:T(8,128)S(1)}, u32[]{:S(2)}, u32[]{:S(2)}) async-start(f32[4,16,24,128]{3,1,2,0:T(8,128)} %broadcast_in_dim.176), calls=%async_computation.1 | async-start | bytes 1572864 | tf_op jit(solution)/shard_map/all_to_all | solution.py:11
  83.2 13.2 %all-to-all-start.2 = ((f32[4,16,24,128]{3,1,2,0:T(8,128)}), f32[4,16,24,128]{3,1,2,0:T(8,128)S(1)}, u32[]{:S(2)}, u32[]{:S(2)}) async-start(f32[4,16,24,128]{3,1,2,0:T(8,128)} %broadcast_in_dim.181), calls=%async_computation.2 | async-start | bytes 1572864 | tf_op jit(solution)/shard_map/all_to_all | solution.py:11
  96.4 2.3 %copy-start.2 = (f32[3,8,16,24,128]{4,3,2,1,0:T(8,128)S(1)}, f32[3,8,16,24,128]{4,3,2,1,0:T(8,128)}, u32[]{:S(2)}) copy-start(f32[3,8,16,24,128]{4,3,2,1,0:T(8,128)} %get-tuple-element.266) | copy-start | bytes 14155780
  134.5 12.0 %all-to-all-start.3 = ((f32[4,16,24,128]{3,1,2,0:T(8,128)}), f32[4,16,24,128]{3,1,2,0:T(8,128)S(1)}, u32[]{:S(2)}, u32[]{:S(2)}) async-start(f32[4,16,24,128]{3,1,2,0:T(8,128)} %broadcast_in_dim.183), calls=%async_computation.3 | async-start | bytes 1572864 | tf_op jit(solution)/shard_map/all_to_all | solution.py:11
  173.2 12.4 %copy-start.1 = (f32[3,8,16,24,128]{4,2,3,1,0:T(8,128)S(1)}, f32[3,8,16,24,128]{4,2,3,1,0:T(8,128)}, u32[]{:S(2)}) copy-start(f32[3,8,16,24,128]{4,2,3,1,0:T(8,128)} %get-tuple-element.268) | copy-start | bytes 14155780
  185.5 12.1 %copy-start.3 = (f32[24,128]{1,0:T(8,128)S(1)}, f32[24,128]{1,0:T(8,128)}, u32[]{:S(2)}) copy-start(f32[24,128]{1,0:T(8,128)} %param.13) | copy-start | bytes 36868
  186.5 24.7 %collective-permute-start = (f32[24,16,4,128]{3,1,2,0:T(8,128)S(1)}, f32[24,16,4,128]{3,1,2,0:T(8,128)S(1)}, u32[]{:S(2)}, u32[]{:S(2)}) collective-permute-start(f32[24,16,4,128]{3,1,2,0:T(8,128)S(1)} %get-tuple-element.533), channel_id=1, source_target_pairs={{0,1},{1,2},{2,3},{3,4},{4,5},{5,6},{6,7},{7,8},{8,9},{9,10},{10,1... | collective-permute-start | bytes 2359304 | tf_op jit(solution)/shard_map/ppermute | solution.py:41
  195.7 15.5 %collective-permute-start.1 = (f32[24,16,4,128]{3,1,2,0:T(8,128)S(1)}, f32[24,16,4,128]{3,1,2,0:T(8,128)S(1)}, u32[]{:S(2)}, u32[]{:S(2)}) collective-permute-start(f32[24,16,4,128]{3,1,2,0:T(8,128)S(1)} %get-tuple-element.534), channel_id=1, source_target_pairs={{1,0},{2,1},{3,2},{4,3},{5,4},{6,5},{7,6},{8,7},{9,8},{10,9},{11,1... | collective-permute-start | bytes 2359304 | tf_op jit(solution)/shard_map/ppermute | solution.py:44
  197.7 7.9 %collective-permute-start.2 = (f32[4,128]{1,0:T(4,128)S(1)}, f32[4,128]{1,0:T(4,128)S(1)}, u32[]{:S(2)}, u32[]{:S(2)}) collective-permute-start(f32[4,128]{1,0:T(4,128)S(1)} %get-tuple-element.545), channel_id=1, source_target_pairs={{0,1},{1,2},{2,3},{3,4},{4,5},{5,6},{6,7},{7,8},{8,9},{9,10},{10,1... | collective-permute-start | bytes 6152 | tf_op jit(solution)/shard_map/ppermute | solution.py:41
  203.4 7.7 %collective-permute-start.3 = (f32[4,128]{1,0:T(4,128)S(1)}, f32[4,128]{1,0:T(4,128)S(1)}, u32[]{:S(2)}, u32[]{:S(2)}) collective-permute-start(f32[4,128]{1,0:T(4,128)S(1)} %get-tuple-element.546), channel_id=1, source_target_pairs={{1,0},{2,1},{3,2},{4,3},{5,4},{6,5},{7,6},{8,7},{9,8},{10,9},{11,1... | collective-permute-start | bytes 6152 | tf_op jit(solution)/shard_map/ppermute | solution.py:44
where the time goes:
time: 232 us; the launch traced here: 230 us
  other arithmetic  107 us (46%)
  local copies, waits for them, and re-layouts  43 us (19%)
  starting transfers between devices  34.4 us (15%)
  waiting for transfers between devices  33.2 us (14%)
  blocking collectives  10.9 us (5%)
    while x66, other arithmetic  70.6 us
    all_to_all x4, waiting for transfers between devices, sent_to_all(): lax.all_to_all(jnp.broadcast_to(x[None], (peers, *x.shape)), axis, 0, 0,...  27.6 us
    dynamic_update_slice x12, local copies, waits for them, and re-layouts, sweep_levels(): lax.scan(run_block, start, (rate_blocks, field_blocks), reverse=backward)  15.7 us
    all_to_all x4, starting transfers between devices, sent_to_all(): lax.all_to_all(jnp.broadcast_to(x[None], (peers, *x.shape)), axis, 0, 0,...  15.4 us
    ppermute x2, starting transfers between devices, with_halo(): lax.ppermute(lax.slice_in_dim(block, block.shape[dim] - width, None, axis...  14.9 us
    add x4, other arithmetic, per_device(): center + kappa_part[None, None] * (current[:, :, 2:] + current[:, :, :-2]...  12 us
    all_to_all x1, blocking collectives, sent_to_all(): lax.all_to_all(jnp.broadcast_to(x[None], (peers, *x.shape)), axis, 0, 0,...  10.9 us
    another operation x4, local copies, waits for them, and re-layouts  10.9 us
  transfers between devices with their start and end apart: 8, of which 4 were waited for; matrix products, arithmetic and copies ran while one was open for 15% of the time, Pallas kernels for 0%

commit v1 on v0

v1 whole, which is shorter than its diff:
```python
import functools

import jax
import jax.numpy as jnp
from jax import lax
from jax.experimental import pallas as pl
from jax.experimental.pallas import tpu as pltpu
from jax.sharding import PartitionSpec as P

SMOOTH = 4
LEVELS = 24
MEMBERS = 16
LONS = 24
LATS = 128
BLOCKS = 4
RECORD = 72
STATES = 64
GROUP = 4
CHUNKS = ((0, 4, 6),)
HALO_ROWS = LEVELS * GROUP * MEMBERS
MESSAGE_ROWS = HALO_ROWS + 8
PLANE_LEVELS = 2
STEP_LEVELS = 4

ANY = pl.BlockSpec(memory_space=pl.ANY)
F32 = jnp.float32


def shape(*dims):
    return jax.ShapeDtypeStruct(dims, F32)


def row(ref, at):
    return ref[pl.ds(at, 8, stride=0), :]


def responses(rates, profiles, scratch):
    tiles = [slice(8 * tile, 8 * tile + 8) for tile in range(LONS // 8)]
    up, down = range(LEVELS), range(LEVELS - 1, -1, -1)

    def sweep(order, source, target):
        state = [None] * len(tiles)
        for level in order:
            for at, lons in enumerate(tiles):
                rate = rates[level, lons, :]
                if source is None:
                    state[at] = rate if state[at] is None else rate * state[at]
                else:
                    value = (1.0 - rate) * source[level, lons, :]
                    state[at] = value if state[at] is None else rate * state[at] + value
                target[level, lons, :] = state[at]
        return state

    through = sweep(up, None, scratch.at[0])
    sweep(down, None, profiles.at[3])
    q21 = sweep(down, scratch.at[0], profiles.at[2])
    q32 = sweep(up, profiles.at[3], scratch.at[1])
    q31 = sweep(up, profiles.at[2], scratch.at[0])
    q42 = sweep(down, scratch.at[1], profiles.at[1])
    q41 = sweep(down, scratch.at[0], profiles.at[0])
    return through, q21, q31, q32, q41, q42


def sweep_kernel(chunk, first, field, rate, *refs):
    base, step, groups = chunk
    count = GROUP * groups
    share = count // BLOCKS
    if first:
        local, pieces, profiles_out, refs = refs[0], refs[1:5], refs[5], refs[6:]
    else:
        local, pieces, refs = refs[0], refs[1:5], refs[5:]
        profiles_out = None
    xs, rates, swept, exits, profiles, scratch, in_sems, out_sems = refs
    here = lax.axis_index("lev")
    rate_copy = pltpu.make_async_copy(rate, rates, in_sems.at[3])
    rate_copy.start()
    needed = sorted({(base + step * g) // 8 for g in range(groups)})
    loads = []
    for tile in needed:
        lons = pl.ds(8 * tile, 8)
        loads.append(pltpu.make_async_copy(field.at[:, lons, :], xs.at[:, lons, :], in_sems.at[tile]))
        loads[-1].start()
    rate_copy.wait()
    coefficients = responses(rates, profiles, scratch)
    outs = []
    if profiles_out is not None:
        outs.append(pltpu.make_async_copy(profiles, profiles_out, out_sems.at[4]))
        outs[-1].start()
    for at in range(count):
        lon = base + step * (at // GROUP) + at % GROUP
        for which, tiles in enumerate(coefficients):
            record = at * RECORD + STATES + which
            exits[record : record + 1, :] = tiles[lon // 8][lon % 8 : lon % 8 + 1, :]
    for load in loads:
        load.wait()
    values = xs.reshape(LEVELS * MEMBERS * LONS, LATS)
    weights = rates.reshape(LEVELS * LONS, LATS)

    def run(group, carry):
        lon = base + step * group
        for number in range(4):
            order = range(LEVELS) if number % 2 == 0 else range(LEVELS - 1, -1, -1)
            state = {}
            for level in order:
                for j in range(GROUP):
                    weight = row(weights, level * LONS + lon + j)
                    rest = 1.0 - weight
                    for half in range(2):
                        if number == 0:
                            start = (level * MEMBERS + 8 * half) * LONS + lon + j
                            value = values[pl.ds(start, 8, stride=LONS), :]
                        else:
                            value = swept[level, group * GROUP + j, 8 * half : 8 * half + 8, :]
                        value = rest * value
                        if (j, half) in state:
                            value = weight * state[j, half] + value
                        state[j, half] = value
                        swept[level, group * GROUP + j, 8 * half : 8 * half + 8, :] = value
            for (j, half), value in state.items():
                record = (group * GROUP + j) * RECORD + 16 * number + 8 * half
                exits[pl.ds(record, 8), :] = value
        return carry

    lax.fori_loop(0, groups, run, 0)
    for shift in range(BLOCKS):
        target = lax.rem(here + shift, BLOCKS)
        rows = pl.ds(target * (share * RECORD), share * RECORD)
        outs.append(pltpu.make_async_copy(exits.at[rows, :], pieces[shift], out_sems.at[shift]))
        outs[-1].start()
    outs.append(pltpu.make_async_copy(swept, local, out_sems.at[5]))
    outs[-1].start()
    for out in outs:
        out.wait()


def sweep_call(chunk, first, field, rate):
    count = GROUP * chunk[2]
    share = count // BLOCKS
    outs = [shape(LEVELS, count, MEMBERS, LATS)] + [shape(share * RECORD, LATS)] * BLOCKS
    if first:
        outs.append(shape(4, LEVELS, LONS, LATS))
    return pl.pallas_call(
        functools.partial(sweep_kernel, chunk, first),
        out_shape=outs,
        in_specs=[ANY] * 2,
        out_specs=[ANY] * len(outs),
        scratch_shapes=[
            pltpu.VMEM((LEVELS * MEMBERS, LONS, LATS), F32),
            pltpu.VMEM((LEVELS, LONS, LATS), F32),
            pltpu.VMEM((LEVELS, count, MEMBERS, LATS), F32),
            pltpu.VMEM((count * RECORD, LATS), F32),
            pltpu.VMEM((4, LEVELS, LONS, LATS), F32),
            pltpu.VMEM((2, LEVELS, LONS, LATS), F32),
            pltpu.SemaphoreType.DMA((4,)),
            pltpu.SemaphoreType.DMA((6,)),
        ],
        name="sweeps",
    )(field, rate)


def solve_kernel(share, *refs):
    pieces, outs, (records, states, in_sems, out_sems) = refs[:4], refs[4:8], refs[8:]
    here = lax.axis_index("lev")
    copies = []
    for shift in range(BLOCKS):
        source = lax.rem(here - shift + BLOCKS, BLOCKS)
        rows = pl.ds(source * (share * RECORD), share * RECORD)
        copies.append(pltpu.make_async_copy(pieces[shift], records.at[rows, :], in_sems.at[shift]))
        copies[-1].start()
    for copy in copies:
        copy.wait()

    def run(lon, carry):
        def exit_of(block, number, half):
            at = (block * share + lon) * RECORD + 16 * number + 8 * half
            return records[pl.ds(at, 8), :]

        def response(block, which):
            return row(records, (block * share + lon) * RECORD + STATES + which)

        for half in range(2):
            zero = jnp.zeros((8, LATS), F32)
            f1, b1, f2, b2 = ([zero] * BLOCKS for _ in range(4))
            for d in range(BLOCKS - 1):
                f1[d + 1] = exit_of(d, 0, half) + response(d, 0) * f1[d]
            for d in range(BLOCKS - 1, 0, -1):
                b1[d - 1] = exit_of(d, 1, half) + response(d, 1) * f1[d] + response(d, 0) * b1[d]
            for d in range(BLOCKS - 1):
                f2[d + 1] = (
                    exit_of(d, 2, half)
                    + response(d, 2) * f1[d]
                    + response(d, 3) * b1[d]
                    + response(d, 0) * f2[d]
                )
            for d in range(BLOCKS - 1, 0, -1):
                b2[d - 1] = (
                    exit_of(d, 3, half)
                    + response(d, 4) * f1[d]
                    + response(d, 5) * b1[d]
                    + response(d, 1) * f2[d]
                    + response(d, 0) * b2[d]
                )
            for d in range(BLOCKS):
                for number, entering in enumerate((f1, b1, f2, b2)):
                    at = (d * share + lon) * STATES + 16 * number + 8 * half
                    states[pl.ds(at, 8), :] = entering[d]
        return carry

    lax.fori_loop(0, share, run, 0)
    copies = []
    for shift in range(BLOCKS):
        target = lax.rem(here + shift, BLOCKS)
        rows = pl.ds(target * (share * STATES), share * STATES)
        copies.append(pltpu.make_async_copy(states.at[rows, :], outs[shift], out_sems.at[shift]))
        copies[-1].start()
    for copy in copies:
        copy.wait()


def solve_call(share, pieces):
    return pl.pallas_call(
        functools.partial(solve_kernel, share),
        out_shape=[shape(share * STATES, LATS)] * BLOCKS,
        in_specs=[ANY] * BLOCKS,
        out_specs=[ANY] * BLOCKS,
        scratch_shapes=[
            pltpu.VMEM((BLOCKS * share * RECORD, LATS), F32),
            pltpu.VMEM((BLOCKS * share * STATES, LATS), F32),
            pltpu.SemaphoreType.DMA((4,)),
            pltpu.SemaphoreType.DMA((4,)),
        ],
        name="solve",
    )(*pieces)


def gather_states(share, pieces, states, sems):
    here = lax.axis_index("lev")
    copies = []
    for shift in range(BLOCKS):
        source = lax.rem(here - shift + BLOCKS, BLOCKS)
        rows = pl.ds(source * (share * STATES), share * STATES)
        copies.append(pltpu.make_async_copy(pieces[shift], states.at[rows, :], sems.at[shift]))
        copies[-1].start()
    return copies


def corrected(local, profiles, entering):
    return local + profiles[0] * entering[0] + profiles[1] * entering[1] + profiles[2] * entering[2] + profiles[3] * entering[3]


def edge_kernel(chunk, local, profiles, diffusivity, *refs):
    base, step, groups = chunk
    share = groups
    pieces, outs = refs[:4], refs[4:6]
    block, rows, states, kappa, packed, in_sems, state_sems, out_sems = refs[6:]
    loads = gather_states(share, pieces, states, state_sems)
    for side, group in enumerate((0, groups - 1)):
        loads.append(pltpu.make_async_copy(local.at[:, pl.ds(group * GROUP, GROUP)], block.at[:, pl.ds(side * GROUP, GROUP)], in_sems.at[side]))
        loads[-1].start()
    loads.append(pltpu.make_async_copy(profiles, rows, in_sems.at[2]))
    loads[-1].start()
    loads.append(pltpu.make_async_copy(diffusivity, kappa, in_sems.at[3]))
    loads[-1].start()
    for load in loads:
        load.wait()
    profile_rows = rows.reshape(4 * LEVELS * LONS, LATS)
    for side, group in enumerate((0, groups - 1)):
        lon = base + step * group
        packed[side, HALO_ROWS : HALO_ROWS + 8, :] = kappa[(lon // 8) * 8 : (lon // 8) * 8 + 8, :]
        for j in range(GROUP):
            entering = [
                [states[(group * GROUP + j) * STATES + 16 * n + 8 * half : (group * GROUP + j) * STATES + 16 * n + 8 * half + 8, :] for n in range(4)]
                for half in range(2)
            ]

            def run(level, carry):
                mine = [row(profile_rows, (n * LEVELS + level) * LONS + lon + j) for n in range(4)]
                for half in range(2):
                    value = corrected(block[level, side * GROUP + j, 8 * half : 8 * half + 8, :], mine, entering[half])
                    packed[side, pl.ds(level * (GROUP * MEMBERS) + j * MEMBERS + 8 * half, 8), :] = value
                return carry

            lax.fori_loop(0, LEVELS, run, 0, unroll=8)
    copies = []
    for side in range(2):
        copies.append(pltpu.make_async_copy(packed.at[side], outs[side], out_sems.at[side]))
        copies[-1].start()
    for copy in copies:
        copy.wait()


def edge_call(chunk, local, profiles, diffusivity, pieces):
    share = chunk[2]
    return pl.pallas_call(
        functools.partial(edge_kernel, chunk),
        out_shape=[shape(MESSAGE_ROWS, LATS)] * 2,
        in_specs=[ANY] * 7,
        out_specs=[ANY] * 2,
        scratch_shapes=[
            pltpu.VMEM((LEVELS, 2 * GROUP, MEMBERS, LATS), F32),
            pltpu.VMEM((4, LEVELS, LONS, LATS), F32),
            pltpu.VMEM((BLOCKS * share * STATES, LATS), F32),
            pltpu.VMEM((LONS, LATS), F32),
            pltpu.VMEM((2, MESSAGE_ROWS, LATS), F32),
            pltpu.SemaphoreType.DMA((4,)),
            pltpu.SemaphoreType.DMA((4,)),
            pltpu.SemaphoreType.DMA((2,)),
        ],
        name="edges",
    )(local, profiles, diffusivity, *pieces)


def diffuse_kernel(chunks, *refs):
    n = len(chunks)
    locals_, refs = refs[:n], refs[n:]
    profiles, low, high, low_k, high_k, own_k, refs = *refs[:6], refs[6:]
    pieces, refs = refs[: 4 * n], refs[4 * n :]
    out, refs = refs[0], refs[1:]
    states, kappa, center, buffers, sems = refs[:n], *refs[n:]
    wide = LONS + 2 * GROUP

    @pl.when(pl.program_id(0) == 0)
    def _():
        copies = []
        for at, chunk in enumerate(chunks):
            copies += gather_states(chunk[2], pieces[4 * at : 4 * at + 4], states[at], sems.at[at])
        kappa[0:GROUP, :] = low_k[GROUP : 2 * GROUP, :]
        kappa[GROUP : GROUP + LONS, :] = own_k[...]
        kappa[GROUP + LONS : wide, :] = high_k[0:GROUP, :]
        center[...] = 1.0 - 4.0 * kappa[...]
        for copy in copies:
            copy.wait()

    where = {}
    for at, (base, step, groups) in enumerate(chunks):
        for index in range(GROUP * groups):
            where[base + step * (index // GROUP) + index % GROUP] = (at, index)
    profile_rows = profiles.reshape(4 * STEP_LEVELS * LONS, LATS)
    out_rows = out.reshape(STEP_LEVELS * MEMBERS * LONS, LATS)
    planes = [(level, half) for level in range(PLANE_LEVELS) for half in range(2)]
    lane = lax.broadcasted_iota(jnp.int32, (8, LATS), 1)
    first, last = lane == 0, lane == LATS - 1

    def run(part, carry):
        top = part * PLANE_LEVELS
        for lon in range(wide):
            own = lon - GROUP
            if 0 <= own < LONS:
                at, index = where[own]
                entering = [
                    [states[at][index * STATES + 16 * n + 8 * half : index * STATES + 16 * n + 8 * half + 8, :] for n in range(4)]
                    for half in range(2)
                ]
                for level in range(PLANE_LEVELS):
                    mine = [row(profile_rows, (n * STEP_LEVELS + top + level) * LONS + own) for n in range(4)]
                    for half in range(2):
                        value = corrected(locals_[at][top + level, index, 8 * half : 8 * half + 8, :], mine, entering[half])
                        buffers[0, 2 * level + half, lon] = value
            else:
                side, j = (low, lon) if own < 0 else (high, own - LONS)
                for level in range(PLANE_LEVELS):
                    for half in range(2):
                        start = (top + level) * (GROUP * MEMBERS) + j * MEMBERS + 8 * half
                        buffers[0, 2 * level + half, lon] = side[pl.ds(start, 8), :]
        for step in range(SMOOTH):
            source, target = step % 2, (step + 1) % 2
            west = [buffers[source, p, step] for p in range(len(planes))]
            here = [buffers[source, p, step + 1] for p in range(len(planes))]
            for lon in range(step + 1, wide - step - 1):
                k, c = row(kappa, lon), row(center, lon)
                for p, (level, half) in enumerate(planes):
                    east = buffers[source, p, lon + 1]
                    south = jnp.where(first, 0.0, pltpu.roll(here[p], 1, 1))
                    north = jnp.where(last, 0.0, pltpu.roll(here[p], LATS - 1, 1))
                    value = c * here[p] + k * ((east + west[p]) + (south + north))
                    west[p], here[p] = here[p], east
                    if step < SMOOTH - 1:
                        buffers[target, p, lon] = value
                    else:
                        start = ((top + level) * MEMBERS + 8 * half) * LONS + lon - GROUP
                        out_rows[pl.ds(start, 8, stride=LONS), :] = value
        return carry

    lax.fori_loop(0, STEP_LEVELS // PLANE_LEVELS, run, 0)


def diffuse_call(chunks, locals_, profiles, low, high, diffusivity, pieces):
    n = len(chunks)
    wide = LONS + 2 * GROUP
    rows = STEP_LEVELS * GROUP * MEMBERS
    fixed = lambda i: (HALO_ROWS // 8, 0)
    in_specs = [pl.BlockSpec((STEP_LEVELS, GROUP * chunk[2], MEMBERS, LATS), lambda i: (i, 0, 0, 0)) for chunk in chunks]
    in_specs += [
        pl.BlockSpec((4, STEP_LEVELS, LONS, LATS), lambda i: (0, i, 0, 0)),
        pl.BlockSpec((rows, LATS), lambda i: (i, 0)),
        pl.BlockSpec((rows, LATS), lambda i: (i, 0)),
        pl.BlockSpec((8, LATS), fixed),
        pl.BlockSpec((8, LATS), fixed),
        pl.BlockSpec((LONS, LATS), lambda i: (0, 0)),
    ]
    in_specs += [ANY] * (4 * n)
    return pl.pallas_call(
        functools.partial(diffuse_kernel, chunks),
        grid=(LEVELS // STEP_LEVELS,),
        out_shape=shape(LEVELS * MEMBERS, LONS, LATS),
        in_specs=in_specs,
        out_specs=pl.BlockSpec((STEP_LEVELS * MEMBERS, LONS, LATS), lambda i: (i, 0, 0)),
        scratch_shapes=[pltpu.VMEM((GROUP * chunk[2] * STATES, LATS), F32) for chunk in chunks]
        + [
            pltpu.VMEM((wide, LATS), F32),
            pltpu.VMEM((wide, LATS), F32),
            pltpu.VMEM((2, 2 * PLANE_LEVELS, wide, 8, LATS), F32),
            pltpu.SemaphoreType.DMA((n, 4)),
        ],
        name="diffuse",
    )(*locals_, profiles, low, high, low, high, diffusivity, *pieces)


def shifted(pieces):
    moved = [pieces[0]]
    for shift in (1, 2, 3):
        moved.append(lax.ppermute(pieces[shift], "lev", [(i, (i + shift) % BLOCKS) for i in range(BLOCKS)]))
    return moved


def per_device(control_field, decay_rate, diffusivity):
    field = control_field.reshape(LEVELS * MEMBERS, LONS, LATS)
    locals_, states, profiles = [], [], None
    for at, chunk in enumerate(CHUNKS):
        local, *rest = sweep_call(chunk, at == 0, field, decay_rate)
        if at == 0:
            profiles = rest.pop()
        locals_.append(local)
        states.append(shifted(solve_call(chunk[2], shifted(rest))))
    to_low, to_high = edge_call(CHUNKS[0], locals_[0], profiles, diffusivity, states[0])
    count = lax.axis_size("col")
    forward = [(i, i + 1) for i in range(count - 1)]
    low = lax.ppermute(to_high, "col", forward)
    high = lax.ppermute(to_low, "col", [(b, a) for a, b in forward])
    out = diffuse_call(CHUNKS, locals_, profiles, low, high, diffusivity, sum(states, []))
    return out.reshape(control_field.shape)


def solution(mesh):
    in_specs = (P("lev", None, "col", None), P("lev", "col", None), P("col", None))
    out_specs = P("lev", None, "col", None)
    return jax.shard_map(
        per_device, mesh=mesh, in_specs=in_specs, out_specs=out_specs, check_vma=False
    )
```

time: 232 us -> 79.7 us (0.34)
  the two profiles are of different devices: /device:TPU:7 before, /device:TPU:39 now
where the time goes in v1:
time: 79.7 us; the launch traced here: 79.5 us
  waiting for transfers between devices  31.4 us (39%)
  Pallas kernels  29.8 us (37%)
  starting transfers between devices  15.8 us (20%)
  local copies, waits for them, and re-layouts  2.46 us (3%)
    ppermute x6, waiting for transfers between devices, shifted(): lax.ppermute(pieces[shift], 'lev', [(i, (i + shift) % BLOCKS) for i in ra...  17.6 us
    pallas_call x1, Pallas kernels, diffuse_call(): pl.pallas_call(functools.partial(diffuse_kernel, chunks), grid=(LEVELS //...  15.7 us
    ppermute x6, starting transfers between devices, shifted(): lax.ppermute(pieces[shift], 'lev', [(i, (i + shift) % BLOCKS) for i in ra...  9.18 us
    pallas_call x1, Pallas kernels, sweep_call(): pl.pallas_call(functools.partial(sweep_kernel, chunk, first), out_shape=o...  7.92 us
    ppermute x1, waiting for transfers between devices, per_device(): low = lax.ppermute(to_high, 'col', forward)  7.34 us
    ppermute x1, waiting for transfers between devices, per_device(): high = lax.ppermute(to_low, 'col', [(b, a) for a, b in forward])  6.4 us
    ppermute x1, starting transfers between devices, per_device(): low = lax.ppermute(to_high, 'col', forward)  4.7 us
    pallas_call x1, Pallas kernels, edge_call(): pl.pallas_call(functools.partial(edge_kernel, chunk), out_shape=[shape(ME...  3.71 us
  transfers between devices with their start and end apart: 8, of which 6 were waited for; matrix products, arithmetic and copies ran while one was open for 0% of the time, Pallas kernels for 0%

profile of v1, /device:TPU:39, one launch (start us, length us, event | category | flops | bytes accessed | tf_op | source)
XLA Modules:
  0.0 79.5 jit_solution(3316611342610439212)
XLA Ops:
  0.0 7.9 %sweeps.1 = (f32[24,24,16,128]{3,2,1,0:T(8,128)}, f32[432,128]{1,0:T(8,128)}, f32[432,128]{1,0:T(8,128)}, f32[432,128]{1,0:T(8,128)}, f32[432,128]{1,0:T(8,128)}, /*index=5*/f32[4,24,24,128]{3,2,1,0:T(8,128)}) custom-call(f32[384,24,128]{2,1,0:T(8,128)} %bitcast.2, f32[24,24,128]{2,1,0:T(8,128)} %rate.1), custom_call_target="tpu_custom_call" | custom-call | tf_op jit(solution)/shard_map/sweeps/pallas_call | solution.py:142
  7.9 1.4 %collective-permute-start = (f32[432,128]{1,0:T(8,128)}, f32[432,128]{1,0:T(8,128)S(1)}, u32[]{:S(2)}, u32[]{:S(2)}) collective-permute-start(f32[432,128]{1,0:T(8,128)} %get-tuple-element.20), channel_id=1, source_target_pairs={{0,32},{32,64},{64,96},{96,0},{1,33},{33,65},{65,97},{97,1},{2,34}... | collective-permute-start | bytes 663560 | tf_op jit(solution)/shard_map/ppermute | solution.py:422
  9.3 2.6 %collective-permute-start.1 = (f32[432,128]{1,0:T(8,128)}, f32[432,128]{1,0:T(8,128)S(1)}, u32[]{:S(2)}, u32[]{:S(2)}) collective-permute-start(f32[432,128]{1,0:T(8,128)} %get-tuple-element.21), channel_id=1, source_target_pairs={{0,64},{32,96},{64,0},{96,32},{1,65},{33,97},{65,1},{97,33},{2,66}... | collective-permute-start | bytes 663560 | tf_op jit(solution)/shard_map/ppermute | solution.py:422
  11.9 1.1 %collective-permute-start.2 = (f32[432,128]{1,0:T(8,128)}, f32[432,128]{1,0:T(8,128)S(1)}, u32[]{:S(2)}, u32[]{:S(2)}) collective-permute-start(f32[432,128]{1,0:T(8,128)} %get-tuple-element.22), channel_id=1, source_target_pairs={{0,96},{32,0},{64,32},{96,64},{1,97},{33,1},{65,33},{97,65},{2,98}... | collective-permute-start | bytes 663560 | tf_op jit(solution)/shard_map/ppermute | solution.py:422
  13.0 2.9 %collective-permute-done.refs_1_ = f32[432,128]{1,0:T(8,128)S(1)} collective-permute-done((f32[432,128]{1,0:T(8,128)}, f32[432,128]{1,0:T(8,128)S(1)}, u32[]{:S(2)}, u32[]{:S(2)}) %collective-permute-start) | collective-permute-done | bytes 221216 | tf_op jit(solution)/shard_map/ppermute | solution.py:422
  15.9 0.0 copy-start.5
  15.9 5.9 %collective-permute-done.1.refs_2_ = f32[432,128]{1,0:T(8,128)S(1)} collective-permute-done((f32[432,128]{1,0:T(8,128)}, f32[432,128]{1,0:T(8,128)S(1)}, u32[]{:S(2)}, u32[]{:S(2)}) %collective-permute-start.1) | collective-permute-done | bytes 221216 | tf_op jit(solution)/shard_map/ppermute | solution.py:422
  21.7 0.0 copy-start.6
  21.7 0.0 collective-permute-done.2.refs_3_
  21.7 0.0 copy-start.7
  21.7 0.0 copy-done.5
  21.7 0.7 copy-done.6
  22.4 0.1 copy-done.7
  22.5 2.4 %solve.1 = (f32[384,128]{1,0:T(8,128)}, f32[384,128]{1,0:T(8,128)}, f32[384,128]{1,0:T(8,128)}, f32[384,128]{1,0:T(8,128)}) custom-call(f32[432,128]{1,0:T(8,128)} %get-tuple-element.19.refs_0_, f32[432,128]{1,0:T(8,128)} %copy-done.5, f32[432,128]{1,0:T(8,128)} %copy-done.6, f32[432,128]{1,0:T(8,128)} %copy-done.7), custom_call_target="tpu_custom_call" | custom-call | tf_op jit(solution)/shard_map/solve/pallas_call | solution.py:221
  24.9 1.3 %collective-permute-start.3 = (f32[384,128]{1,0:T(8,128)}, f32[384,128]{1,0:T(8,128)S(1)}, u32[]{:S(2)}, u32[]{:S(2)}) collective-permute-start(f32[384,128]{1,0:T(8,128)} %get-tuple-element.24), channel_id=1, source_target_pairs={{0,32},{32,64},{64,96},{96,0},{1,33},{33,65},{65,97},{97,1},{2,34}... | collective-permute-start | bytes 589832 | tf_op jit(solution)/shard_map/ppermute | solution.py:422
  26.2 2.8 %collective-permute-start.4 = (f32[384,128]{1,0:T(8,128)}, f32[384,128]{1,0:T(8,128)S(1)}, u32[]{:S(2)}, u32[]{:S(2)}) collective-permute-start(f32[384,128]{1,0:T(8,128)} %get-tuple-element.25), channel_id=1, source_target_pairs={{0,64},{32,96},{64,0},{96,32},{1,65},{33,97},{65,1},{97,33},{2,66}... | collective-permute-start | bytes 589832 | tf_op jit(solution)/shard_map/ppermute | solution.py:422
  29.0 0.0 collective-permute-start.5
  29.0 2.6 %collective-permute-done.3.refs_1_.refs_8_ = f32[384,128]{1,0:T(8,128)S(1)} collective-permute-done((f32[384,128]{1,0:T(8,128)}, f32[384,128]{1,0:T(8,128)S(1)}, u32[]{:S(2)}, u32[]{:S(2)}) %collective-permute-start.3) | collective-permute-done | bytes 196640 | tf_op jit(solution)/shard_map/ppermute | solution.py:422
  31.7 0.0 copy-start.2
  31.7 6.3 %collective-permute-done.4.refs_2_.refs_9_ = f32[384,128]{1,0:T(8,128)S(1)} collective-permute-done((f32[384,128]{1,0:T(8,128)}, f32[384,128]{1,0:T(8,128)S(1)}, u32[]{:S(2)}, u32[]{:S(2)}) %collective-permute-start.4) | collective-permute-done | bytes 196640 | tf_op jit(solution)/shard_map/ppermute | solution.py:422
  37.9 0.0 copy-start.3
  37.9 0.0 collective-permute-done.5.refs_3_.refs_10_
  37.9 0.0 copy-start.4
  37.9 0.0 copy-done.2
  37.9 0.7 copy-done.3
  38.6 0.1 copy-done.4
  38.7 3.7 %edges.1 = (f32[1544,128]{1,0:T(8,128)}, f32[1544,128]{1,0:T(8,128)}) custom-call(f32[24,24,16,128]{3,2,1,0:T(8,128)} %get-tuple-element.17.local.refs_0_, f32[4,24,24,128]{3,2,1,0:T(8,128)} %get-tuple-element.18.profiles.refs_1_, f32[24,128]{1,0:T(8,128)} %refs_6_.1, f32[384,128]{1,0:T(8,128)} %get-tuple-element.23.refs_0_.refs_7_, f32[384,128]{1,0:T(8,128)} %copy-done.2, ...), custom_call_target="tpu_custom_call" | custom-call | tf_op jit(solution)/shard_map/edges/pallas_call | solution.py:294
  42.4 4.7 %collective-permute-start.6 = (f32[1544,128]{1,0:T(8,128)}, f32[1544,128]{1,0:T(8,128)S(1)}, u32[]{:S(2)}, u32[]{:S(2)}) collective-permute-start(f32[1544,128]{1,0:T(8,128)} %get-tuple-element.27), channel_id=1, source_target_pairs={{0,1},{1,2},{2,3},{3,4},{4,5},{5,6},{6,7},{7,8},{8,9},{9,10},{10,1... | collective-permute-start | bytes 2371592 | tf_op jit(solution)/shard_map/ppermute | solution.py:438
  47.1 1.9 %collective-permute-start.7 = (f32[1544,128]{1,0:T(8,128)}, f32[1544,128]{1,0:T(8,128)S(1)}, u32[]{:S(2)}, u32[]{:S(2)}) collective-permute-start(f32[1544,128]{1,0:T(8,128)} %get-tuple-element.28), channel_id=1, source_target_pairs={{1,0},{2,1},{3,2},{4,3},{5,4},{6,5},{7,6},{8,7},{9,8},{10,9},{11,1... | collective-permute-start | bytes 2371592 | tf_op jit(solution)/shard_map/ppermute | solution.py:439
  49.1 7.3 %collective-permute-done.6.refs_2_.refs_4_ = f32[1544,128]{1,0:T(8,128)S(1)} collective-permute-done((f32[1544,128]{1,0:T(8,128)}, f32[1544,128]{1,0:T(8,128)S(1)}, u32[]{:S(2)}, u32[]{:S(2)}) %collective-permute-start.6) | collective-permute-done | bytes 790560 | tf_op jit(solution)/shard_map/ppermute | solution.py:438
  56.4 0.0 copy-start
  56.4 6.4 %collective-permute-done.7.refs_3_.refs_5_ = f32[1544,128]{1,0:T(8,128)S(1)} collective-permute-done((f32[1544,128]{1,0:T(8,128)}, f32[1544,128]{1,0:T(8,128)S(1)}, u32[]{:S(2)}, u32[]{:S(2)}) %collective-permute-start.7) | collective-permute-done | bytes 790560 | tf_op jit(solution)/shard_map/ppermute | solution.py:439
  62.8 0.0 copy-done
  62.8 0.0 copy-start.1
  62.8 0.9 %copy-done.1 = f32[1544,128]{1,0:T(8,128)} copy-done((f32[1544,128]{1,0:T(8,128)}, f32[1544,128]{1,0:T(8,128)S(1)}, u32[]{:S(2)}) %copy-start.1) | copy-done | bytes 790552
  63.7 15.7 %diffuse.1 = f32[384,24,128]{2,1,0:T(8,128)} custom-call(f32[24,24,16,128]{3,2,1,0:T(8,128)} %get-tuple-element.17.local.refs_0_, f32[4,24,24,128]{3,2,1,0:T(8,128)} %get-tuple-element.18.profiles.refs_1_, f32[1544,128]{1,0:T(8,128)} %copy-done, f32[1544,128]{1,0:T(8,128)} %copy-done.1, f32[1544,128]{1,0:T(8,128)} %copy-done, f32[1544,128]{1,0:T(8,128)} %copy-done.1, ...), custom_call_target="tpu_custom_call" | custom-call | tf_op jit(solution)/shard_map/diffuse/pallas_call | solution.py:402
Async XLA Ops:
  7.9 7.9 %collective-permute-start = (f32[432,128]{1,0:T(8,128)}, f32[432,128]{1,0:T(8,128)S(1)}, u32[]{:S(2)}, u32[]{:S(2)}) collective-permute-start(f32[432,128]{1,0:T(8,128)} %get-tuple-element.20), channel_id=1, source_target_pairs={{0,32},{32,64},{64,96},{96,0},{1,33},{33,65},{65,97},{97,1},{2,34}... | collective-permute-start | bytes 663560 | tf_op jit(solution)/shard_map/ppermute | solution.py:422
  9.3 12.4 %collective-permute-start.1 = (f32[432,128]{1,0:T(8,128)}, f32[432,128]{1,0:T(8,128)S(1)}, u32[]{:S(2)}, u32[]{:S(2)}) collective-permute-start(f32[432,128]{1,0:T(8,128)} %get-tuple-element.21), channel_id=1, source_target_pairs={{0,64},{32,96},{64,0},{96,32},{1,65},{33,97},{65,1},{97,33},{2,66}... | collective-permute-start | bytes 663560 | tf_op jit(solution)/shard_map/ppermute | solution.py:422
  11.9 9.8 %collective-permute-start.2 = (f32[432,128]{1,0:T(8,128)}, f32[432,128]{1,0:T(8,128)S(1)}, u32[]{:S(2)}, u32[]{:S(2)}) collective-permute-start(f32[432,128]{1,0:T(8,128)} %get-tuple-element.22), channel_id=1, source_target_pairs={{0,96},{32,0},{64,32},{96,64},{1,97},{33,1},{65,33},{97,65},{2,98}... | collective-permute-start | bytes 663560 | tf_op jit(solution)/shard_map/ppermute | solution.py:422
  15.9 5.9 %copy-start.5 = (f32[432,128]{1,0:T(8,128)}, f32[432,128]{1,0:T(8,128)S(1)}, u32[]{:S(2)}) copy-start(f32[432,128]{1,0:T(8,128)S(1)} %collective-permute-done.refs_1_) | copy-start | bytes 663556
  21.7 0.7 copy-start.6
  21.7 0.8 copy-start.7
  24.9 6.8 %collective-permute-start.3 = (f32[384,128]{1,0:T(8,128)}, f32[384,128]{1,0:T(8,128)S(1)}, u32[]{:S(2)}, u32[]{:S(2)}) collective-permute-start(f32[384,128]{1,0:T(8,128)} %get-tuple-element.24), channel_id=1, source_target_pairs={{0,32},{32,64},{64,96},{96,0},{1,33},{33,65},{65,97},{97,1},{2,34}... | collective-permute-start | bytes 589832 | tf_op jit(solution)/shard_map/ppermute | solution.py:422
  26.2 11.7 %collective-permute-start.4 = (f32[384,128]{1,0:T(8,128)}, f32[384,128]{1,0:T(8,128)S(1)}, u32[]{:S(2)}, u32[]{:S(2)}) collective-permute-start(f32[384,128]{1,0:T(8,128)} %get-tuple-element.25), channel_id=1, source_target_pairs={{0,64},{32,96},{64,0},{96,32},{1,65},{33,97},{65,1},{97,33},{2,66}... | collective-permute-start | bytes 589832 | tf_op jit(solution)/shard_map/ppermute | solution.py:422
  29.0 8.9 %collective-permute-start.5 = (f32[384,128]{1,0:T(8,128)}, f32[384,128]{1,0:T(8,128)S(1)}, u32[]{:S(2)}, u32[]{:S(2)}) collective-permute-start(f32[384,128]{1,0:T(8,128)} %get-tuple-element.26), channel_id=1, source_target_pairs={{0,96},{32,0},{64,32},{96,64},{1,97},{33,1},{65,33},{97,65},{2,98}... | collective-permute-start | bytes 589832 | tf_op jit(solution)/shard_map/ppermute | solution.py:422
  31.7 6.3 %copy-start.2 = (f32[384,128]{1,0:T(8,128)}, f32[384,128]{1,0:T(8,128)S(1)}, u32[]{:S(2)}) copy-start(f32[384,128]{1,0:T(8,128)S(1)} %collective-permute-done.3.refs_1_.refs_8_) | copy-start | bytes 589828
  37.9 0.7 copy-start.3
  37.9 0.8 copy-start.4
  42.4 14.0 %collective-permute-start.6 = (f32[1544,128]{1,0:T(8,128)}, f32[1544,128]{1,0:T(8,128)S(1)}, u32[]{:S(2)}, u32[]{:S(2)}) collective-permute-start(f32[1544,128]{1,0:T(8,128)} %get-tuple-element.27), channel_id=1, source_target_pairs={{0,1},{1,2},{2,3},{3,4},{4,5},{5,6},{6,7},{7,8},{8,9},{9,10},{10,1... | collective-permute-start | bytes 2371592 | tf_op jit(solution)/shard_map/ppermute | solution.py:438
  47.1 15.7 %collective-permute-start.7 = (f32[1544,128]{1,0:T(8,128)}, f32[1544,128]{1,0:T(8,128)S(1)}, u32[]{:S(2)}, u32[]{:S(2)}) collective-permute-start(f32[1544,128]{1,0:T(8,128)} %get-tuple-element.28), channel_id=1, source_target_pairs={{1,0},{2,1},{3,2},{4,3},{5,4},{6,5},{7,6},{8,7},{9,8},{10,9},{11,1... | collective-permute-start | bytes 2371592 | tf_op jit(solution)/shard_map/ppermute | solution.py:439
  56.4 6.4 %copy-start = (f32[1544,128]{1,0:T(8,128)}, f32[1544,128]{1,0:T(8,128)S(1)}, u32[]{:S(2)}) copy-start(f32[1544,128]{1,0:T(8,128)S(1)} %collective-permute-done.6.refs_2_.refs_4_) | copy-start | bytes 2371588
  62.8 0.9 %copy-start.1 = (f32[1544,128]{1,0:T(8,128)}, f32[1544,128]{1,0:T(8,128)S(1)}, u32[]{:S(2)}) copy-start(f32[1544,128]{1,0:T(8,128)S(1)} %collective-permute-done.7.refs_3_.refs_5_) | copy-start | bytes 2371588

commit v2 on v0

v2 whole, which is shorter than its diff:
```python
import functools

import jax
import jax.numpy as jnp
from jax import lax
from jax.experimental import pallas as pl
from jax.experimental.pallas import tpu as pltpu
from jax.sharding import PartitionSpec as P

SMOOTH = 4
LEVELS = 24
MEMBERS = 16
LONS = 24
LATS = 128
BLOCKS = 4
SHARE = LONS // BLOCKS
RECORD = 72
STATES = 64
GROUP = 4
GROUPS = LONS // GROUP
SLAB = 8
SLABS = LEVELS // SLAB
PAD = LATS + 16

ANY = pl.BlockSpec(memory_space=pl.ANY)
F32 = jnp.float32


def shape(*dims):
    return jax.ShapeDtypeStruct(dims, F32)


def row(ref, at):
    return ref[pl.ds(at, 8, stride=0), :]


def slot(lon):
    if lon < GROUP:
        return lon * SHARE
    if lon >= LONS - GROUP:
        return (lon - LONS + GROUP) * SHARE + 1
    return (lon - GROUP) // GROUP * SHARE + 2 + lon % GROUP


def start_all(copies):
    for copy in copies:
        copy.start()
    return copies


def wait_all(copies):
    for copy in copies:
        copy.wait()


def responses(rates, profiles, scratch):
    tiles = [slice(8 * tile, 8 * tile + 8) for tile in range(LONS // 8)]
    up, down = range(LEVELS), range(LEVELS - 1, -1, -1)

    def sweep(order, source, target):
        state = [None] * len(tiles)
        for level in order:
            for at, lons in enumerate(tiles):
                rate = rates[level, lons, :]
                if source is None:
                    state[at] = rate if state[at] is None else rate * state[at]
                else:
                    value = (1.0 - rate) * source[level, lons, :]
                    state[at] = value if state[at] is None else rate * state[at] + value
                target[level, lons, :] = state[at]
        return state

    through = sweep(up, None, scratch.at[0])
    sweep(down, None, profiles.at[3])
    q21 = sweep(down, scratch.at[0], profiles.at[2])
    q32 = sweep(up, profiles.at[3], scratch.at[1])
    q31 = sweep(up, profiles.at[2], scratch.at[0])
    q42 = sweep(down, scratch.at[1], profiles.at[1])
    q41 = sweep(down, scratch.at[0], profiles.at[0])
    return through, q21, q31, q32, q41, q42


def sweep_kernel(field, rate, diffusivity, local, p0, p1, p2, p3, profiles_out, to_low, to_high, *refs):
    xs, rates, kappa, swept, exits, profiles, scratch, packed, in_sems, out_sems, local_sems, halo_sems = refs
    here = lax.axis_index("lev")
    small = start_all(
        [
            pltpu.make_async_copy(rate, rates, in_sems.at[3]),
            pltpu.make_async_copy(diffusivity, kappa, in_sems.at[4]),
        ]
    )
    loads = []
    for tile in range(LONS // 8):
        lons = pl.ds(8 * tile, 8)
        loads.append(pltpu.make_async_copy(field.at[:, lons, :], xs.at[:, lons, :], in_sems.at[tile]))
    start_all(loads)
    wait_all(small)
    coefficients = responses(rates, profiles, scratch)
    outs = start_all([pltpu.make_async_copy(profiles, profiles_out, out_sems.at[4])])
    for lon in range(LONS):
        for which, tiles in enumerate(coefficients):
            record = slot(lon) * RECORD + STATES + which
            exits[record : record + 1, :] = tiles[lon // 8][lon % 8 : lon % 8 + 1, :]
    profile_rows = profiles.reshape(4 * LEVELS * LONS, LATS)
    for side, lon in enumerate((0, LONS - GROUP)):
        packed[side, pl.ds(4, GROUP, stride=8), :] = kappa[lon : lon + GROUP, :]
        for level in range(LEVELS):
            for n in range(4):
                start = (n * LEVELS + level) * LONS + lon
                packed[side, pl.ds(level * GROUP * 8 + n, GROUP, stride=8), :] = profile_rows[pl.ds(start, GROUP), :]
    values = xs.reshape(LEVELS * MEMBERS * LONS, LATS)
    weights = rates.reshape(LEVELS * LONS, LATS)

    def save(group):
        lons = pl.ds(group * GROUP, GROUP)
        return pltpu.make_async_copy(swept.at[:, lons], local.at[:, lons], local_sems.at[group])

    def run(group, carry):
        lon = GROUP * group
        for number in range(4):
            order = range(LEVELS) if number % 2 == 0 else range(LEVELS - 1, -1, -1)
            state = {}
            for level in order:
                for j in range(GROUP):
                    weight = row(weights, level * LONS + lon + j)
                    rest = 1.0 - weight
                    for half in range(2):
                        if number == 0:
                            start = (level * MEMBERS + 8 * half) * LONS + lon + j
                            value = values[pl.ds(start, 8, stride=LONS), :]
                        else:
                            value = swept[level, lon + j, 8 * half : 8 * half + 8, :]
                        value = rest * value
                        if (j, half) in state:
                            value = weight * state[j, half] + value
                        state[j, half] = value
                        swept[level, lon + j, 8 * half : 8 * half + 8, :] = value
            for (j, half), value in state.items():
                edge = jnp.where(group == 0, j * SHARE, j * SHARE + 1)
                inner = (group - 1) * SHARE + 2 + j
                place = jnp.where((group == 0) | (group == GROUPS - 1), edge, inner)
                exits[pl.ds(pl.multiple_of(place * RECORD + 16 * number + 8 * half, 8), 8), :] = value
        save(group).start()
        return carry

    for tile in range(LONS // 8):
        loads[tile].wait()
        lax.fori_loop(2 * tile, 2 * tile + 2, run, 0)
    for shift, piece in enumerate((p0, p1, p2, p3)):
        target = lax.rem(here + shift, BLOCKS)
        rows = pl.ds(target * (SHARE * RECORD), SHARE * RECORD)
        outs += start_all([pltpu.make_async_copy(exits.at[rows, :], piece, out_sems.at[shift])])
    for side, (lon, out) in enumerate(((0, to_low), (LONS - GROUP, to_high))):
        outs += start_all(
            [
                pltpu.make_async_copy(swept.at[:, pl.ds(lon, GROUP)], out.at[:, :, pl.ds(0, MEMBERS), :], halo_sems.at[2 * side]),
                pltpu.make_async_copy(
                    packed.at[side].reshape(LEVELS, GROUP, 8, LATS), out.at[:, :, pl.ds(MEMBERS, 8), :], halo_sems.at[2 * side + 1]
                ),
            ]
        )
    wait_all(outs)
    wait_all([save(group) for group in range(GROUPS)])


def sweep_call(field, rate, diffusivity):
    halo = shape(LEVELS, GROUP, MEMBERS + 8, LATS)
    outs = [shape(LEVELS, LONS, MEMBERS, LATS)] + [shape(SHARE * RECORD, LATS)] * BLOCKS
    outs += [shape(4, LEVELS, LONS, LATS), halo, halo]
    return pl.pallas_call(
        sweep_kernel,
        out_shape=outs,
        in_specs=[ANY] * 3,
        out_specs=[ANY] * len(outs),
        scratch_shapes=[
            pltpu.VMEM((LEVELS * MEMBERS, LONS, LATS), F32),
            pltpu.VMEM((LEVELS, LONS, LATS), F32),
            pltpu.VMEM((LONS, LATS), F32),
            pltpu.VMEM((LEVELS, LONS, MEMBERS, LATS), F32),
            pltpu.VMEM((LONS * RECORD, LATS), F32),
            pltpu.VMEM((4, LEVELS, LONS, LATS), F32),
            pltpu.VMEM((2, LEVELS, LONS, LATS), F32),
            pltpu.VMEM((2, LEVELS * GROUP * 8, LATS), F32),
            pltpu.SemaphoreType.DMA((5,)),
            pltpu.SemaphoreType.DMA((5,)),
            pltpu.SemaphoreType.DMA((GROUPS,)),
            pltpu.SemaphoreType.DMA((4,)),
        ],
        name="sweeps",
    )(field, rate, diffusivity)


def solve_kernel(*refs):
    pieces, outs, (records, states, in_sems, out_sems) = refs[:4], refs[4:8], refs[8:]
    here = lax.axis_index("lev")
    copies = []
    for shift in range(BLOCKS):
        source = lax.rem(here - shift + BLOCKS, BLOCKS)
        rows = pl.ds(source * (SHARE * RECORD), SHARE * RECORD)
        copies.append(pltpu.make_async_copy(pieces[shift], records.at[rows, :], in_sems.at[shift]))
    wait_all(start_all(copies))

    def run(lon, carry):
        def exit_of(block, number, half):
            at = (block * SHARE + lon) * RECORD + 16 * number + 8 * half
            return records[pl.ds(pl.multiple_of(at, 8), 8), :]

        def response(block, which):
            return row(records, (block * SHARE + lon) * RECORD + STATES + which)

        for half in range(2):
            zero = jnp.zeros((8, LATS), F32)
            f1, b1, f2, b2 = ([zero] * BLOCKS for _ in range(4))
            for d in range(BLOCKS - 1):
                f1[d + 1] = exit_of(d, 0, half) + response(d, 0) * f1[d]
            for d in range(BLOCKS - 1, 0, -1):
                b1[d - 1] = exit_of(d, 1, half) + response(d, 1) * f1[d] + response(d, 0) * b1[d]
            for d in range(BLOCKS - 1):
                f2[d + 1] = (
                    exit_of(d, 2, half)
                    + response(d, 2) * f1[d]
                    + response(d, 3) * b1[d]
                    + response(d, 0) * f2[d]
                )
            for d in range(BLOCKS - 1, 0, -1):
                b2[d - 1] = (
                    exit_of(d, 3, half)
                    + response(d, 4) * f1[d]
                    + response(d, 5) * b1[d]
                    + response(d, 1) * f2[d]
                    + response(d, 0) * b2[d]
                )
            for d in range(BLOCKS):
                for number, entering in enumerate((f1, b1, f2, b2)):
                    at = (d * SHARE + lon) * STATES + 16 * number + 8 * half
                    states[pl.ds(pl.multiple_of(at, 8), 8), :] = entering[d]
        return carry

    lax.fori_loop(0, SHARE, run, 0)
    copies = []
    for shift in range(BLOCKS):
        target = lax.rem(here + shift, BLOCKS)
        rows = pl.ds(target * (SHARE * STATES), SHARE * STATES)
        copies.append(pltpu.make_async_copy(states.at[rows, :], outs[shift], out_sems.at[shift]))
    wait_all(start_all(copies))


def solve_call(pieces):
    return pl.pallas_call(
        solve_kernel,
        out_shape=[shape(SHARE * STATES, LATS)] * BLOCKS,
        in_specs=[ANY] * BLOCKS,
        out_specs=[ANY] * BLOCKS,
        scratch_shapes=[
            pltpu.VMEM((BLOCKS * SHARE * RECORD, LATS), F32),
            pltpu.VMEM((BLOCKS * SHARE * STATES, LATS), F32),
            pltpu.SemaphoreType.DMA((4,)),
            pltpu.SemaphoreType.DMA((4,)),
        ],
        name="solve",
    )(*pieces)


def pieces_into(pieces, target, rows_each, sems):
    here = lax.axis_index("lev")
    copies = []
    for shift, piece in enumerate(pieces):
        source = lax.rem(here - shift + BLOCKS, BLOCKS)
        rows = pl.ds(pl.multiple_of(source * rows_each, 8), rows_each)
        copies.append(pltpu.make_async_copy(piece, target.at[rows, :], sems.at[shift]))
    return copies


def corrected_block(value_of, profile_of, entering):
    parts = []
    for level in range(SLAB):
        mine = [profile_of(n, level) for n in range(4)]
        for half in range(2):
            value = value_of(level, half)
            for n in range(4):
                value = value + mine[n] * entering[half][n]
            parts.append(value)
    return jnp.concatenate(parts, axis=0)


def entering_of(states, start):
    return [[states[start + 16 * n + 8 * half : start + 16 * n + 8 * half + 8, :] for n in range(4)] for half in range(2)]


def spread(kappa_row):
    return jnp.transpose(jnp.broadcast_to(kappa_row, (LATS, LATS)))


def diffuse(rows, spread_rows, base, wide):
    slots = rows.shape[0] // (2 * PAD)

    def at(which, lon, offset):
        return (which * slots + base + lon) * PAD + 8 + offset

    for step in range(SMOOTH):
        source, target = step % 2, (step + 1) % 2

        def tile(t, carry):
            top = pl.multiple_of(8 * t, 8)
            west = rows[pl.ds(at(source, step, top), 8), :]
            here = rows[pl.ds(at(source, step + 1, top), 8), :]
            for lon in range(step + 1, wide - step - 1):
                east = rows[pl.ds(at(source, lon + 1, top), 8), :]
                north = rows[pl.ds(at(source, lon, top - 1), 8), :]
                south = rows[pl.ds(at(source, lon, top + 1), 8), :]
                k = spread_rows[base + lon, pl.ds(top, 8), :]
                around = (east + west) + (north + south)
                rows[pl.ds(at(target, lon, top), 8), :] = here + k * (around - 4.0 * here)
                west, here = here, east
            return carry

        lax.fori_loop(0, LATS // 8, tile, 0, unroll=2)


def clear_pads(buffers):
    zero = jnp.zeros((8, LATS), F32)
    for which in range(2):
        for lon in range(buffers.shape[1]):
            buffers[which, lon, 0:8, :] = zero
            buffers[which, lon, PAD - 8 : PAD, :] = zero


def inner_kernel(local, profiles, diffusivity, s0, s1, s2, s3, out, *refs):
    ls, rows, states, kappa, spread_rows, buffers, made, in_sems, state_sems, local_sems, out_sems = refs
    first = start_all(
        pieces_into((s0, s1, s2, s3), states, SHARE * STATES, state_sems)
        + [pltpu.make_async_copy(diffusivity, kappa, in_sems.at[0]), pltpu.make_async_copy(profiles, rows, in_sems.at[1])]
    )

    def load(slab):
        levels = pl.ds(slab * SLAB, SLAB)
        return pltpu.make_async_copy(local.at[levels], ls.at[levels], local_sems.at[slab])

    def save(slab):
        part = pl.ds(slab * SLAB * MEMBERS, SLAB * MEMBERS)
        return pltpu.make_async_copy(made.at[part], out.at[part], out_sems.at[slab])

    for slab in range(SLABS):
        load(slab).start()
    clear_pads(buffers)
    wait_all(first)
    for lon in range(LONS):
        spread_rows[lon] = spread(kappa[lon : lon + 1, :])
    profile_rows = rows.reshape(4 * LEVELS * LONS, LATS)
    made_rows = made.reshape(LEVELS * MEMBERS * LONS, LATS)
    flat = buffers.reshape(2 * LONS * PAD, LATS)

    def run(slab, carry):
        load(slab).wait()
        for lon in range(LONS):
            block = corrected_block(
                lambda level, half: ls[slab * SLAB + level, lon, 8 * half : 8 * half + 8, :],
                lambda n, level: row(profile_rows, (n * LEVELS + slab * SLAB + level) * LONS + lon),
                entering_of(states, slot(lon) * STATES),
            )
            buffers[0, lon, 8 : 8 + LATS, :] = jnp.transpose(block)
        diffuse(flat, spread_rows, 0, LONS)
        for lon in range(GROUP, LONS - GROUP):
            block = jnp.transpose(buffers[0, lon, 8 : 8 + LATS, :])
            for part in range(2 * SLAB):
                start = (slab * SLAB * MEMBERS + 8 * part) * LONS + lon
                made_rows[pl.ds(start, 8, stride=LONS), :] = block[8 * part : 8 * part + 8, :]
        save(slab).start()
        return carry

    lax.fori_loop(0, SLABS, run, 0)
    wait_all([save(slab) for slab in range(SLABS)])


def inner_call(local, profiles, diffusivity, pieces):
    return pl.pallas_call(
        inner_kernel,
        out_shape=shape(LEVELS * MEMBERS, LONS, LATS),
        in_specs=[ANY] * 7,
        out_specs=ANY,
        scratch_shapes=[
            pltpu.VMEM((LEVELS, LONS, MEMBERS, LATS), F32),
            pltpu.VMEM((4, LEVELS, LONS, LATS), F32),
            pltpu.VMEM((LONS * STATES, LATS), F32),
            pltpu.VMEM((LONS, LATS), F32),
            pltpu.VMEM((LONS, LATS, LATS), F32),
            pltpu.VMEM((2, LONS, PAD, LATS), F32),
            pltpu.VMEM((LEVELS * MEMBERS, LONS, LATS), F32),
            pltpu.SemaphoreType.DMA((2,)),
            pltpu.SemaphoreType.DMA((4,)),
            pltpu.SemaphoreType.DMA((SLABS,)),
            pltpu.SemaphoreType.DMA((SLABS,)),
        ],
        cost_estimate=pl.CostEstimate(flops=10**8, transcendentals=0, bytes_accessed=10**7),
        name="inner",
    )(local, profiles, diffusivity, *pieces)


def outer_kernel(begun, local, profiles, diffusivity, s0, s1, s2, s3, low, high, low_s, high_s, out, *refs):
    ls, rows, states, kappa, spread_rows, buffers, made, halos, halo_states, *sems = refs
    in_sems, state_sems, halo_sems, local_sems, begun_sems, out_sems = sems
    here = lax.axis_index("lev")
    first = start_all(
        pieces_into((s0, s1, s2, s3), states, SHARE * STATES, state_sems)
        + [pltpu.make_async_copy(diffusivity, kappa, in_sems.at[0]), pltpu.make_async_copy(profiles, rows, in_sems.at[1])]
        + [
            pltpu.make_async_copy(source.at[pl.ds(shift * STATES, STATES), :], halo_states.at[side, lax.rem(here - shift + BLOCKS, BLOCKS)], halo_sems.at[side, shift])
            for side, source in enumerate((low_s, high_s))
            for shift in range(BLOCKS)
        ]
    )

    def loads(slab):
        levels = pl.ds(slab * SLAB, SLAB)
        part = pl.ds(slab * SLAB * MEMBERS, SLAB * MEMBERS)
        copies = []
        for side, (halo, lon) in enumerate(((low, 0), (high, 16))):
            copies.append(pltpu.make_async_copy(local.at[levels, pl.ds(lon, 8)], ls.at[side, levels], local_sems.at[slab, side]))
            copies.append(pltpu.make_async_copy(halo.at[levels], halos.at[side, levels], local_sems.at[slab, 2 + side]))
            copies.append(pltpu.make_async_copy(begun.at[part, pl.ds(lon, 8), :], made.at[side, part], begun_sems.at[slab, side]))
        return copies

    def saves(slab):
        part = pl.ds(slab * SLAB * MEMBERS, SLAB * MEMBERS)
        return [
            pltpu.make_async_copy(made.at[side, part], out.at[part, pl.ds(lon, 8), :], out_sems.at[slab, side])
            for side, lon in enumerate((0, 16))
        ]

    for slab in range(SLABS):
        start_all(loads(slab))
    clear_pads(buffers)
    wait_all(first)
    wait_all(loads(0))
    for side in range(2):
        for j in range(8):
            lon = 16 * side + j
            at = 4 + j if side == 0 else 12 + j
            spread_rows[at] = spread(kappa[lon : lon + 1, :])
        for j in range(GROUP):
            spread_rows[j if side == 0 else 20 + j] = spread(halos[side, 0, j, MEMBERS + 4 : MEMBERS + 5, :])
    profile_rows = rows.reshape(4 * LEVELS * LONS, LATS)
    halo_rows = halos.reshape(2 * LEVELS * GROUP * (MEMBERS + 8), LATS)
    made_rows = made.reshape(2 * LEVELS * MEMBERS * 8, LATS)
    flat = buffers.reshape(2 * LONS * PAD, LATS)

    def run(slab, carry):
        @pl.when(slab > 0)
        def _():
            wait_all(loads(slab))

        for side in range(2):
            for j in range(8):
                lon = 16 * side + j
                at = 4 + j if side == 0 else 12 + j
                block = corrected_block(
                    lambda level, half: ls[side, slab * SLAB + level, j, 8 * half : 8 * half + 8, :],
                    lambda n, level: row(profile_rows, (n * LEVELS + slab * SLAB + level) * LONS + lon),
                    entering_of(states, slot(lon) * STATES),
                )
                buffers[0, at, 8 : 8 + LATS, :] = jnp.transpose(block)
            for j in range(GROUP):
                at = j if side == 0 else 20 + j
                block = corrected_block(
                    lambda level, half: halos[side, slab * SLAB + level, j, 8 * half : 8 * half + 8, :],
                    lambda n, level: row(halo_rows, ((side * LEVELS + slab * SLAB + level) * GROUP + j) * (MEMBERS + 8) + MEMBERS + n),
                    entering_of(halo_states.at[side, j], 0),
                )
                buffers[0, at, 8 : 8 + LATS, :] = jnp.transpose(block)
        for side in range(2):
            diffuse(flat, spread_rows, 12 * side, 12)
        for side in range(2):
            for j in range(GROUP):
                block = jnp.transpose(buffers[0, 12 * side + 4 + j, 8 : 8 + LATS, :])
                for part in range(2 * SLAB):
                    start = ((side * LEVELS + slab * SLAB) * MEMBERS + 8 * part) * 8 + 4 * side + j
                    made_rows[pl.ds(start, 8, stride=8), :] = block[8 * part : 8 * part + 8, :]
        start_all(saves(slab))
        return carry

    lax.fori_loop(0, SLABS, run, 0)
    for slab in range(SLABS):
        wait_all(saves(slab))


def outer_call(begun, local, profiles, diffusivity, pieces, low, high, low_s, high_s):
    return pl.pallas_call(
        outer_kernel,
        out_shape=shape(LEVELS * MEMBERS, LONS, LATS),
        in_specs=[ANY] * 12,
        out_specs=ANY,
        input_output_aliases={0: 0},
        scratch_shapes=[
            pltpu.VMEM((2, LEVELS, 8, MEMBERS, LATS), F32),
            pltpu.VMEM((4, LEVELS, LONS, LATS), F32),
            pltpu.VMEM((LONS * STATES, LATS), F32),
            pltpu.VMEM((LONS, LATS), F32),
            pltpu.VMEM((LONS, LATS, LATS), F32),
            pltpu.VMEM((2, LONS, PAD, LATS), F32),
            pltpu.VMEM((2, LEVELS * MEMBERS, 8, LATS), F32),
            pltpu.VMEM((2, LEVELS, GROUP, MEMBERS + 8, LATS), F32),
            pltpu.VMEM((2, GROUP, STATES, LATS), F32),
            pltpu.SemaphoreType.DMA((2,)),
            pltpu.SemaphoreType.DMA((4,)),
            pltpu.SemaphoreType.DMA((2, 4)),
            pltpu.SemaphoreType.DMA((SLABS, 4)),
            pltpu.SemaphoreType.DMA((SLABS, 2)),
            pltpu.SemaphoreType.DMA((SLABS, 2)),
        ],
        name="outer",
    )(begun, local, profiles, diffusivity, *pieces, low, high, low_s, high_s)


def shifted(pieces):
    moved = [pieces[0]]
    for shift in (1, 2, 3):
        moved.append(lax.ppermute(pieces[shift], "lev", [(i, (i + shift) % BLOCKS) for i in range(BLOCKS)]))
    return moved


def exchanged(to_low, to_high):
    count = lax.axis_size("col")
    forward = [(i, i + 1) for i in range(count - 1)]
    backward = [(b, a) for a, b in forward]
    return lax.ppermute(to_high, "col", forward), lax.ppermute(to_low, "col", backward)


def per_device(control_field, decay_rate, diffusivity):
    field = control_field.reshape(LEVELS * MEMBERS, LONS, LATS)
    local, *pieces, profiles, to_low, to_high = sweep_call(field, decay_rate, diffusivity)
    pieces = shifted(pieces)
    low, high = exchanged(to_low, to_high)
    states = shifted(solve_call(pieces))
    low_s, high_s = exchanged(
        jnp.concatenate([piece[:STATES] for piece in states]),
        jnp.concatenate([piece[STATES : 2 * STATES] for piece in states]),
    )
    begun = inner_call(local, profiles, diffusivity, states)
    out = outer_call(begun, local, profiles, diffusivity, states, low, high, low_s, high_s)
    return out.reshape(control_field.shape)


def solution(mesh):
    in_specs = (P("lev", None, "col", None), P("lev", "col", None), P("col", None))
    out_specs = P("lev", None, "col", None)
    return jax.shard_map(
        per_device, mesh=mesh, in_specs=in_specs, out_specs=out_specs, check_vma=False
    )
```

time: 232 us -> 70.5 us (0.30)
  the two profiles are of different devices: /device:TPU:7 before, /device:TPU:64 now
where the time goes in v2:
time: 70.5 us; the launch traced here: 70.2 us
  Pallas kernels  31.9 us (45%)
  starting transfers between devices  26.4 us (37%)
  waiting for transfers between devices  7.91 us (11%)
  local copies, waits for them, and re-layouts  3.7 us (5%)
    pallas_call x1, Pallas kernels, outer_call(): pl.pallas_call(outer_kernel, out_shape=shape(LEVELS * MEMBERS, LONS, LATS...  12.1 us
    ppermute x2, starting transfers between devices, exchanged(): lax.ppermute(to_low, 'col', backward)  11.5 us
    pallas_call x1, Pallas kernels, inner_call(): pl.pallas_call(inner_kernel, out_shape=shape(LEVELS * MEMBERS, LONS, LATS...  11.3 us
    ppermute x6, starting transfers between devices, shifted(): lax.ppermute(pieces[shift], 'lev', [(i, (i + shift) % BLOCKS) for i in ra...  11.1 us
    ppermute x6, waiting for transfers between devices, shifted(): lax.ppermute(pieces[shift], 'lev', [(i, (i + shift) % BLOCKS) for i in ra...  7.9 us
    pallas_call x1, Pallas kernels, sweep_call(): pl.pallas_call(sweep_kernel, out_shape=outs, in_specs=[ANY] * 3, out_spec...  6.16 us
    ppermute x2, starting transfers between devices, exchanged(): lax.ppermute(to_high, 'col', forward)  3.83 us
    unnamed x20, local copies, waits for them, and re-layouts  2.91 us
  transfers between devices with their start and end apart: 10, of which 3 were waited for; matrix products, arithmetic and copies ran while one was open for 1% of the time, Pallas kernels for 20%

profile of v2, /device:TPU:64, one launch (start us, length us, event | category | flops | bytes accessed | tf_op | source)
XLA Modules:
  0.0 70.2 jit_solution(8352989797042720623)
XLA Ops:
  0.0 6.2 %sweeps.1 = (f32[24,24,16,128]{3,2,1,0:T(8,128)}, f32[432,128]{1,0:T(8,128)}, f32[432,128]{1,0:T(8,128)}, f32[432,128]{1,0:T(8,128)}, f32[432,128]{1,0:T(8,128)}...) custom-call(f32[384,24,128]{2,1,0:T(8,128)} %bitcast.2, f32[24,24,128]{2,1,0:T(8,128)} %rate.1, ...), custom_call_target="tpu_custom_call" | custom-call | tf_op jit(solution)/shard_map/sweeps/pallas_call | solution.py:170
  6.2 1.6 %collective-permute-start = (f32[432,128]{1,0:T(8,128)}, f32[432,128]{1,0:T(8,128)S(1)}, u32[]{:S(2)}, u32[]{:S(2)}) collective-permute-start(f32[432,128]{1,0:T(8,128)} %get-tuple-element.20), channel_id=1, source_target_pairs={{0,32},{32,64},{64,96},{96,0},{1,33},{33,65},{65,97},{97,1},{2,34}... | collective-permute-start | bytes 663560 | tf_op jit(solution)/shard_map/ppermute | solution.py:517
  7.8 2.9 %collective-permute-start.1 = (f32[432,128]{1,0:T(8,128)}, f32[432,128]{1,0:T(8,128)S(1)}, u32[]{:S(2)}, u32[]{:S(2)}) collective-permute-start(f32[432,128]{1,0:T(8,128)} %get-tuple-element.21), channel_id=1, source_target_pairs={{0,64},{32,96},{64,0},{96,32},{1,65},{33,97},{65,1},{97,33},{2,66}... | collective-permute-start | bytes 663560 | tf_op jit(solution)/shard_map/ppermute | solution.py:517
  10.7 1.3 %collective-permute-start.2 = (f32[432,128]{1,0:T(8,128)}, f32[432,128]{1,0:T(8,128)S(1)}, u32[]{:S(2)}, u32[]{:S(2)}) collective-permute-start(f32[432,128]{1,0:T(8,128)} %get-tuple-element.22), channel_id=1, source_target_pairs={{0,96},{32,0},{64,32},{96,64},{1,97},{33,1},{65,33},{97,65},{2,98}... | collective-permute-start | bytes 663560 | tf_op jit(solution)/shard_map/ppermute | solution.py:517
  12.1 1.9 %collective-permute-start.6 = (f32[24,4,24,128]{3,2,1,0:T(8,128)}, f32[24,4,24,128]{3,2,1,0:T(8,128)S(1)}, u32[]{:S(2)}, u32[]{:S(2)}) collective-permute-start(f32[24,4,24,128]{3,2,1,0:T(8,128)} %get-tuple-element.27), channel_id=1, source_target_pairs={{0,1},{1,2},{2,3},{3,4},{4,5},{5,6},{6,7},{7,8},{8,9},{9,10},{10,1... | collective-permute-start | bytes 3538952 | tf_op jit(solution)/shard_map/ppermute | solution.py:525
  14.0 5.8 %collective-permute-start.7 = (f32[24,4,24,128]{3,2,1,0:T(8,128)}, f32[24,4,24,128]{3,2,1,0:T(8,128)S(1)}, u32[]{:S(2)}, u32[]{:S(2)}) collective-permute-start(f32[24,4,24,128]{3,2,1,0:T(8,128)} %get-tuple-element.28), channel_id=1, source_target_pairs={{1,0},{2,1},{3,2},{4,3},{5,4},{6,5},{7,6},{8,7},{9,8},{10,9},{11,1... | collective-permute-start | bytes 3538952 | tf_op jit(solution)/shard_map/ppermute | solution.py:525
  19.7 0.0 collective-permute-done.refs_1_
  19.7 0.0 copy-start.5
  19.8 1.0 %collective-permute-done.1.refs_2_ = f32[432,128]{1,0:T(8,128)S(1)} collective-permute-done((f32[432,128]{1,0:T(8,128)}, f32[432,128]{1,0:T(8,128)S(1)}, u32[]{:S(2)}, u32[]{:S(2)}) %collective-permute-start.1) | collective-permute-done | bytes 221216 | tf_op jit(solution)/shard_map/ppermute | solution.py:517
  20.8 0.0 copy-start.6
  20.8 0.0 collective-permute-done.2.refs_3_
  20.8 0.0 copy-start.7
  20.8 0.0 copy-done.5
  20.8 0.7 copy-done.6
  21.5 0.1 copy-done.7
  21.6 2.4 %solve.1 = (f32[384,128]{1,0:T(8,128)}, f32[384,128]{1,0:T(8,128)}, f32[384,128]{1,0:T(8,128)}, f32[384,128]{1,0:T(8,128)}) custom-call(f32[432,128]{1,0:T(8,128)} %get-tuple-element.19.refs_0_, f32[432,128]{1,0:T(8,128)} %copy-done.5, f32[432,128]{1,0:T(8,128)} %copy-done.6, f32[432,128]{1,0:T(8,128)} %copy-done.7), custom_call_target="tpu_custom_call" | custom-call | tf_op jit(solution)/shard_map/solve/pallas_call | solution.py:249
  24.0 1.2 %collective-permute-start.3 = (f32[384,128]{1,0:T(8,128)}, f32[384,128]{1,0:T(8,128)S(1)}, u32[]{:S(2)}, u32[]{:S(2)}) collective-permute-start(f32[384,128]{1,0:T(8,128)} %get-tuple-element.24), channel_id=1, source_target_pairs={{0,32},{32,64},{64,96},{96,0},{1,33},{33,65},{65,97},{97,1},{2,34}... | collective-permute-start | bytes 589832 | tf_op jit(solution)/shard_map/ppermute | solution.py:517
  25.2 2.4 %collective-permute-start.4 = (f32[384,128]{1,0:T(8,128)}, f32[384,128]{1,0:T(8,128)S(1)}, u32[]{:S(2)}, u32[]{:S(2)}) collective-permute-start(f32[384,128]{1,0:T(8,128)} %get-tuple-element.25), channel_id=1, source_target_pairs={{0,64},{32,96},{64,0},{96,32},{1,65},{33,97},{65,1},{97,33},{2,66}... | collective-permute-start | bytes 589832 | tf_op jit(solution)/shard_map/ppermute | solution.py:517
  27.6 1.6 %collective-permute-start.5 = (f32[384,128]{1,0:T(8,128)}, f32[384,128]{1,0:T(8,128)S(1)}, u32[]{:S(2)}, u32[]{:S(2)}) collective-permute-start(f32[384,128]{1,0:T(8,128)} %get-tuple-element.26), channel_id=1, source_target_pairs={{0,96},{32,0},{64,32},{96,64},{1,97},{33,1},{65,33},{97,65},{2,98}... | collective-permute-start | bytes 589832 | tf_op jit(solution)/shard_map/ppermute | solution.py:517
  29.2 0.8 %fusion = (f32[64,128]{1,0:T(8,128)S(1)}, f32[64,128]{1,0:T(8,128)S(1)}) fusion(f32[384,128]{1,0:T(8,128)} %get-tuple-element.23.s0), kind=kLoop, calls=%fused_computation.2 | loop fusion | bytes 131072 | tf_op jit(solution)/shard_map/slice | solution.py:535
  30.0 1.5 %collective-permute-done.3.s1 = f32[384,128]{1,0:T(8,128)S(1)} collective-permute-done((f32[384,128]{1,0:T(8,128)}, f32[384,128]{1,0:T(8,128)S(1)}, u32[]{:S(2)}, u32[]{:S(2)}) %collective-permute-start.3) | collective-permute-done | bytes 196640 | tf_op jit(solution)/shard_map/ppermute | solution.py:517
  31.4 0.0 copy-start.2
  31.4 5.4 %collective-permute-done.4.s2 = f32[384,128]{1,0:T(8,128)S(1)} collective-permute-done((f32[384,128]{1,0:T(8,128)}, f32[384,128]{1,0:T(8,128)S(1)}, u32[]{:S(2)}, u32[]{:S(2)}) %collective-permute-start.4) | collective-permute-done | bytes 196640 | tf_op jit(solution)/shard_map/ppermute | solution.py:517
  36.8 0.0 copy-start.3
  36.8 0.0 collective-permute-done.5.s3
  36.8 0.0 copy-start.4
  36.9 1.9 %collective-permute-start.8 = (f32[256,128]{1,0:T(8,128)S(1)}, f32[256,128]{1,0:T(8,128)S(1)}, u32[]{:S(2)}, u32[]{:S(2)}) collective-permute-start(f32[256,128]{1,0:T(8,128)S(1)} %pad_maximum_fusion), channel_id=1, source_target_pairs={{0,1},{1,2},{2,3},{3,4},{4,5},{5,6},{6,7},{7,8},{8,9},{9,10},{10,1... | collective-permute-start | bytes 393224 | tf_op jit(solution)/shard_map/ppermute | solution.py:525
  38.8 5.8 %collective-permute-start.9 = (f32[256,128]{1,0:T(8,128)S(1)}, f32[256,128]{1,0:T(8,128)S(1)}, u32[]{:S(2)}, u32[]{:S(2)}) collective-permute-start(f32[256,128]{1,0:T(8,128)S(1)} %pad_maximum_fusion.1), channel_id=1, source_target_pairs={{1,0},{2,1},{3,2},{4,3},{5,4},{6,5},{7,6},{8,7},{9,8},{10,9},{11,1... | collective-permute-start | bytes 393224 | tf_op jit(solution)/shard_map/ppermute | solution.py:525
  44.6 0.0 copy-done.2
  44.6 0.0 copy-done.3
  44.6 0.0 copy-done.4
  44.6 11.3 %inner.1.begun = f32[384,24,128]{2,1,0:T(8,128)} custom-call(f32[24,24,16,128]{3,2,1,0:T(8,128)} %get-tuple-element.17.local, f32[4,24,24,128]{3,2,1,0:T(8,128)} %get-tuple-element.18.profiles, f32[24,128]{1,0:T(8,128)} %diffusivity.5, f32[384,128]{1,0:T(8,128)} %get-tuple-element.23.s0, f32[384,128]{1,0:T(8,128)} %copy-done.2, f32[384,128]{1,0:T(8,128)} %copy-done.3, ...), custom_call_target="tpu_custom_call" | custom-call | flops 100000000 | bytes 10000000 | tf_op jit(solution)/shard_map/inner/pallas_call | solution.py:376
  55.9 0.0 collective-permute-done.8.low_s
  55.9 0.0 copy-start.8
  56.0 0.0 collective-permute-done.9.high_s
  56.0 0.0 copy-start.9
  56.0 0.0 collective-permute-done.6.low
  56.0 0.0 copy-start
  56.0 0.0 collective-permute-done.7.high
  56.0 0.6 copy-done.8
  56.6 0.0 copy-done.9
  56.6 0.5 copy-done
  57.1 0.0 copy-start.1
  57.1 1.0 %copy-done.1 = f32[24,4,24,128]{3,2,1,0:T(8,128)} copy-done((f32[24,4,24,128]{3,2,1,0:T(8,128)}, f32[24,4,24,128]{3,2,1,0:T(8,128)S(1)}, u32[]{:S(2)}) %copy-start.1) | copy-done | bytes 1179672
  58.1 12.1 %outer.1 = f32[384,24,128]{2,1,0:T(8,128)} custom-call(f32[384,24,128]{2,1,0:T(8,128)} %inner.1.begun, f32[24,24,16,128]{3,2,1,0:T(8,128)} %get-tuple-element.17.local, f32[4,24,24,128]{3,2,1,0:T(8,128)} %get-tuple-element.18.profiles, f32[24,128]{1,0:T(8,128)} %diffusivity.5, f32[384,128]{1,0:T(8,128)} %get-tuple-element.23.s0, ...), custom_call_target="tpu_custom_call", output_to_operand_aliasing={{}: (0, {})} | custom-call | tf_op jit(solution)/shard_map/outer/pallas_call | solution.py:487
  (5 shorter events, 0.0 us)
Async XLA Ops:
  6.2 13.6 %collective-permute-start = (f32[432,128]{1,0:T(8,128)}, f32[432,128]{1,0:T(8,128)S(1)}, u32[]{:S(2)}, u32[]{:S(2)}) collective-permute-start(f32[432,128]{1,0:T(8,128)} %get-tuple-element.20), channel_id=1, source_target_pairs={{0,32},{32,64},{64,96},{96,0},{1,33},{33,65},{65,97},{97,1},{2,34}... | collective-permute-start | bytes 663560 | tf_op jit(solution)/shard_map/ppermute | solution.py:517
  7.8 13.0 %collective-permute-start.1 = (f32[432,128]{1,0:T(8,128)}, f32[432,128]{1,0:T(8,128)S(1)}, u32[]{:S(2)}, u32[]{:S(2)}) collective-permute-start(f32[432,128]{1,0:T(8,128)} %get-tuple-element.21), channel_id=1, source_target_pairs={{0,64},{32,96},{64,0},{96,32},{1,65},{33,97},{65,1},{97,33},{2,66}... | collective-permute-start | bytes 663560 | tf_op jit(solution)/shard_map/ppermute | solution.py:517
  10.7 10.1 %collective-permute-start.2 = (f32[432,128]{1,0:T(8,128)}, f32[432,128]{1,0:T(8,128)S(1)}, u32[]{:S(2)}, u32[]{:S(2)}) collective-permute-start(f32[432,128]{1,0:T(8,128)} %get-tuple-element.22), channel_id=1, source_target_pairs={{0,96},{32,0},{64,32},{96,64},{1,97},{33,1},{65,33},{97,65},{2,98}... | collective-permute-start | bytes 663560 | tf_op jit(solution)/shard_map/ppermute | solution.py:517
  12.1 43.9 %collective-permute-start.6 = (f32[24,4,24,128]{3,2,1,0:T(8,128)}, f32[24,4,24,128]{3,2,1,0:T(8,128)S(1)}, u32[]{:S(2)}, u32[]{:S(2)}) collective-permute-start(f32[24,4,24,128]{3,2,1,0:T(8,128)} %get-tuple-element.27), channel_id=1, source_target_pairs={{0,1},{1,2},{2,3},{3,4},{4,5},{5,6},{6,7},{7,8},{8,9},{9,10},{10,1... | collective-permute-start | bytes 3538952 | tf_op jit(solution)/shard_map/ppermute | solution.py:525
  14.0 42.0 %collective-permute-start.7 = (f32[24,4,24,128]{3,2,1,0:T(8,128)}, f32[24,4,24,128]{3,2,1,0:T(8,128)S(1)}, u32[]{:S(2)}, u32[]{:S(2)}) collective-permute-start(f32[24,4,24,128]{3,2,1,0:T(8,128)} %get-tuple-element.28), channel_id=1, source_target_pairs={{1,0},{2,1},{3,2},{4,3},{5,4},{6,5},{7,6},{8,7},{9,8},{10,9},{11,1... | collective-permute-start | bytes 3538952 | tf_op jit(solution)/shard_map/ppermute | solution.py:525
  19.7 1.1 %copy-start.5 = (f32[432,128]{1,0:T(8,128)}, f32[432,128]{1,0:T(8,128)S(1)}, u32[]{:S(2)}) copy-start(f32[432,128]{1,0:T(8,128)S(1)} %collective-permute-done.refs_1_) | copy-start | bytes 663556
  20.8 0.7 %copy-start.6 = (f32[432,128]{1,0:T(8,128)}, f32[432,128]{1,0:T(8,128)S(1)}, u32[]{:S(2)}) copy-start(f32[432,128]{1,0:T(8,128)S(1)} %collective-permute-done.1.refs_2_) | copy-start | bytes 663556
  20.8 0.8 %copy-start.7 = (f32[432,128]{1,0:T(8,128)}, f32[432,128]{1,0:T(8,128)S(1)}, u32[]{:S(2)}) copy-start(f32[432,128]{1,0:T(8,128)S(1)} %collective-permute-done.2.refs_3_) | copy-start | bytes 663556
  24.0 7.4 %collective-permute-start.3 = (f32[384,128]{1,0:T(8,128)}, f32[384,128]{1,0:T(8,128)S(1)}, u32[]{:S(2)}, u32[]{:S(2)}) collective-permute-start(f32[384,128]{1,0:T(8,128)} %get-tuple-element.24), channel_id=1, source_target_pairs={{0,32},{32,64},{64,96},{96,0},{1,33},{33,65},{65,97},{97,1},{2,34}... | collective-permute-start | bytes 589832 | tf_op jit(solution)/shard_map/ppermute | solution.py:517
  25.2 11.6 %collective-permute-start.4 = (f32[384,128]{1,0:T(8,128)}, f32[384,128]{1,0:T(8,128)S(1)}, u32[]{:S(2)}, u32[]{:S(2)}) collective-permute-start(f32[384,128]{1,0:T(8,128)} %get-tuple-element.25), channel_id=1, source_target_pairs={{0,64},{32,96},{64,0},{96,32},{1,65},{33,97},{65,1},{97,33},{2,66}... | collective-permute-start | bytes 589832 | tf_op jit(solution)/shard_map/ppermute | solution.py:517
  27.6 9.2 %collective-permute-start.5 = (f32[384,128]{1,0:T(8,128)}, f32[384,128]{1,0:T(8,128)S(1)}, u32[]{:S(2)}, u32[]{:S(2)}) collective-permute-start(f32[384,128]{1,0:T(8,128)} %get-tuple-element.26), channel_id=1, source_target_pairs={{0,96},{32,0},{64,32},{96,64},{1,97},{33,1},{65,33},{97,65},{2,98}... | collective-permute-start | bytes 589832 | tf_op jit(solution)/shard_map/ppermute | solution.py:517
  31.4 13.2 %copy-start.2 = (f32[384,128]{1,0:T(8,128)}, f32[384,128]{1,0:T(8,128)S(1)}, u32[]{:S(2)}) copy-start(f32[384,128]{1,0:T(8,128)S(1)} %collective-permute-done.3.s1) | copy-start | bytes 589828
  36.8 7.8 %copy-start.3 = (f32[384,128]{1,0:T(8,128)}, f32[384,128]{1,0:T(8,128)S(1)}, u32[]{:S(2)}) copy-start(f32[384,128]{1,0:T(8,128)S(1)} %collective-permute-done.4.s2) | copy-start | bytes 589828
  36.8 7.8 %copy-start.4 = (f32[384,128]{1,0:T(8,128)}, f32[384,128]{1,0:T(8,128)S(1)}, u32[]{:S(2)}) copy-start(f32[384,128]{1,0:T(8,128)S(1)} %collective-permute-done.5.s3) | copy-start | bytes 589828
  36.9 19.1 %collective-permute-start.8 = (f32[256,128]{1,0:T(8,128)S(1)}, f32[256,128]{1,0:T(8,128)S(1)}, u32[]{:S(2)}, u32[]{:S(2)}) collective-permute-start(f32[256,128]{1,0:T(8,128)S(1)} %pad_maximum_fusion), channel_id=1, source_target_pairs={{0,1},{1,2},{2,3},{3,4},{4,5},{5,6},{6,7},{7,8},{8,9},{9,10},{10,1... | collective-permute-start | bytes 393224 | tf_op jit(solution)/shard_map/ppermute | solution.py:525
  38.8 17.1 %collective-permute-start.9 = (f32[256,128]{1,0:T(8,128)S(1)}, f32[256,128]{1,0:T(8,128)S(1)}, u32[]{:S(2)}, u32[]{:S(2)}) collective-permute-start(f32[256,128]{1,0:T(8,128)S(1)} %pad_maximum_fusion.1), channel_id=1, source_target_pairs={{1,0},{2,1},{3,2},{4,3},{5,4},{6,5},{7,6},{8,7},{9,8},{10,9},{11,1... | collective-permute-start | bytes 393224 | tf_op jit(solution)/shard_map/ppermute | solution.py:525
  55.9 0.6 copy-start.8
  56.0 0.7 copy-start.9
  56.0 1.1 %copy-start = (f32[24,4,24,128]{3,2,1,0:T(8,128)}, f32[24,4,24,128]{3,2,1,0:T(8,128)S(1)}, u32[]{:S(2)}) copy-start(f32[24,4,24,128]{3,2,1,0:T(8,128)S(1)} %collective-permute-done.6.low) | copy-start | bytes 3538948
  57.1 1.0 %copy-start.1 = (f32[24,4,24,128]{3,2,1,0:T(8,128)}, f32[24,4,24,128]{3,2,1,0:T(8,128)S(1)}, u32[]{:S(2)}) copy-start(f32[24,4,24,128]{3,2,1,0:T(8,128)S(1)} %collective-permute-done.7.high) | copy-start | bytes 3538948

commit v3 on v2

v3 whole, which is shorter than its diff:
```python
import functools

import jax
import jax.numpy as jnp
from jax import lax
from jax.experimental import pallas as pl
from jax.experimental.pallas import tpu as pltpu
from jax.sharding import PartitionSpec as P

SMOOTH = 4
LEVELS = 24
MEMBERS = 16
LONS = 24
LATS = 128
BLOCKS = 4
SHARE = LONS // BLOCKS
RECORD = 72
STATES = 64
GROUP = 4
GROUPS = LONS // GROUP
SLAB = 8
SLABS = LEVELS // SLAB
PAD = LATS + 16

OFF_CHIP = pl.BlockSpec(memory_space=pltpu.HBM)
ON_CHIP = pl.BlockSpec(memory_space=pltpu.VMEM)
ROOM = pltpu.CompilerParams(vmem_limit_bytes=28 * 2**20)
F32 = jnp.float32


def shape(*dims):
    return jax.ShapeDtypeStruct(dims, F32)


def resident(*dims):
    return pltpu.VMEM(dims, F32)


def row(ref, at):
    return ref[pl.ds(at, 8, stride=0), :]


def slot(lon):
    if lon < GROUP:
        return lon * SHARE
    if lon >= LONS - GROUP:
        return (lon - LONS + GROUP) * SHARE + 1
    return (lon - GROUP) // GROUP * SHARE + 2 + lon % GROUP


def start_all(copies):
    for copy in copies:
        copy.start()
    return copies


def wait_all(copies):
    for copy in copies:
        copy.wait()


def in_order(pieces, target, rows):
    here = lax.axis_index("lev")
    for shift, piece in enumerate(pieces):
        source = lax.rem(here - shift + BLOCKS, BLOCKS)
        target[pl.ds(pl.multiple_of(source * rows, 8), rows), :] = piece[...]


def responses(rates, profiles, scratch):
    tiles = [slice(8 * tile, 8 * tile + 8) for tile in range(LONS // 8)]
    up, down = range(LEVELS), range(LEVELS - 1, -1, -1)

    def sweep(order, source, target):
        state = [None] * len(tiles)
        for level in order:
            for at, lons in enumerate(tiles):
                rate = rates[level, lons, :]
                if source is None:
                    state[at] = rate if state[at] is None else rate * state[at]
                else:
                    value = (1.0 - rate) * source[level, lons, :]
                    state[at] = value if state[at] is None else rate * state[at] + value
                target[level, lons, :] = state[at]
        return state

    through = sweep(up, None, scratch.at[0])
    sweep(down, None, profiles.at[3])
    q21 = sweep(down, scratch.at[0], profiles.at[2])
    q32 = sweep(up, profiles.at[3], scratch.at[1])
    q31 = sweep(up, profiles.at[2], scratch.at[0])
    q42 = sweep(down, scratch.at[1], profiles.at[1])
    q41 = sweep(down, scratch.at[0], profiles.at[0])
    return through, q21, q31, q32, q41, q42


def sweep_kernel(field, rate, diffusivity, local, p0, p1, p2, p3, profiles, to_low, to_high, xs, rates, kappa, exits, scratch, sems):
    here = lax.axis_index("lev")
    small = start_all([pltpu.make_async_copy(rate, rates, sems.at[3]), pltpu.make_async_copy(diffusivity, kappa, sems.at[4])])
    loads = []
    for tile in range(LONS // 8):
        lons = pl.ds(8 * tile, 8)
        loads.append(pltpu.make_async_copy(field.at[:, lons, :], xs.at[:, lons, :], sems.at[tile]))
    start_all(loads)
    wait_all(small)
    coefficients = responses(rates, profiles, scratch)
    for lon in range(LONS):
        for which, tiles in enumerate(coefficients):
            record = slot(lon) * RECORD + STATES + which
            exits[record : record + 1, :] = tiles[lon // 8][lon % 8 : lon % 8 + 1, :]
    profile_rows = profiles.reshape(4 * LEVELS * LONS, LATS)
    height = MEMBERS + 8
    for lon, out in ((0, to_low), (LONS - GROUP, to_high)):
        packed = out.reshape(LEVELS * GROUP * height, LATS)
        packed[pl.ds(MEMBERS + 4, GROUP, stride=height), :] = kappa[lon : lon + GROUP, :]
        for level in range(LEVELS):
            for n in range(4):
                start = (n * LEVELS + level) * LONS + lon
                packed[pl.ds(level * GROUP * height + MEMBERS + n, GROUP, stride=height), :] = profile_rows[pl.ds(start, GROUP), :]
    values = xs.reshape(LEVELS * MEMBERS * LONS, LATS)
    weights = rates.reshape(LEVELS * LONS, LATS)

    def run(group, carry):
        lon = GROUP * group
        for number in range(4):
            order = range(LEVELS) if number % 2 == 0 else range(LEVELS - 1, -1, -1)
            state = {}
            for level in order:
                for j in range(GROUP):
                    weight = row(weights, level * LONS + lon + j)
                    rest = 1.0 - weight
                    for half in range(2):
                        if number == 0:
                            start = (level * MEMBERS + 8 * half) * LONS + lon + j
                            value = values[pl.ds(start, 8, stride=LONS), :]
                        else:
                            value = local[level, lon + j, 8 * half : 8 * half + 8, :]
                        value = rest * value
                        if (j, half) in state:
                            value = weight * state[j, half] + value
                        state[j, half] = value
                        local[level, lon + j, 8 * half : 8 * half + 8, :] = value
            for (j, half), value in state.items():
                edge = jnp.where(group == 0, j * SHARE, j * SHARE + 1)
                inner = (group - 1) * SHARE + 2 + j
                place = jnp.where((group == 0) | (group == GROUPS - 1), edge, inner)
                exits[pl.ds(pl.multiple_of(place * RECORD + 16 * number + 8 * half, 8), 8), :] = value
        return carry

    for tile in range(LONS // 8):
        loads[tile].wait()
        lax.fori_loop(2 * tile, 2 * tile + 2, run, 0)
    for shift, piece in enumerate((p0, p1, p2, p3)):
        target = lax.rem(here + shift, BLOCKS)
        piece[...] = exits[pl.ds(pl.multiple_of(target * (SHARE * RECORD), 8), SHARE * RECORD), :]
    for lon, out in ((0, to_low), (LONS - GROUP, to_high)):
        for j in range(GROUP):
            out[:, j, 0:MEMBERS, :] = local[:, lon + j]


def sweep_call(field, rate, diffusivity):
    halo = resident(LEVELS, GROUP, MEMBERS + 8, LATS)
    outs = [resident(LEVELS, LONS, MEMBERS, LATS)] + [resident(SHARE * RECORD, LATS)] * BLOCKS
    outs += [resident(4, LEVELS, LONS, LATS), halo, halo]
    return pl.pallas_call(
        sweep_kernel,
        out_shape=outs,
        in_specs=[OFF_CHIP] * 3,
        out_specs=[ON_CHIP] * len(outs),
        scratch_shapes=[
            pltpu.VMEM((LEVELS * MEMBERS, LONS, LATS), F32),
            pltpu.VMEM((LEVELS, LONS, LATS), F32),
            pltpu.VMEM((LONS, LATS), F32),
            pltpu.VMEM((LONS * RECORD, LATS), F32),
            pltpu.VMEM((2, LEVELS, LONS, LATS), F32),
            pltpu.SemaphoreType.DMA((5,)),
        ],
        compiler_params=ROOM,
        name="sweeps",
    )(*(pltpu.with_memory_space_constraint(x, pltpu.HBM) for x in (field, rate, diffusivity)))


def solve_kernel(*refs):
    pieces, outs, (records, states) = refs[:4], refs[4:8], refs[8:]
    here = lax.axis_index("lev")
    in_order(pieces, records, SHARE * RECORD)

    def run(lon, carry):
        def exit_of(block, number, half):
            at = (block * SHARE + lon) * RECORD + 16 * number + 8 * half
            return records[pl.ds(pl.multiple_of(at, 8), 8), :]

        def response(block, which):
            return row(records, (block * SHARE + lon) * RECORD + STATES + which)

        for half in range(2):
            zero = jnp.zeros((8, LATS), F32)
            f1, b1, f2, b2 = ([zero] * BLOCKS for _ in range(4))
            for d in range(BLOCKS - 1):
                f1[d + 1] = exit_of(d, 0, half) + response(d, 0) * f1[d]
            for d in range(BLOCKS - 1, 0, -1):
                b1[d - 1] = exit_of(d, 1, half) + response(d, 1) * f1[d] + response(d, 0) * b1[d]
            for d in range(BLOCKS - 1):
                f2[d + 1] = (
                    exit_of(d, 2, half)
                    + response(d, 2) * f1[d]
                    + response(d, 3) * b1[d]
                    + response(d, 0) * f2[d]
                )
            for d in range(BLOCKS - 1, 0, -1):
                b2[d - 1] = (
                    exit_of(d, 3, half)
                    + response(d, 4) * f1[d]
                    + response(d, 5) * b1[d]
                    + response(d, 1) * f2[d]
                    + response(d, 0) * b2[d]
                )
            for d in range(BLOCKS):
                for number, entering in enumerate((f1, b1, f2, b2)):
                    at = (d * SHARE + lon) * STATES + 16 * number + 8 * half
                    states[pl.ds(pl.multiple_of(at, 8), 8), :] = entering[d]
        return carry

    lax.fori_loop(0, SHARE, run, 0)
    for shift, out in enumerate(outs):
        target = lax.rem(here + shift, BLOCKS)
        out[...] = states[pl.ds(pl.multiple_of(target * (SHARE * STATES), 8), SHARE * STATES), :]


def solve_call(pieces):
    return pl.pallas_call(
        solve_kernel,
        out_shape=[resident(SHARE * STATES, LATS)] * BLOCKS,
        in_specs=[ON_CHIP] * BLOCKS,
        out_specs=[ON_CHIP] * BLOCKS,
        scratch_shapes=[
            pltpu.VMEM((BLOCKS * SHARE * RECORD, LATS), F32),
            pltpu.VMEM((BLOCKS * SHARE * STATES, LATS), F32),
        ],
        compiler_params=ROOM,
        name="solve",
    )(*pieces)


def corrected_block(value_of, profile_of, entering):
    parts = []
    for level in range(SLAB):
        mine = [profile_of(n, level) for n in range(4)]
        for half in range(2):
            value = value_of(level, half)
            for n in range(4):
                value = value + mine[n] * entering[half][n]
            parts.append(value)
    return jnp.concatenate(parts, axis=0)


def entering_of(states, start):
    return [[states[start + 16 * n + 8 * half : start + 16 * n + 8 * half + 8, :] for n in range(4)] for half in range(2)]


def spread(kappa_row):
    return jnp.transpose(jnp.broadcast_to(kappa_row, (LATS, LATS)))


def stepped(here, around, k):
    return here + k * (around - 4.0 * here)


def clear_pads(rows, blocks):
    zero = jnp.zeros((8, LATS), F32)
    for block in range(blocks):
        rows[block * PAD : block * PAD + 8, :] = zero
        rows[block * PAD + LATS + 8 : (block + 1) * PAD, :] = zero


def inner_kernel(local, profiles, kappa, s0, s1, s2, s3, out, begun, kept, spread_rows, states, buffers, made, sems):
    def save(slab):
        part = pl.ds(slab * SLAB * MEMBERS, SLAB * MEMBERS)
        return pltpu.make_async_copy(made.at[part], out.at[part, pl.ds(8, 8), :], sems.at[slab])

    in_order((s0, s1, s2, s3), states, SHARE * STATES)
    rows = buffers.reshape(2 * LONS * PAD, LATS)
    kept_rows = kept.reshape(SLABS * 2 * 2 * SMOOTH * PAD, LATS)
    clear_pads(rows, 2 * LONS)
    clear_pads(kept_rows, SLABS * 2 * 2 * SMOOTH)
    for lon in range(LONS):
        spread_rows[lon] = spread(kappa[lon : lon + 1, :])
    profile_rows = profiles.reshape(4 * LEVELS * LONS, LATS)
    made_rows = made.reshape(LEVELS * MEMBERS * 8, LATS)
    begun_rows = begun.reshape(2 * LEVELS * MEMBERS * 8, LATS)

    def run(slab, carry):
        def keep(step, lon):
            for side, m in enumerate((lon, LONS - 1 - lon)):
                if step <= m < step + 2 and step < SMOOTH:
                    return ((slab * 2 + side) * 2 * SMOOTH + 2 * step + m - step) * PAD + 8
            return None

        for lon in range(LONS):
            block = jnp.transpose(
                corrected_block(
                    lambda level, half: local[slab * SLAB + level, lon, 8 * half : 8 * half + 8, :],
                    lambda n, level: row(profile_rows, (n * LEVELS + slab * SLAB + level) * LONS + lon),
                    entering_of(states, slot(lon) * STATES),
                )
            )
            buffers[0, lon, 8 : 8 + LATS, :] = block
            start = keep(0, lon)
            if start is not None:
                kept_rows[pl.ds(pl.multiple_of(start, 8), LATS), :] = block
        for step in range(SMOOTH):

            def at(which, lon, offset):
                return (which * LONS + lon) * PAD + 8 + offset

            def tile(t, carry):
                source, target = step % 2, (step + 1) % 2
                top = pl.multiple_of(8 * t, 8)
                west = rows[pl.ds(at(source, step, top), 8), :]
                here = rows[pl.ds(at(source, step + 1, top), 8), :]
                for lon in range(step + 1, LONS - step - 1):
                    east = rows[pl.ds(at(source, lon + 1, top), 8), :]
                    north = rows[pl.ds(at(source, lon, top - 1), 8), :]
                    south = rows[pl.ds(at(source, lon, top + 1), 8), :]
                    k = spread_rows[lon, pl.ds(top, 8), :]
                    value = stepped(here, (east + west) + (north + south), k)
                    rows[pl.ds(at(target, lon, top), 8), :] = value
                    start = keep(step + 1, lon)
                    if start is not None:
                        kept_rows[pl.ds(pl.multiple_of(start + top, 8), 8), :] = value
                    west, here = here, east
                return carry

            lax.fori_loop(0, LATS // 8, tile, 0, unroll=2)
        for lon in range(GROUP, LONS - GROUP):
            block = jnp.transpose(buffers[0, lon, 8 : 8 + LATS, :])
            for part in range(2 * SLAB):
                first = slab * SLAB * MEMBERS + 8 * part
                piece = block[8 * part : 8 * part + 8, :]
                if 8 <= lon < 16:
                    made_rows[pl.ds(first * 8 + lon - 8, 8, stride=8), :] = piece
                else:
                    side = lon // 16
                    begun_rows[pl.ds((side * LEVELS * MEMBERS + first) * 8 + lon - 16 * side, 8, stride=8), :] = piece
        save(slab).start()
        return carry

    lax.fori_loop(0, SLABS, run, 0)
    wait_all([save(slab) for slab in range(SLABS)])


def inner_call(local, profiles, diffusivity, pieces):
    return pl.pallas_call(
        inner_kernel,
        out_shape=[
            shape(LEVELS * MEMBERS, LONS, LATS),
            resident(2, LEVELS * MEMBERS, 8, LATS),
            resident(SLABS, 2, 2 * SMOOTH, PAD, LATS),
            resident(LONS, LATS, LATS),
        ],
        in_specs=[ON_CHIP] * 7,
        out_specs=[OFF_CHIP, ON_CHIP, ON_CHIP, ON_CHIP],
        scratch_shapes=[
            pltpu.VMEM((LONS * STATES, LATS), F32),
            pltpu.VMEM((2, LONS, PAD, LATS), F32),
            pltpu.VMEM((LEVELS * MEMBERS, 8, LATS), F32),
            pltpu.SemaphoreType.DMA((SLABS,)),
        ],
        compiler_params=ROOM,
        cost_estimate=pl.CostEstimate(flops=10**8, transcendentals=0, bytes_accessed=10**7),
        name="inner",
    )(local, profiles, diffusivity, *pieces)


def outer_kernel(whole, begun, kept, spread_rows, low, high, low_s, high_s, out, filled, buffers, halo_spread, sems):
    here = lax.axis_index("lev")
    places = 2 * SMOOTH

    def saves(slab):
        part = pl.ds(slab * SLAB * MEMBERS, SLAB * MEMBERS)
        return [
            pltpu.make_async_copy(filled.at[side, part], out.at[part, pl.ds(lon, 8), :], sems.at[slab, side])
            for side, lon in enumerate((0, 16))
        ]

    rows = buffers.reshape(2 * 2 * places * PAD, LATS)
    kept_rows = kept.reshape(SLABS * 2 * 2 * SMOOTH * PAD, LATS)
    clear_pads(rows, 2 * 2 * places)
    height = MEMBERS + 8
    halos = [(low, low_s), (high, high_s)]
    for side, (halo, _) in enumerate(halos):
        for j in range(GROUP):
            place = j if side == 0 else GROUP - 1 - j
            halo_spread[side, place] = spread(halo[0, j, MEMBERS + 4 : MEMBERS + 5, :])
    filled_rows = filled.reshape(2 * LEVELS * MEMBERS * 8, LATS)

    def run(slab, carry):
        for side, (halo, halo_states) in enumerate(halos):
            halo_rows = halo.reshape(LEVELS * GROUP * height, LATS)
            for j in range(GROUP):
                place = j if side == 0 else GROUP - 1 - j
                start = lax.rem(here - j + BLOCKS, BLOCKS) * STATES
                entering = [
                    [halo_states[pl.ds(pl.multiple_of(start + 16 * n + 8 * half, 8), 8), :] for n in range(4)] for half in range(2)
                ]
                block = corrected_block(
                    lambda level, half: halo[slab * SLAB + level, j, 8 * half : 8 * half + 8, :],
                    lambda n, level: row(halo_rows, ((slab * SLAB + level) * GROUP + j) * height + MEMBERS + n),
                    entering,
                )
                buffers[0, side, place, 8 : 8 + LATS, :] = jnp.transpose(block)
        for step in range(SMOOTH):

            def tile(t, carry):
                top = pl.multiple_of(8 * t, 8)
                for side in range(2):

                    def value_at(place, offset):
                        if place < step + SMOOTH:
                            start = ((step % 2 * 2 + side) * places + place) * PAD
                            return rows[pl.ds(start + 8 + top + offset, 8), :]
                        start = ((slab * 2 + side) * 2 * SMOOTH + 2 * step + place - step - SMOOTH) * PAD
                        return kept_rows[pl.ds(start + 8 + top + offset, 8), :]

                    west, here = value_at(step, 0), value_at(step + 1, 0)
                    for place in range(step + 1, step + SMOOTH + 1):
                        east = value_at(place + 1, 0)
                        around = (east + west) + (value_at(place, -1) + value_at(place, 1))
                        if place < GROUP:
                            k = halo_spread[side, place, pl.ds(top, 8), :]
                        else:
                            m = place - GROUP
                            k = spread_rows[m if side == 0 else LONS - 1 - m, pl.ds(top, 8), :]
                        start = (((step + 1) % 2 * 2 + side) * places + place) * PAD
                        rows[pl.ds(pl.multiple_of(start + 8 + top, 8), 8), :] = stepped(here, around, k)
                        west, here = here, east
                return carry

            lax.fori_loop(0, LATS // 8, tile, 0, unroll=2)
        for side in range(2):
            for m in range(GROUP):
                block = jnp.transpose(buffers[0, side, GROUP + m, 8 : 8 + LATS, :])
                for part in range(2 * SLAB):
                    first = (side * LEVELS + slab * SLAB) * MEMBERS + 8 * part
                    lon = m if side == 0 else 7 - m
                    filled_rows[pl.ds(first * 8 + lon, 8, stride=8), :] = block[8 * part : 8 * part + 8, :]
        start_all(saves(slab))
        return carry

    lax.fori_loop(0, SLABS, run, 0)
    for slab in range(SLABS):
        wait_all(saves(slab))


def outer_call(whole, begun, kept, spread_rows, low, high, low_s, high_s):
    return pl.pallas_call(
        outer_kernel,
        out_shape=[shape(LEVELS * MEMBERS, LONS, LATS), resident(2, LEVELS * MEMBERS, 8, LATS)],
        in_specs=[OFF_CHIP] + [ON_CHIP] * 7,
        out_specs=[OFF_CHIP, ON_CHIP],
        input_output_aliases={0: 0, 1: 1},
        scratch_shapes=[
            pltpu.VMEM((2, 2, 2 * SMOOTH, PAD, LATS), F32),
            pltpu.VMEM((2, GROUP, LATS, LATS), F32),
            pltpu.SemaphoreType.DMA((SLABS, 2)),
        ],
        compiler_params=ROOM,
        name="outer",
    )(whole, begun, kept, spread_rows, low, high, low_s, high_s)


def shifted(pieces):
    moved = [pieces[0]]
    for shift in (1, 2, 3):
        moved.append(lax.ppermute(pieces[shift], "lev", [(i, (i + shift) % BLOCKS) for i in range(BLOCKS)]))
    return moved


def exchanged(to_low, to_high):
    count = lax.axis_size("col")
    forward = [(i, i + 1) for i in range(count - 1)]
    backward = [(b, a) for a, b in forward]
    return lax.ppermute(to_high, "col", forward), lax.ppermute(to_low, "col", backward)


def per_device(control_field, decay_rate, diffusivity):
    field = control_field.reshape(LEVELS * MEMBERS, LONS, LATS)
    local, *pieces, profiles, to_low, to_high = sweep_call(field, decay_rate, diffusivity)
    pieces = shifted(pieces)
    low, high = exchanged(to_low, to_high)
    states = shifted(solve_call(pieces))
    low_s, high_s = exchanged(
        jnp.concatenate([piece[:STATES] for piece in states]),
        jnp.concatenate([piece[STATES : 2 * STATES] for piece in states]),
    )
    whole, begun, kept, spread_rows = inner_call(local, profiles, diffusivity, states)
    out, _ = outer_call(whole, begun, kept, spread_rows, low, high, low_s, high_s)
    return out.reshape(control_field.shape)


def solution(mesh):
    in_specs = (P("lev", None, "col", None), P("lev", "col", None), P("col", None))
    out_specs = P("lev", None, "col", None)
    return jax.shard_map(
        per_device, mesh=mesh, in_specs=in_specs, out_specs=out_specs, check_vma=False
    )
```

time: 70.5 us -> 54.2 us (0.77)
  Pallas kernels: 31.9 us -> 19.1 us
  local copies, waits for them, and re-layouts: 3.7 us -> 0.03 us
    pallas_call x4, Pallas kernels: 31.9 us -> 19.1 us  [the longest x1 9.29 us: inner_call(): pl.pallas_call(inner_kernel, out_shape=[shape(LEVELS * MEMBERS, LONS, LAT...]
    unnamed x20 -> x2, local copies, waits for them, and re-layouts: 2.91 us -> 0.01 us
    slice x4, local copies, waits for them, and re-layouts: 0.8 us -> 0.02 us  [per_device(): piece[:STATES]]
  transfers between devices with their start and end apart: 10 -> 10, of which waited for: 3 -> 3; matrix products, arithmetic and copies ran while one was open for 1% -> 0% of each run, Pallas kernels for 20% -> 18%
where the time goes in v3:
time: 54.2 us; the launch traced here: 54 us
  starting transfers between devices  26.5 us (49%)
  Pallas kernels  19.1 us (35%)
  waiting for transfers between devices  8.28 us (15%)
    ppermute x2, starting transfers between devices, exchanged(): lax.ppermute(to_low, 'col', backward)  11.5 us
    ppermute x6, starting transfers between devices, shifted(): lax.ppermute(pieces[shift], 'lev', [(i, (i + shift) % BLOCKS) for i in ra...  11.2 us
    pallas_call x1, Pallas kernels, inner_call(): pl.pallas_call(inner_kernel, out_shape=[shape(LEVELS * MEMBERS, LONS, LAT...  9.29 us
    ppermute x6, waiting for transfers between devices, shifted(): lax.ppermute(pieces[shift], 'lev', [(i, (i + shift) % BLOCKS) for i in ra...  8.27 us
    pallas_call x1, Pallas kernels, outer_call(): pl.pallas_call(outer_kernel, out_shape=[shape(LEVELS * MEMBERS, LONS, LAT...  5.13 us
    pallas_call x1, Pallas kernels, sweep_call(): pl.pallas_call(sweep_kernel, out_shape=outs, in_specs=[OFF_CHIP] * 3, out...  4.34 us
    ppermute x2, starting transfers between devices, exchanged(): lax.ppermute(to_high, 'col', forward)  3.83 us
  transfers between devices with their start and end apart: 10, of which 3 were waited for; matrix products, arithmetic and copies ran while one was open for 0% of the time, Pallas kernels for 18%

profile of v3, /device:TPU:64, one launch (start us, length us, event | category | flops | bytes accessed | tf_op | source)
XLA Modules:
  0.0 54.0 jit_solution(13509267194499546254)
XLA Ops:
  0.0 0.0 copy-start
  0.0 4.3 %sweeps.1 = (f32[24,24,16,128]{3,2,1,0:T(8,128)S(1)}, f32[432,128]{1,0:T(8,128)S(1)}, f32[432,128]{1,0:T(8,128)S(1)}, f32[432,128]{1,0:T(8,128)S(1)}, f32[432,12...) custom-call(f32[384,24,128]{2,1,0:T(8,128)} %bitcast.2, ...), custom_call_target="tpu_custom_call" | custom-call | tf_op jit(solution)/shard_map/sweeps/pallas_call | solution.py:164
  4.3 1.6 %collective-permute-start = (f32[432,128]{1,0:T(8,128)S(1)}, f32[432,128]{1,0:T(8,128)S(1)}, u32[]{:S(2)}, u32[]{:S(2)}) collective-permute-start(f32[432,128]{1,0:T(8,128)S(1)} %get-tuple-element.25), channel_id=1, source_target_pairs={{0,32},{32,64},{64,96},{96,0},{1,33},{33,65},{65,97},{97,1},{2,34}... | collective-permute-start | bytes 663560 | tf_op jit(solution)/shard_map/ppermute | solution.py:474
  6.0 2.9 %collective-permute-start.1 = (f32[432,128]{1,0:T(8,128)S(1)}, f32[432,128]{1,0:T(8,128)S(1)}, u32[]{:S(2)}, u32[]{:S(2)}) collective-permute-start(f32[432,128]{1,0:T(8,128)S(1)} %get-tuple-element.26), channel_id=1, source_target_pairs={{0,64},{32,96},{64,0},{96,32},{1,65},{33,97},{65,1},{97,33},{2,66}... | collective-permute-start | bytes 663560 | tf_op jit(solution)/shard_map/ppermute | solution.py:474
  8.9 1.3 %collective-permute-start.2 = (f32[432,128]{1,0:T(8,128)S(1)}, f32[432,128]{1,0:T(8,128)S(1)}, u32[]{:S(2)}, u32[]{:S(2)}) collective-permute-start(f32[432,128]{1,0:T(8,128)S(1)} %get-tuple-element.27), channel_id=1, source_target_pairs={{0,96},{32,0},{64,32},{96,64},{1,97},{33,1},{65,33},{97,65},{2,98}... | collective-permute-start | bytes 663560 | tf_op jit(solution)/shard_map/ppermute | solution.py:474
  10.2 1.9 %collective-permute-start.6 = (f32[24,4,24,128]{3,2,1,0:T(8,128)S(1)}, f32[24,4,24,128]{3,2,1,0:T(8,128)S(1)}, u32[]{:S(2)}, u32[]{:S(2)}) collective-permute-start(f32[24,4,24,128]{3,2,1,0:T(8,128)S(1)} %get-tuple-element.36), channel_id=1, source_target_pairs={{0,1},{1,2},{2,3},{3,4},{4,5},{5,6},{6,7},{7,8},{8,9},{9,10},{10,1... | collective-permute-start | bytes 3538952 | tf_op jit(solution)/shard_map/ppermute | solution.py:482
  12.2 5.8 %collective-permute-start.7 = (f32[24,4,24,128]{3,2,1,0:T(8,128)S(1)}, f32[24,4,24,128]{3,2,1,0:T(8,128)S(1)}, u32[]{:S(2)}, u32[]{:S(2)}) collective-permute-start(f32[24,4,24,128]{3,2,1,0:T(8,128)S(1)} %get-tuple-element.37), channel_id=1, source_target_pairs={{1,0},{2,1},{3,2},{4,3},{5,4},{6,5},{7,6},{8,7},{9,8},{10,9},{11,1... | collective-permute-start | bytes 3538952 | tf_op jit(solution)/shard_map/ppermute | solution.py:482
  17.9 0.0 collective-permute-done.refs_1_
  17.9 0.8 %collective-permute-done.1.refs_2_ = f32[432,128]{1,0:T(8,128)S(1)} collective-permute-done((f32[432,128]{1,0:T(8,128)S(1)}, f32[432,128]{1,0:T(8,128)S(1)}, u32[]{:S(2)}, u32[]{:S(2)}) %collective-permute-start.1) | collective-permute-done | bytes 221216 | tf_op jit(solution)/shard_map/ppermute | solution.py:474
  18.8 0.0 collective-permute-done.2.refs_3_
  18.8 0.3 solve.1
  19.1 1.3 %collective-permute-start.3 = (f32[384,128]{1,0:T(8,128)S(1)}, f32[384,128]{1,0:T(8,128)S(1)}, u32[]{:S(2)}, u32[]{:S(2)}) collective-permute-start(f32[384,128]{1,0:T(8,128)S(1)} %get-tuple-element.29), channel_id=1, source_target_pairs={{0,32},{32,64},{64,96},{96,0},{1,33},{33,65},{65,97},{97,1},{2,34}... | collective-permute-start | bytes 589832 | tf_op jit(solution)/shard_map/ppermute | solution.py:474
  20.4 2.4 %collective-permute-start.4 = (f32[384,128]{1,0:T(8,128)S(1)}, f32[384,128]{1,0:T(8,128)S(1)}, u32[]{:S(2)}, u32[]{:S(2)}) collective-permute-start(f32[384,128]{1,0:T(8,128)S(1)} %get-tuple-element.30), channel_id=1, source_target_pairs={{0,64},{32,96},{64,0},{96,32},{1,65},{33,97},{65,1},{97,33},{2,66}... | collective-permute-start | bytes 589832 | tf_op jit(solution)/shard_map/ppermute | solution.py:474
  22.8 1.6 %collective-permute-start.5 = (f32[384,128]{1,0:T(8,128)S(1)}, f32[384,128]{1,0:T(8,128)S(1)}, u32[]{:S(2)}, u32[]{:S(2)}) collective-permute-start(f32[384,128]{1,0:T(8,128)S(1)} %get-tuple-element.31), channel_id=1, source_target_pairs={{0,96},{32,0},{64,32},{96,64},{1,97},{33,1},{65,33},{97,65},{2,98}... | collective-permute-start | bytes 589832 | tf_op jit(solution)/shard_map/ppermute | solution.py:474
  24.4 2.0 %collective-permute-done.3.s1 = f32[384,128]{1,0:T(8,128)S(1)} collective-permute-done((f32[384,128]{1,0:T(8,128)S(1)}, f32[384,128]{1,0:T(8,128)S(1)}, u32[]{:S(2)}, u32[]{:S(2)}) %collective-permute-start.3) | collective-permute-done | bytes 196640 | tf_op jit(solution)/shard_map/ppermute | solution.py:474
  26.4 5.4 %collective-permute-done.4.s2 = f32[384,128]{1,0:T(8,128)S(1)} collective-permute-done((f32[384,128]{1,0:T(8,128)S(1)}, f32[384,128]{1,0:T(8,128)S(1)}, u32[]{:S(2)}, u32[]{:S(2)}) %collective-permute-start.4) | collective-permute-done | bytes 196640 | tf_op jit(solution)/shard_map/ppermute | solution.py:474
  31.8 0.0 collective-permute-done.5.s3
  31.9 1.9 %collective-permute-start.8 = (f32[256,128]{1,0:T(8,128)S(1)}, f32[256,128]{1,0:T(8,128)S(1)}, u32[]{:S(2)}, u32[]{:S(2)}) collective-permute-start(f32[256,128]{1,0:T(8,128)S(1)} %pad_maximum_fusion), channel_id=1, source_target_pairs={{0,1},{1,2},{2,3},{3,4},{4,5},{5,6},{6,7},{7,8},{8,9},{9,10},{10,1... | collective-permute-start | bytes 393224 | tf_op jit(solution)/shard_map/ppermute | solution.py:482
  33.8 5.8 %collective-permute-start.9 = (f32[256,128]{1,0:T(8,128)S(1)}, f32[256,128]{1,0:T(8,128)S(1)}, u32[]{:S(2)}, u32[]{:S(2)}) collective-permute-start(f32[256,128]{1,0:T(8,128)S(1)} %pad_maximum_fusion.1), channel_id=1, source_target_pairs={{1,0},{2,1},{3,2},{4,3},{5,4},{6,5},{7,6},{8,7},{9,8},{10,9},{11,1... | collective-permute-start | bytes 393224 | tf_op jit(solution)/shard_map/ppermute | solution.py:482
  39.6 0.0 copy-done
  39.6 9.3 %inner.1 = (f32[384,24,128]{2,1,0:T(8,128)}, f32[2,384,8,128]{3,2,1,0:T(8,128)S(1)}, f32[3,2,8,144,128]{4,3,2,1,0:T(8,128)S(1)}, f32[24,128,128]{2,1,0:T(8,128)S(1)}) custom-call(f32[24,24,16,128]{3,2,1,0:T(8,128)S(1)} %get-tuple-element.22.local, f32[4,24,24,128]{3,2,1,0:T(8,128)S(1)} %get-tuple-element.23.profiles, f32[24,128]{1,0:T(8,128)S(1)} %copy-done, ...), custom_call_target="tpu_custom_call" | custom-call | flops 100000000 | bytes 10000000 | tf_op jit(solution)/shard_map/inner/pallas_call | solution.py:352
  48.9 0.0 collective-permute-done.8.low_s
  48.9 0.0 collective-permute-done.9.high_s
  48.9 0.0 collective-permute-done.6.low
  48.9 0.0 collective-permute-done.7.high
  48.9 5.1 %outer.1 = (f32[384,24,128]{2,1,0:T(8,128)}, f32[2,384,8,128]{3,2,1,0:T(8,128)S(1)}) custom-call(f32[384,24,128]{2,1,0:T(8,128)} %get-tuple-element.32.whole, f32[2,384,8,128]{3,2,1,0:T(8,128)S(1)} %get-tuple-element.33.begun, f32[3,2,8,144,128]{4,3,2,1,0:T(8,128)S(1)} %get-tuple-element.34.kept, ...), custom_call_target="tpu_custom_call", output_to_operand_aliasing={{0}: (0, {}), {1}: (1, {})} | custom-call | tf_op jit(solution)/shard_map/outer/pallas_call | solution.py:455
  (6 shorter events, 0.0 us)
Async XLA Ops:
  0.0 39.6 %copy-start = (f32[24,128]{1,0:T(8,128)S(1)}, f32[24,128]{1,0:T(8,128)}, u32[]{:S(2)}) copy-start(f32[24,128]{1,0:T(8,128)} %kappa.1) | copy-start | bytes 36868
  4.3 13.6 %collective-permute-start = (f32[432,128]{1,0:T(8,128)S(1)}, f32[432,128]{1,0:T(8,128)S(1)}, u32[]{:S(2)}, u32[]{:S(2)}) collective-permute-start(f32[432,128]{1,0:T(8,128)S(1)} %get-tuple-element.25), channel_id=1, source_target_pairs={{0,32},{32,64},{64,96},{96,0},{1,33},{33,65},{65,97},{97,1},{2,34}... | collective-permute-start | bytes 663560 | tf_op jit(solution)/shard_map/ppermute | solution.py:474
  6.0 12.8 %collective-permute-start.1 = (f32[432,128]{1,0:T(8,128)S(1)}, f32[432,128]{1,0:T(8,128)S(1)}, u32[]{:S(2)}, u32[]{:S(2)}) collective-permute-start(f32[432,128]{1,0:T(8,128)S(1)} %get-tuple-element.26), channel_id=1, source_target_pairs={{0,64},{32,96},{64,0},{96,32},{1,65},{33,97},{65,1},{97,33},{2,66}... | collective-permute-start | bytes 663560 | tf_op jit(solution)/shard_map/ppermute | solution.py:474
  8.9 9.9 %collective-permute-start.2 = (f32[432,128]{1,0:T(8,128)S(1)}, f32[432,128]{1,0:T(8,128)S(1)}, u32[]{:S(2)}, u32[]{:S(2)}) collective-permute-start(f32[432,128]{1,0:T(8,128)S(1)} %get-tuple-element.27), channel_id=1, source_target_pairs={{0,96},{32,0},{64,32},{96,64},{1,97},{33,1},{65,33},{97,65},{2,98}... | collective-permute-start | bytes 663560 | tf_op jit(solution)/shard_map/ppermute | solution.py:474
  10.2 38.6 %collective-permute-start.6 = (f32[24,4,24,128]{3,2,1,0:T(8,128)S(1)}, f32[24,4,24,128]{3,2,1,0:T(8,128)S(1)}, u32[]{:S(2)}, u32[]{:S(2)}) collective-permute-start(f32[24,4,24,128]{3,2,1,0:T(8,128)S(1)} %get-tuple-element.36), channel_id=1, source_target_pairs={{0,1},{1,2},{2,3},{3,4},{4,5},{5,6},{6,7},{7,8},{8,9},{9,10},{10,1... | collective-permute-start | bytes 3538952 | tf_op jit(solution)/shard_map/ppermute | solution.py:482
  12.2 36.7 %collective-permute-start.7 = (f32[24,4,24,128]{3,2,1,0:T(8,128)S(1)}, f32[24,4,24,128]{3,2,1,0:T(8,128)S(1)}, u32[]{:S(2)}, u32[]{:S(2)}) collective-permute-start(f32[24,4,24,128]{3,2,1,0:T(8,128)S(1)} %get-tuple-element.37), channel_id=1, source_target_pairs={{1,0},{2,1},{3,2},{4,3},{5,4},{6,5},{7,6},{8,7},{9,8},{10,9},{11,1... | collective-permute-start | bytes 3538952 | tf_op jit(solution)/shard_map/ppermute | solution.py:482
  19.1 7.3 %collective-permute-start.3 = (f32[384,128]{1,0:T(8,128)S(1)}, f32[384,128]{1,0:T(8,128)S(1)}, u32[]{:S(2)}, u32[]{:S(2)}) collective-permute-start(f32[384,128]{1,0:T(8,128)S(1)} %get-tuple-element.29), channel_id=1, source_target_pairs={{0,32},{32,64},{64,96},{96,0},{1,33},{33,65},{65,97},{97,1},{2,34}... | collective-permute-start | bytes 589832 | tf_op jit(solution)/shard_map/ppermute | solution.py:474
  20.4 11.4 %collective-permute-start.4 = (f32[384,128]{1,0:T(8,128)S(1)}, f32[384,128]{1,0:T(8,128)S(1)}, u32[]{:S(2)}, u32[]{:S(2)}) collective-permute-start(f32[384,128]{1,0:T(8,128)S(1)} %get-tuple-element.30), channel_id=1, source_target_pairs={{0,64},{32,96},{64,0},{96,32},{1,65},{33,97},{65,1},{97,33},{2,66}... | collective-permute-start | bytes 589832 | tf_op jit(solution)/shard_map/ppermute | solution.py:474
  22.8 9.0 %collective-permute-start.5 = (f32[384,128]{1,0:T(8,128)S(1)}, f32[384,128]{1,0:T(8,128)S(1)}, u32[]{:S(2)}, u32[]{:S(2)}) collective-permute-start(f32[384,128]{1,0:T(8,128)S(1)} %get-tuple-element.31), channel_id=1, source_target_pairs={{0,96},{32,0},{64,32},{96,64},{1,97},{33,1},{65,33},{97,65},{2,98}... | collective-permute-start | bytes 589832 | tf_op jit(solution)/shard_map/ppermute | solution.py:474
  31.9 17.0 %collective-permute-start.8 = (f32[256,128]{1,0:T(8,128)S(1)}, f32[256,128]{1,0:T(8,128)S(1)}, u32[]{:S(2)}, u32[]{:S(2)}) collective-permute-start(f32[256,128]{1,0:T(8,128)S(1)} %pad_maximum_fusion), channel_id=1, source_target_pairs={{0,1},{1,2},{2,3},{3,4},{4,5},{5,6},{6,7},{7,8},{8,9},{9,10},{10,1... | collective-permute-start | bytes 393224 | tf_op jit(solution)/shard_map/ppermute | solution.py:482
  33.8 15.1 %collective-permute-start.9 = (f32[256,128]{1,0:T(8,128)S(1)}, f32[256,128]{1,0:T(8,128)S(1)}, u32[]{:S(2)}, u32[]{:S(2)}) collective-permute-start(f32[256,128]{1,0:T(8,128)S(1)} %pad_maximum_fusion.1), channel_id=1, source_target_pairs={{1,0},{2,1},{3,2},{4,3},{5,4},{6,5},{7,6},{8,7},{9,8},{10,9},{11,1... | collective-permute-start | bytes 393224 | tf_op jit(solution)/shard_map/ppermute | solution.py:482

commit v4 on v3

--- a/solution.py
+++ b/solution.py
@@ -7,20 +7,22 @@
 from jax.experimental.pallas import tpu as pltpu
 from jax.sharding import PartitionSpec as P
 
+
 SMOOTH = 4
 LEVELS = 24
 MEMBERS = 16
 LONS = 24
 LATS = 128
 BLOCKS = 4
-SHARE = LONS // BLOCKS
 RECORD = 72
 STATES = 64
 GROUP = 4
-GROUPS = LONS // GROUP
+EDGE = (0, 5)
+INNER = (1, 2, 3, 4)
 SLAB = 8
 SLABS = LEVELS // SLAB
 PAD = LATS + 16
+HALO = GROUP * SLABS * LATS
 
 OFF_CHIP = pl.BlockSpec(memory_space=pltpu.HBM)
 ON_CHIP = pl.BlockSpec(memory_space=pltpu.VMEM)
@@ -28,6 +30,10 @@
 F32 = jnp.float32
 
 
+def cost(flops):
+    return pl.CostEstimate(flops=flops, transcendentals=0, bytes_accessed=10**6)
+
+
 def shape(*dims):
     return jax.ShapeDtypeStruct(dims, F32)
 
@@ -40,12 +46,8 @@
     return ref[pl.ds(at, 8, stride=0), :]
 
 
-def slot(lon):
-    if lon < GROUP:
-        return lon * SHARE
-    if lon >= LONS - GROUP:
-        return (lon - LONS + GROUP) * SHARE + 1
-    return (lon - GROUP) // GROUP * SHARE + 2 + lon % GROUP
+def slot(groups, index, j):
+    return 2 * j + index if groups == EDGE else GROUP * index + j
 
 
 def start_all(copies):
@@ -93,34 +95,12 @@
     return through, q21, q31, q32, q41, q42
 
 
-def sweep_kernel(field, rate, diffusivity, local, p0, p1, p2, p3, profiles, to_low, to_high, xs, rates, kappa, exits, scratch, sems):
-    here = lax.axis_index("lev")
-    small = start_all([pltpu.make_async_copy(rate, rates, sems.at[3]), pltpu.make_async_copy(diffusivity, kappa, sems.at[4])])
-    loads = []
-    for tile in range(LONS // 8):
-        lons = pl.ds(8 * tile, 8)
-        loads.append(pltpu.make_async_copy(field.at[:, lons, :], xs.at[:, lons, :], sems.at[tile]))
-    start_all(loads)
-    wait_all(small)
-    coefficients = responses(rates, profiles, scratch)
-    for lon in range(LONS):
-        for which, tiles in enumerate(coefficients):
-            record = slot(lon) * RECORD + STATES + which
-            exits[record : record + 1, :] = tiles[lon // 8][lon % 8 : lon % 8 + 1, :]
-    profile_rows = profiles.reshape(4 * LEVELS * LONS, LATS)
-    height = MEMBERS + 8
-    for lon, out in ((0, to_low), (LONS - GROUP, to_high)):
-        packed = out.reshape(LEVELS * GROUP * height, LATS)
-        packed[pl.ds(MEMBERS + 4, GROUP, stride=height), :] = kappa[lon : lon + GROUP, :]
-        for level in range(LEVELS):
-            for n in range(4):
-                start = (n * LEVELS + level) * LONS + lon
-                packed[pl.ds(level * GROUP * height + MEMBERS + n, GROUP, stride=height), :] = profile_rows[pl.ds(start, GROUP), :]
+def sweep_groups(groups, xs, rates, table, local, exits, before):
     values = xs.reshape(LEVELS * MEMBERS * LONS, LATS)
     weights = rates.reshape(LEVELS * LONS, LATS)
 
-    def run(group, carry):
-        lon = GROUP * group
+    def run(index, carry):
+        lon = GROUP * (groups[0] + index * (groups[1] - groups[0]))
         for number in range(4):
             order = range(LEVELS) if number % 2 == 0 else range(LEVELS - 1, -1, -1)
             state = {}
@@ -133,64 +113,106 @@
                             start = (level * MEMBERS + 8 * half) * LONS + lon + j
                             value = values[pl.ds(start, 8, stride=LONS), :]
                         else:
-                            value = local[level, lon + j, 8 * half : 8 * half + 8, :]
+                            value = local[level, GROUP * index + j, 8 * half : 8 * half + 8, :]
                         value = rest * value
                         if (j, half) in state:
                             value = weight * state[j, half] + value
                         state[j, half] = value
-                        local[level, lon + j, 8 * half : 8 * half + 8, :] = value
+                        local[level, GROUP * index + j, 8 * half : 8 * half + 8, :] = value
             for (j, half), value in state.items():
-                edge = jnp.where(group == 0, j * SHARE, j * SHARE + 1)
-                inner = (group - 1) * SHARE + 2 + j
-                place = jnp.where((group == 0) | (group == GROUPS - 1), edge, inner)
-                exits[pl.ds(pl.multiple_of(place * RECORD + 16 * number + 8 * half, 8), 8), :] = value
+                place = slot(groups, index, j) * RECORD + 16 * number + 8 * half
+                exits[pl.ds(place if isinstance(place, int) else pl.multiple_of(place, 8), 8), :] = value
         return carry
 
-    for tile in range(LONS // 8):
-        loads[tile].wait()
-        lax.fori_loop(2 * tile, 2 * tile + 2, run, 0)
-    for shift, piece in enumerate((p0, p1, p2, p3)):
+    for index, group in enumerate(groups):
+        for j in range(GROUP):
+            lon = GROUP * group + j
+            for which in range(6):
+                record = slot(groups, index, j) * RECORD + STATES + which
+                exits[record : record + 1, :] = table[which, lon : lon + 1, :]
+    if groups == EDGE:
+        for index in range(len(groups)):
+            before[index]()
+            run(index, 0)
+    else:
+        lax.fori_loop(0, len(groups), run, 0)
+
+
+def share_out(exits, pieces, rows):
+    here = lax.axis_index("lev")
+    for shift, piece in enumerate(pieces):
         target = lax.rem(here + shift, BLOCKS)
-        piece[...] = exits[pl.ds(pl.multiple_of(target * (SHARE * RECORD), 8), SHARE * RECORD), :]
-    for lon, out in ((0, to_low), (LONS - GROUP, to_high)):
-        for j in range(GROUP):
-            out[:, j, 0:MEMBERS, :] = local[:, lon + j]
-
-
-def sweep_call(field, rate, diffusivity):
-    halo = resident(LEVELS, GROUP, MEMBERS + 8, LATS)
-    outs = [resident(LEVELS, LONS, MEMBERS, LATS)] + [resident(SHARE * RECORD, LATS)] * BLOCKS
-    outs += [resident(4, LEVELS, LONS, LATS), halo, halo]
+        piece[...] = exits[pl.ds(pl.multiple_of(target * rows, 8), rows), :]
+
+
+def edge_sweep_kernel(field, rate, local, p0, p1, p2, p3, profiles, table, xs, rates, exits, scratch, sems):
+    small = pltpu.make_async_copy(rate, rates, sems.at[3])
+    small.start()
+    loads = {}
+    for tile in (0, 2, 1):
+        lons = pl.ds(8 * tile, 8)
+        loads[tile] = pltpu.make_async_copy(field.at[:, lons, :], xs.at[:, lons, :], sems.at[tile])
+        loads[tile].start()
+    small.wait()
+    for which, tiles in enumerate(responses(rates, profiles, scratch)):
+        for tile, value in enumerate(tiles):
+            table[which, 8 * tile : 8 * tile + 8, :] = value
+    sweep_groups(EDGE, xs, rates, table, local, exits, [loads[0].wait, loads[2].wait])
+    share_out(exits, (p0, p1, p2, p3), len(EDGE) * RECORD)
+    loads[1].wait()
+
+
+def edge_sweep_call(field, rate):
+    count = GROUP * len(EDGE)
+    outs = [resident(LEVELS, count, MEMBERS, LATS)] + [resident(len(EDGE) * RECORD, LATS)] * BLOCKS
+    outs += [resident(4, LEVELS, LONS, LATS), resident(6, LONS, LATS), resident(LEVELS * MEMBERS, LONS, LATS), resident(LEVELS, LONS, LATS)]
     return pl.pallas_call(
-        sweep_kernel,
+        edge_sweep_kernel,
         out_shape=outs,
-        in_specs=[OFF_CHIP] * 3,
+        in_specs=[OFF_CHIP] * 2,
         out_specs=[ON_CHIP] * len(outs),
         scratch_shapes=[
-            pltpu.VMEM((LEVELS * MEMBERS, LONS, LATS), F32),
-            pltpu.VMEM((LEVELS, LONS, LATS), F32),
-            pltpu.VMEM((LONS, LATS), F32),
-            pltpu.VMEM((LONS * RECORD, LATS), F32),
+            pltpu.VMEM((count * RECORD, LATS), F32),
             pltpu.VMEM((2, LEVELS, LONS, LATS), F32),
-            pltpu.SemaphoreType.DMA((5,)),
+            pltpu.SemaphoreType.DMA((4,)),
         ],
         compiler_params=ROOM,
-        name="sweeps",
-    )(*(pltpu.with_memory_space_constraint(x, pltpu.HBM) for x in (field, rate, diffusivity)))
-
-
-def solve_kernel(*refs):
+        cost_estimate=cost(3 * 10**7),
+        name="edge_sweeps",
+    )(*(pltpu.with_memory_space_constraint(x, pltpu.HBM) for x in (field, rate)))
+
+
+def inner_sweep_kernel(xs, rates, table, local, p0, p1, p2, p3, exits):
+    sweep_groups(INNER, xs, rates, table, local, exits, None)
+    share_out(exits, (p0, p1, p2, p3), len(INNER) * RECORD)
+
+
+def inner_sweep_call(xs, rates, table):
+    count = GROUP * len(INNER)
+    outs = [resident(LEVELS, count, MEMBERS, LATS)] + [resident(len(INNER) * RECORD, LATS)] * BLOCKS
+    return pl.pallas_call(
+        inner_sweep_kernel,
+        out_shape=outs,
+        in_specs=[ON_CHIP] * 3,
+        out_specs=[ON_CHIP] * len(outs),
+        scratch_shapes=[pltpu.VMEM((count * RECORD, LATS), F32)],
+        compiler_params=ROOM,
+        cost_estimate=cost(5 * 10**7),
+        name="inner_sweeps",
+    )(xs, rates, table)
+
+
+def solve_kernel(share, *refs):
     pieces, outs, (records, states) = refs[:4], refs[4:8], refs[8:]
-    here = lax.axis_index("lev")
-    in_order(pieces, records, SHARE * RECORD)
+    in_order(pieces, records, share * RECORD)
 
     def run(lon, carry):
         def exit_of(block, number, half):
-            at = (block * SHARE + lon) * RECORD + 16 * number + 8 * half
+            at = (block * share + lon) * RECORD + 16 * number + 8 * half
             return records[pl.ds(pl.multiple_of(at, 8), 8), :]
 
         def response(block, which):
-            return row(records, (block * SHARE + lon) * RECORD + STATES + which)
+            return row(records, (block * share + lon) * RECORD + STATES + which)
 
         for half in range(2):
             zero = jnp.zeros((8, LATS), F32)
@@ -216,28 +238,26 @@
                 )
             for d in range(BLOCKS):
                 for number, entering in enumerate((f1, b1, f2, b2)):
-                    at = (d * SHARE + lon) * STATES + 16 * number + 8 * half
+                    at = (d * share + lon) * STATES + 16 * number + 8 * half
                     states[pl.ds(pl.multiple_of(at, 8), 8), :] = entering[d]
         return carry
 
-    lax.fori_loop(0, SHARE, run, 0)
-    for shift, out in enumerate(outs):
-        target = lax.rem(here + shift, BLOCKS)
-        out[...] = states[pl.ds(pl.multiple_of(target * (SHARE * STATES), 8), SHARE * STATES), :]
+    lax.fori_loop(0, share, run, 0)
+    share_out(states, outs, share * STATES)
 
 
 def solve_call(pieces):
+    share = pieces[0].shape[0] // RECORD
     return pl.pallas_call(
-        solve_kernel,
-        out_shape=[resident(SHARE * STATES, LATS)] * BLOCKS,
+        functools.partial(solve_kernel, share),
+        out_shape=[resident(share * STATES, LATS)] * BLOCKS,
         in_specs=[ON_CHIP] * BLOCKS,
         out_specs=[ON_CHIP] * BLOCKS,
         scratch_shapes=[
-            pltpu.VMEM((BLOCKS * SHARE * RECORD, LATS), F32),
-            pltpu.VMEM((BLOCKS * SHARE * STATES, LATS), F32),
+            pltpu.VMEM((BLOCKS * share * RECORD, LATS), F32),
+            pltpu.VMEM((BLOCKS * share * STATES, LATS), F32),
         ],
         compiler_params=ROOM,
-        name="solve",
     )(*pieces)
 
 
@@ -272,12 +292,47 @@
         rows[block * PAD + LATS + 8 : (block + 1) * PAD, :] = zero
 
 
-def inner_kernel(local, profiles, kappa, s0, s1, s2, s3, out, begun, kept, spread_rows, states, buffers, made, sems):
+def edge_kernel(local, profiles, kappa, s0, s1, s2, s3, to_low, to_high, states):
+    in_order((s0, s1, s2, s3), states, len(EDGE) * STATES)
+    profile_rows = profiles.reshape(4 * LEVELS * LONS, LATS)
+    for index, out in enumerate((to_low, to_high)):
+        lon = GROUP * EDGE[index]
+        out[HALO : HALO + 8, :] = kappa[8 * (lon // 8) : 8 * (lon // 8) + 8, :]
+
+    def run(slab, carry):
+        for index, out in enumerate((to_low, to_high)):
+            for j in range(GROUP):
+                lon = GROUP * EDGE[index] + j
+                block = corrected_block(
+                    lambda level, half: local[slab * SLAB + level, GROUP * index + j, 8 * half : 8 * half + 8, :],
+                    lambda n, level: row(profile_rows, (n * LEVELS + slab * SLAB + level) * LONS + lon),
+                    entering_of(states, slot(EDGE, index, j) * STATES),
+                )
+                out[pl.ds(pl.multiple_of((j * SLABS + slab) * LATS, 8), LATS), :] = jnp.transpose(block)
+        return carry
+
+    lax.fori_loop(0, SLABS, run, 0)
+
+
+def edge_call(local, profiles, diffusivity, pieces):
+    return pl.pallas_call(
+        edge_kernel,
+        out_shape=[resident(HALO + 8, LATS)] * 2,
+        in_specs=[ON_CHIP] * 7,
+        out_specs=[ON_CHIP] * 2,
+        scratch_shapes=[pltpu.VMEM((GROUP * len(EDGE) * STATES, LATS), F32)],
+        compiler_params=ROOM,
+        cost_estimate=cost(10**7),
+        name="edges",
+    )(local, profiles, diffusivity, *pieces)
+
+
+def inner_kernel(local, profiles, kappa, to_low, to_high, s0, s1, s2, s3, out, begun, kept, spread_rows, states, buffers, made, sems):
     def save(slab):
         part = pl.ds(slab * SLAB * MEMBERS, SLAB * MEMBERS)
         return pltpu.make_async_copy(made.at[part], out.at[part, pl.ds(8, 8), :], sems.at[slab])
 
-    in_order((s0, s1, s2, s3), states, SHARE * STATES)
+    in_order((s0, s1, s2, s3), states, len(INNER) * STATES)
     rows = buffers.reshape(2 * LONS * PAD, LATS)
     kept_rows = kept.reshape(SLABS * 2 * 2 * SMOOTH * PAD, LATS)
     clear_pads(rows, 2 * LONS)
@@ -296,13 +351,17 @@
             return None
 
         for lon in range(LONS):
-            block = jnp.transpose(
-                corrected_block(
-                    lambda level, half: local[slab * SLAB + level, lon, 8 * half : 8 * half + 8, :],
-                    lambda n, level: row(profile_rows, (n * LEVELS + slab * SLAB + level) * LONS + lon),
-                    entering_of(states, slot(lon) * STATES),
+            if GROUP <= lon < LONS - GROUP:
+                block = jnp.transpose(
+                    corrected_block(
+                        lambda level, half: local[slab * SLAB + level, lon - GROUP, 8 * half : 8 * half + 8, :],
+                        lambda n, level: row(profile_rows, (n * LEVELS + slab * SLAB + level) * LONS + lon),
+                        entering_of(states, (lon - GROUP) * STATES),
+                    )
                 )
-            )
+            else:
+                sent, j = (to_low, lon) if lon < GROUP else (to_high, lon - LONS + GROUP)
+                block = sent[pl.ds(pl.multiple_of((j * SLABS + slab) * LATS, 8), LATS), :]
             buffers[0, lon, 8 : 8 + LATS, :] = block
             start = keep(0, lon)
             if start is not None:
@@ -348,7 +407,7 @@
     wait_all([save(slab) for slab in range(SLABS)])
 
 
-def inner_call(local, profiles, diffusivity, pieces):
+def inner_call(local, profiles, diffusivity, to_low, to_high, pieces):
     return pl.pallas_call(
         inner_kernel,
         out_shape=[
@@ -357,22 +416,21 @@
             resident(SLABS, 2, 2 * SMOOTH, PAD, LATS),
             resident(LONS, LATS, LATS),
         ],
-        in_specs=[ON_CHIP] * 7,
+        in_specs=[ON_CHIP] * 9,
         out_specs=[OFF_CHIP, ON_CHIP, ON_CHIP, ON_CHIP],
         scratch_shapes=[
-            pltpu.VMEM((LONS * STATES, LATS), F32),
+            pltpu.VMEM((GROUP * len(INNER) * STATES, LATS), F32),
             pltpu.VMEM((2, LONS, PAD, LATS), F32),
             pltpu.VMEM((LEVELS * MEMBERS, 8, LATS), F32),
             pltpu.SemaphoreType.DMA((SLABS,)),
         ],
         compiler_params=ROOM,
-        cost_estimate=pl.CostEstimate(flops=10**8, transcendentals=0, bytes_accessed=10**7),
+        cost_estimate=cost(2 * 10**8),
         name="inner",
-    )(local, profiles, diffusivity, *pieces)
-
-
-def outer_kernel(whole, begun, kept, spread_rows, low, high, low_s, high_s, out, filled, buffers, halo_spread, sems):
-    here = lax.axis_index("lev")
+    )(local, profiles, diffusivity, to_low, to_high, *pieces)
+
+
+def outer_kernel(whole, begun, kept, spread_rows, low, high, out, filled, buffers, halo_spread, sems):
     places = 2 * SMOOTH
 
     def saves(slab):
@@ -385,29 +443,19 @@
     rows = buffers.reshape(2 * 2 * places * PAD, LATS)
     kept_rows = kept.reshape(SLABS * 2 * 2 * SMOOTH * PAD, LATS)
     clear_pads(rows, 2 * 2 * places)
-    height = MEMBERS + 8
-    halos = [(low, low_s), (high, high_s)]
-    for side, (halo, _) in enumerate(halos):
+    for side, halo in enumerate((low, high)):
         for j in range(GROUP):
             place = j if side == 0 else GROUP - 1 - j
-            halo_spread[side, place] = spread(halo[0, j, MEMBERS + 4 : MEMBERS + 5, :])
+            at = HALO + (GROUP + j if side == 0 else j)
+            halo_spread[side, place] = spread(halo[at : at + 1, :])
     filled_rows = filled.reshape(2 * LEVELS * MEMBERS * 8, LATS)
 
     def run(slab, carry):
-        for side, (halo, halo_states) in enumerate(halos):
-            halo_rows = halo.reshape(LEVELS * GROUP * height, LATS)
+        for side, halo in enumerate((low, high)):
             for j in range(GROUP):
                 place = j if side == 0 else GROUP - 1 - j
-                start = lax.rem(here - j + BLOCKS, BLOCKS) * STATES
-                entering = [
-                    [halo_states[pl.ds(pl.multiple_of(start + 16 * n + 8 * half, 8), 8), :] for n in range(4)] for half in range(2)
-                ]
-                block = corrected_block(
-                    lambda level, half: halo[slab * SLAB + level, j, 8 * half : 8 * half + 8, :],
-                    lambda n, level: row(halo_rows, ((slab * SLAB + level) * GROUP + j) * height + MEMBERS + n),
-                    entering,
-                )
-                buffers[0, side, place, 8 : 8 + LATS, :] = jnp.transpose(block)
+                block = halo[pl.ds(pl.multiple_of((j * SLABS + slab) * LATS, 8), LATS), :]
+                buffers[0, side, place, 8 : 8 + LATS, :] = block
         for step in range(SMOOTH):
 
             def tile(t, carry):
@@ -451,11 +499,11 @@
         wait_all(saves(slab))
 
 
-def outer_call(whole, begun, kept, spread_rows, low, high, low_s, high_s):
+def outer_call(whole, begun, kept, spread_rows, low, high):
     return pl.pallas_call(
         outer_kernel,
         out_shape=[shape(LEVELS * MEMBERS, LONS, LATS), resident(2, LEVELS * MEMBERS, 8, LATS)],
-        in_specs=[OFF_CHIP] + [ON_CHIP] * 7,
+        in_specs=[OFF_CHIP] + [ON_CHIP] * 5,
         out_specs=[OFF_CHIP, ON_CHIP],
         input_output_aliases={0: 0, 1: 1},
         scratch_shapes=[
@@ -465,7 +513,7 @@
         ],
         compiler_params=ROOM,
         name="outer",
-    )(whole, begun, kept, spread_rows, low, high, low_s, high_s)
+    )(whole, begun, kept, spread_rows, low, high)
 
 
 def shifted(pieces):
@@ -479,21 +527,21 @@
     count = lax.axis_size("col")
     forward = [(i, i + 1) for i in range(count - 1)]
     backward = [(b, a) for a, b in forward]
-    return lax.ppermute(to_high, "col", forward), lax.ppermute(to_low, "col", backward)
+    low = lax.ppermute(to_high, "col", forward)
+    high = lax.ppermute(to_low, "col", backward)
+    return low, high
 
 
 def per_device(control_field, decay_rate, diffusivity):
     field = control_field.reshape(LEVELS * MEMBERS, LONS, LATS)
-    local, *pieces, profiles, to_low, to_high = sweep_call(field, decay_rate, diffusivity)
-    pieces = shifted(pieces)
+    edge_local, *edge_pieces, profiles, table, xs, rates = edge_sweep_call(field, decay_rate)
+    inner_local, *inner_pieces = inner_sweep_call(xs, rates, table)
+    edge_states = shifted(solve_call(shifted(edge_pieces)))
+    inner_states = shifted(solve_call(shifted(inner_pieces)))
+    to_low, to_high = edge_call(edge_local, profiles, diffusivity, edge_states)
     low, high = exchanged(to_low, to_high)
-    states = shifted(solve_call(pieces))
-    low_s, high_s = exchanged(
-        jnp.concatenate([piece[:STATES] for piece in states]),
-        jnp.concatenate([piece[STATES : 2 * STATES] for piece in states]),
-    )
-    whole, begun, kept, spread_rows = inner_call(local, profiles, diffusivity, states)
-    out, _ = outer_call(whole, begun, kept, spread_rows, low, high, low_s, high_s)
+    whole, begun, kept, spread_rows = inner_call(inner_local, profiles, diffusivity, to_low, to_high, inner_states)
+    out, _ = outer_call(whole, begun, kept, spread_rows, low, high)
     return out.reshape(control_field.shape)
 
 

time: 54.2 us -> 63 us (1.16)
  waiting for transfers between devices: 8.28 us -> 20.9 us
  starting transfers between devices: 26.5 us -> 23.1 us
    ppermute x6 -> x12, waiting for transfers between devices: 8.27 us -> 20.8 us  [shifted(): lax.ppermute(pieces[shift], 'lev', [(i, (i + shift) % BLOCKS) for i in ra...]
    ppermute x4 -> x2, starting transfers between devices: 15.3 us -> 4.33 us  [the longest x1 2.41 us: exchanged(): low = lax.ppermute(to_high, 'col', forward)]
    ppermute x6 -> x12, starting transfers between devices: 11.2 us -> 18.7 us  [shifted(): lax.ppermute(pieces[shift], 'lev', [(i, (i + shift) % BLOCKS) for i in ra...]
    pallas_call x2 -> x5, Pallas kernels: 4.66 us -> 5.3 us  [the longest x1 2.53 us: edge_sweep_call(): pl.pallas_call(edge_sweep_kernel, out_shape=outs, in_specs=[OFF_CHIP] * 2...]
  transfers between devices with their start and end apart: 10 -> 14, of which waited for: 3 -> 10; matrix products, arithmetic and copies ran while one was open for 0% -> 0% of each run, Pallas kernels for 18% -> 17%
where the time goes in v4:
time: 63 us; the launch traced here: 62.7 us
  starting transfers between devices  23.1 us (37%)
  waiting for transfers between devices  20.9 us (33%)
  Pallas kernels  18.7 us (30%)
    ppermute x12, waiting for transfers between devices, shifted(): lax.ppermute(pieces[shift], 'lev', [(i, (i + shift) % BLOCKS) for i in ra...  20.8 us
    ppermute x12, starting transfers between devices, shifted(): lax.ppermute(pieces[shift], 'lev', [(i, (i + shift) % BLOCKS) for i in ra...  18.7 us
    pallas_call x1, Pallas kernels, inner_call(): pl.pallas_call(inner_kernel, out_shape=[shape(LEVELS * MEMBERS, LONS, LAT...  8.87 us
    pallas_call x1, Pallas kernels, outer_call(): pl.pallas_call(outer_kernel, out_shape=[shape(LEVELS * MEMBERS, LONS, LAT...  4.53 us
    pallas_call x1, Pallas kernels, edge_sweep_call(): pl.pallas_call(edge_sweep_kernel, out_shape=outs, in_specs=[OFF_CHIP] * 2...  2.53 us
    ppermute x1, starting transfers between devices, exchanged(): low = lax.ppermute(to_high, 'col', forward)  2.41 us
    ppermute x1, starting transfers between devices, exchanged(): high = lax.ppermute(to_low, 'col', backward)  1.92 us
    pallas_call x1, Pallas kernels, inner_sweep_call(): pl.pallas_call(inner_sweep_kernel, out_shape=outs, in_specs=[ON_CHIP] * 3...  1.76 us
  transfers between devices with their start and end apart: 14, of which 10 were waited for; matrix products, arithmetic and copies ran while one was open for 0% of the time, Pallas kernels for 17%

profile of v4, /device:TPU:64, one launch (start us, length us, event | category | flops | bytes accessed | tf_op | source)
XLA Modules:
  0.0 62.7 jit_solution(12827272567268063713)
XLA Ops:
  0.0 0.0 copy-start
  0.0 2.5 %edge_sweeps.1 = (f32[24,8,16,128]{3,2,1,0:T(8,128)S(1)}, f32[144,128]{1,0:T(8,128)S(1)}, f32[144,128]{1,0:T(8,128)S(1)}, f32[144,128]{1,0:T(8,128)S(1)}, f32[14...) custom-call(f32[384,24,128]{2,1,0:T(8,128)} %bitcast.2, ...), custom_call_target="tpu_custom_call" | custom-call | flops 30000000 | bytes 1000000 | tf_op jit(solution)/shard_map/edge_sweeps/pallas_call | solution.py:169
  2.5 1.6 %collective-permute-start = (f32[144,128]{1,0:T(8,128)S(1)}, f32[144,128]{1,0:T(8,128)S(1)}, u32[]{:S(2)}, u32[]{:S(2)}) collective-permute-start(f32[144,128]{1,0:T(8,128)S(1)} %get-tuple-element.41), channel_id=1, source_target_pairs={{0,32},{32,64},{64,96},{96,0},{1,33},{33,65},{65,97},{97,1},{2,34}... | collective-permute-start | bytes 221192 | tf_op jit(solution)/shard_map/ppermute | solution.py:522
  4.2 2.9 %collective-permute-start.1 = (f32[144,128]{1,0:T(8,128)S(1)}, f32[144,128]{1,0:T(8,128)S(1)}, u32[]{:S(2)}, u32[]{:S(2)}) collective-permute-start(f32[144,128]{1,0:T(8,128)S(1)} %get-tuple-element.42), channel_id=1, source_target_pairs={{0,64},{32,96},{64,0},{96,32},{1,65},{33,97},{65,1},{97,33},{2,66}... | collective-permute-start | bytes 221192 | tf_op jit(solution)/shard_map/ppermute | solution.py:522
  7.1 1.3 %collective-permute-start.2 = (f32[144,128]{1,0:T(8,128)S(1)}, f32[144,128]{1,0:T(8,128)S(1)}, u32[]{:S(2)}, u32[]{:S(2)}) collective-permute-start(f32[144,128]{1,0:T(8,128)S(1)} %get-tuple-element.43), channel_id=1, source_target_pairs={{0,96},{32,0},{64,32},{96,64},{1,97},{33,1},{65,33},{97,65},{2,98}... | collective-permute-start | bytes 221192 | tf_op jit(solution)/shard_map/ppermute | solution.py:522
  8.4 0.0 collective-permute-done.refs_1_
  8.4 2.2 %collective-permute-done.1.refs_2_ = f32[144,128]{1,0:T(8,128)S(1)} collective-permute-done((f32[144,128]{1,0:T(8,128)S(1)}, f32[144,128]{1,0:T(8,128)S(1)}, u32[]{:S(2)}, u32[]{:S(2)}) %collective-permute-start.1) | collective-permute-done | bytes 73760 | tf_op jit(solution)/shard_map/ppermute | solution.py:522
  10.6 0.8 %collective-permute-done.2.refs_3_ = f32[144,128]{1,0:T(8,128)S(1)} collective-permute-done((f32[144,128]{1,0:T(8,128)S(1)}, f32[144,128]{1,0:T(8,128)S(1)}, u32[]{:S(2)}, u32[]{:S(2)}) %collective-permute-start.2) | collective-permute-done | bytes 73760 | tf_op jit(solution)/shard_map/ppermute | solution.py:522
  11.4 0.1 shard_map.37
  11.6 0.5 collective-permute-start.3
  12.1 3.6 %collective-permute-start.4 = (f32[128,128]{1,0:T(8,128)S(1)}, f32[128,128]{1,0:T(8,128)S(1)}, u32[]{:S(2)}, u32[]{:S(2)}) collective-permute-start(f32[128,128]{1,0:T(8,128)S(1)} %get-tuple-element.46), channel_id=1, source_target_pairs={{0,64},{32,96},{64,0},{96,32},{1,65},{33,97},{65,1},{97,33},{2,66}... | collective-permute-start | bytes 196616 | tf_op jit(solution)/shard_map/ppermute | solution.py:522
  15.7 0.3 collective-permute-start.5
  16.0 1.1 %collective-permute-done.3.s1 = f32[128,128]{1,0:T(8,128)S(1)} collective-permute-done((f32[128,128]{1,0:T(8,128)S(1)}, f32[128,128]{1,0:T(8,128)S(1)}, u32[]{:S(2)}, u32[]{:S(2)}) %collective-permute-start.3) | collective-permute-done | bytes 65568 | tf_op jit(solution)/shard_map/ppermute | solution.py:522
  17.1 1.5 %collective-permute-done.4.s2 = f32[128,128]{1,0:T(8,128)S(1)} collective-permute-done((f32[128,128]{1,0:T(8,128)S(1)}, f32[128,128]{1,0:T(8,128)S(1)}, u32[]{:S(2)}, u32[]{:S(2)}) %collective-permute-start.4) | collective-permute-done | bytes 65568 | tf_op jit(solution)/shard_map/ppermute | solution.py:522
  18.6 1.3 %collective-permute-done.5.s3 = f32[128,128]{1,0:T(8,128)S(1)} collective-permute-done((f32[128,128]{1,0:T(8,128)S(1)}, f32[128,128]{1,0:T(8,128)S(1)}, u32[]{:S(2)}, u32[]{:S(2)}) %collective-permute-start.5) | collective-permute-done | bytes 65568 | tf_op jit(solution)/shard_map/ppermute | solution.py:522
  19.9 0.0 copy-done
  19.9 0.7 %edges.1 = (f32[1544,128]{1,0:T(8,128)S(1)}, f32[1544,128]{1,0:T(8,128)S(1)}) custom-call(f32[24,8,16,128]{3,2,1,0:T(8,128)S(1)} %get-tuple-element.39.local, f32[4,24,24,128]{3,2,1,0:T(8,128)S(1)} %get-tuple-element.38.profiles, f32[24,128]{1,0:T(8,128)S(1)} %copy-done, f32[128,128]{1,0:T(8,128)S(1)} %get-tuple-element.44.s0, ...), custom_call_target="tpu_custom_call" | custom-call | flops 10000000 | bytes 1000000 | tf_op jit(solution)/shard_map/edges/pallas_call | solution.py:318
  20.6 1.9 %collective-permute-start.13 = (f32[1544,128]{1,0:T(8,128)S(1)}, f32[1544,128]{1,0:T(8,128)S(1)}, u32[]{:S(2)}, u32[]{:S(2)}) collective-permute-start(f32[1544,128]{1,0:T(8,128)S(1)} %get-tuple-element.48.to_low), channel_id=1, source_target_pairs={{1,0},{2,1},{3,2},{4,3},{5,4},{6,5},{7,6},{8,7},{9,8},{10,9},{11,1... | collective-permute-start | bytes 2371592 | tf_op jit(solution)/shard_map/ppermute | solution.py:531
  22.5 2.4 %collective-permute-start.12 = (f32[1544,128]{1,0:T(8,128)S(1)}, f32[1544,128]{1,0:T(8,128)S(1)}, u32[]{:S(2)}, u32[]{:S(2)}) collective-permute-start(f32[1544,128]{1,0:T(8,128)S(1)} %get-tuple-element.49.to_high), channel_id=1, source_target_pairs={{0,1},{1,2},{2,3},{3,4},{4,5},{5,6},{6,7},{7,8},{8,9},{9,10},{10,1... | collective-permute-start | bytes 2371592 | tf_op jit(solution)/shard_map/ppermute | solution.py:530
  24.9 1.8 %inner_sweeps.1 = (f32[24,16,16,128]{3,2,1,0:T(8,128)S(1)}, f32[288,128]{1,0:T(8,128)S(1)}, f32[288,128]{1,0:T(8,128)S(1)}, f32[288,128]{1,0:T(8,128)S(1)}, f32[288,128]{1,0:T(8,128)S(1)}) custom-call(f32[384,24,128]{2,1,0:T(8,128)S(1)} %get-tuple-element.34.xs, f32[24,24,128]{2,1,0:T(8,128)S(1)} %get-tuple-element.35.rates, ...), custom_call_target="tpu_custom_call" | custom-call | flops 50000000 | bytes 1000000 | tf_op jit(solution)/shard_map/inner_sweeps/pallas_call | solution.py:193
  26.7 0.1 collective-permute-start.6
  26.9 2.9 %collective-permute-start.7 = (f32[288,128]{1,0:T(8,128)S(1)}, f32[288,128]{1,0:T(8,128)S(1)}, u32[]{:S(2)}, u32[]{:S(2)}) collective-permute-start(f32[288,128]{1,0:T(8,128)S(1)} %get-tuple-element.52), channel_id=1, source_target_pairs={{0,64},{32,96},{64,0},{96,32},{1,65},{33,97},{65,1},{97,33},{2,66}... | collective-permute-start | bytes 442376 | tf_op jit(solution)/shard_map/ppermute | solution.py:522
  29.8 1.1 %collective-permute-start.8 = (f32[288,128]{1,0:T(8,128)S(1)}, f32[288,128]{1,0:T(8,128)S(1)}, u32[]{:S(2)}, u32[]{:S(2)}) collective-permute-start(f32[288,128]{1,0:T(8,128)S(1)} %get-tuple-element.53), channel_id=1, source_target_pairs={{0,96},{32,0},{64,32},{96,64},{1,97},{33,1},{65,33},{97,65},{2,98}... | collective-permute-start | bytes 442376 | tf_op jit(solution)/shard_map/ppermute | solution.py:522
  30.9 3.8 %collective-permute-done.6.refs_1_ = f32[288,128]{1,0:T(8,128)S(1)} collective-permute-done((f32[288,128]{1,0:T(8,128)S(1)}, f32[288,128]{1,0:T(8,128)S(1)}, u32[]{:S(2)}, u32[]{:S(2)}) %collective-permute-start.6) | collective-permute-done | bytes 147488 | tf_op jit(solution)/shard_map/ppermute | solution.py:522
  34.7 2.9 %collective-permute-done.7.refs_2_ = f32[288,128]{1,0:T(8,128)S(1)} collective-permute-done((f32[288,128]{1,0:T(8,128)S(1)}, f32[288,128]{1,0:T(8,128)S(1)}, u32[]{:S(2)}, u32[]{:S(2)}) %collective-permute-start.7) | collective-permute-done | bytes 147488 | tf_op jit(solution)/shard_map/ppermute | solution.py:522
  37.6 1.0 %collective-permute-done.8.refs_3_ = f32[288,128]{1,0:T(8,128)S(1)} collective-permute-done((f32[288,128]{1,0:T(8,128)S(1)}, f32[288,128]{1,0:T(8,128)S(1)}, u32[]{:S(2)}, u32[]{:S(2)}) %collective-permute-start.8) | collective-permute-done | bytes 147488 | tf_op jit(solution)/shard_map/ppermute | solution.py:522
  38.6 0.2 shard_map.38
  38.9 0.9 %collective-permute-start.9 = (f32[256,128]{1,0:T(8,128)S(1)}, f32[256,128]{1,0:T(8,128)S(1)}, u32[]{:S(2)}, u32[]{:S(2)}) collective-permute-start(f32[256,128]{1,0:T(8,128)S(1)} %get-tuple-element.55), channel_id=1, source_target_pairs={{0,32},{32,64},{64,96},{96,0},{1,33},{33,65},{65,97},{97,1},{2,34}... | collective-permute-start | bytes 393224 | tf_op jit(solution)/shard_map/ppermute | solution.py:522
  39.8 3.2 %collective-permute-start.10 = (f32[256,128]{1,0:T(8,128)S(1)}, f32[256,128]{1,0:T(8,128)S(1)}, u32[]{:S(2)}, u32[]{:S(2)}) collective-permute-start(f32[256,128]{1,0:T(8,128)S(1)} %get-tuple-element.56), channel_id=1, source_target_pairs={{0,64},{32,96},{64,0},{96,32},{1,65},{33,97},{65,1},{97,33},{2,66}... | collective-permute-start | bytes 393224 | tf_op jit(solution)/shard_map/ppermute | solution.py:522
  43.0 0.0 collective-permute-start.11
  43.1 2.4 %collective-permute-done.9.s1 = f32[256,128]{1,0:T(8,128)S(1)} collective-permute-done((f32[256,128]{1,0:T(8,128)S(1)}, f32[256,128]{1,0:T(8,128)S(1)}, u32[]{:S(2)}, u32[]{:S(2)}) %collective-permute-start.9) | collective-permute-done | bytes 131104 | tf_op jit(solution)/shard_map/ppermute | solution.py:522
  45.5 3.8 %collective-permute-done.10.s2 = f32[256,128]{1,0:T(8,128)S(1)} collective-permute-done((f32[256,128]{1,0:T(8,128)S(1)}, f32[256,128]{1,0:T(8,128)S(1)}, u32[]{:S(2)}, u32[]{:S(2)}) %collective-permute-start.10) | collective-permute-done | bytes 131104 | tf_op jit(solution)/shard_map/ppermute | solution.py:522
  49.3 0.0 collective-permute-done.11.s3
  49.3 8.9 %inner.1 = (f32[384,24,128]{2,1,0:T(8,128)}, f32[2,384,8,128]{3,2,1,0:T(8,128)S(1)}, f32[3,2,8,144,128]{4,3,2,1,0:T(8,128)S(1)}, f32[24,128,128]{2,1,0:T(8,128)S(1)}) custom-call(f32[24,16,16,128]{3,2,1,0:T(8,128)S(1)} %get-tuple-element.37.local, f32[4,24,24,128]{3,2,1,0:T(8,128)S(1)} %get-tuple-element.38.profiles, f32[24,128]{1,0:T(8,128)S(1)} %copy-done, ...), custom_call_target="tpu_custom_call" | custom-call | flops 200000000 | bytes 1000000 | tf_op jit(solution)/shard_map/inner/pallas_call | solution.py:411
  58.2 0.0 collective-permute-done.13.high
  58.2 0.0 collective-permute-done.12.low
  58.2 4.5 %outer.1 = (f32[384,24,128]{2,1,0:T(8,128)}, f32[2,384,8,128]{3,2,1,0:T(8,128)S(1)}) custom-call(f32[384,24,128]{2,1,0:T(8,128)} %get-tuple-element.58.whole, f32[2,384,8,128]{3,2,1,0:T(8,128)S(1)} %get-tuple-element.59.begun, f32[3,2,8,144,128]{4,3,2,1,0:T(8,128)S(1)} %get-tuple-element.60.kept, ...), custom_call_target="tpu_custom_call", output_to_operand_aliasing={{0}: (0, {}), {1}: (1, {})} | custom-call | tf_op jit(solution)/shard_map/outer/pallas_call | solution.py:503
Async XLA Ops:
  0.0 19.9 %copy-start = (f32[24,128]{1,0:T(8,128)S(1)}, f32[24,128]{1,0:T(8,128)}, u32[]{:S(2)}) copy-start(f32[24,128]{1,0:T(8,128)} %kappa.3) | copy-start | bytes 36868
  2.5 5.9 %collective-permute-start = (f32[144,128]{1,0:T(8,128)S(1)}, f32[144,128]{1,0:T(8,128)S(1)}, u32[]{:S(2)}, u32[]{:S(2)}) collective-permute-start(f32[144,128]{1,0:T(8,128)S(1)} %get-tuple-element.41), channel_id=1, source_target_pairs={{0,32},{32,64},{64,96},{96,0},{1,33},{33,65},{65,97},{97,1},{2,34}... | collective-permute-start | bytes 221192 | tf_op jit(solution)/shard_map/ppermute | solution.py:522
  4.2 6.5 %collective-permute-start.1 = (f32[144,128]{1,0:T(8,128)S(1)}, f32[144,128]{1,0:T(8,128)S(1)}, u32[]{:S(2)}, u32[]{:S(2)}) collective-permute-start(f32[144,128]{1,0:T(8,128)S(1)} %get-tuple-element.42), channel_id=1, source_target_pairs={{0,64},{32,96},{64,0},{96,32},{1,65},{33,97},{65,1},{97,33},{2,66}... | collective-permute-start | bytes 221192 | tf_op jit(solution)/shard_map/ppermute | solution.py:522
  7.1 4.4 %collective-permute-start.2 = (f32[144,128]{1,0:T(8,128)S(1)}, f32[144,128]{1,0:T(8,128)S(1)}, u32[]{:S(2)}, u32[]{:S(2)}) collective-permute-start(f32[144,128]{1,0:T(8,128)S(1)} %get-tuple-element.43), channel_id=1, source_target_pairs={{0,96},{32,0},{64,32},{96,64},{1,97},{33,1},{65,33},{97,65},{2,98}... | collective-permute-start | bytes 221192 | tf_op jit(solution)/shard_map/ppermute | solution.py:522
  11.6 5.5 %collective-permute-start.3 = (f32[128,128]{1,0:T(8,128)S(1)}, f32[128,128]{1,0:T(8,128)S(1)}, u32[]{:S(2)}, u32[]{:S(2)}) collective-permute-start(f32[128,128]{1,0:T(8,128)S(1)} %get-tuple-element.45), channel_id=1, source_target_pairs={{0,32},{32,64},{64,96},{96,0},{1,33},{33,65},{65,97},{97,1},{2,34}... | collective-permute-start | bytes 196616 | tf_op jit(solution)/shard_map/ppermute | solution.py:522
  12.1 6.5 %collective-permute-start.4 = (f32[128,128]{1,0:T(8,128)S(1)}, f32[128,128]{1,0:T(8,128)S(1)}, u32[]{:S(2)}, u32[]{:S(2)}) collective-permute-start(f32[128,128]{1,0:T(8,128)S(1)} %get-tuple-element.46), channel_id=1, source_target_pairs={{0,64},{32,96},{64,0},{96,32},{1,65},{33,97},{65,1},{97,33},{2,66}... | collective-permute-start | bytes 196616 | tf_op jit(solution)/shard_map/ppermute | solution.py:522
  15.7 4.3 %collective-permute-start.5 = (f32[128,128]{1,0:T(8,128)S(1)}, f32[128,128]{1,0:T(8,128)S(1)}, u32[]{:S(2)}, u32[]{:S(2)}) collective-permute-start(f32[128,128]{1,0:T(8,128)S(1)} %get-tuple-element.47), channel_id=1, source_target_pairs={{0,96},{32,0},{64,32},{96,64},{1,97},{33,1},{65,33},{97,65},{2,98}... | collective-permute-start | bytes 196616 | tf_op jit(solution)/shard_map/ppermute | solution.py:522
  20.6 37.6 %collective-permute-start.13 = (f32[1544,128]{1,0:T(8,128)S(1)}, f32[1544,128]{1,0:T(8,128)S(1)}, u32[]{:S(2)}, u32[]{:S(2)}) collective-permute-start(f32[1544,128]{1,0:T(8,128)S(1)} %get-tuple-element.48.to_low), channel_id=1, source_target_pairs={{1,0},{2,1},{3,2},{4,3},{5,4},{6,5},{7,6},{8,7},{9,8},{10,9},{11,1... | collective-permute-start | bytes 2371592 | tf_op jit(solution)/shard_map/ppermute | solution.py:531
  22.5 35.6 %collective-permute-start.12 = (f32[1544,128]{1,0:T(8,128)S(1)}, f32[1544,128]{1,0:T(8,128)S(1)}, u32[]{:S(2)}, u32[]{:S(2)}) collective-permute-start(f32[1544,128]{1,0:T(8,128)S(1)} %get-tuple-element.49.to_high), channel_id=1, source_target_pairs={{0,1},{1,2},{2,3},{3,4},{4,5},{5,6},{6,7},{7,8},{8,9},{9,10},{10,1... | collective-permute-start | bytes 2371592 | tf_op jit(solution)/shard_map/ppermute | solution.py:530
  26.7 8.0 %collective-permute-start.6 = (f32[288,128]{1,0:T(8,128)S(1)}, f32[288,128]{1,0:T(8,128)S(1)}, u32[]{:S(2)}, u32[]{:S(2)}) collective-permute-start(f32[288,128]{1,0:T(8,128)S(1)} %get-tuple-element.51), channel_id=1, source_target_pairs={{0,32},{32,64},{64,96},{96,0},{1,33},{33,65},{65,97},{97,1},{2,34}... | collective-permute-start | bytes 442376 | tf_op jit(solution)/shard_map/ppermute | solution.py:522
  26.9 10.8 %collective-permute-start.7 = (f32[288,128]{1,0:T(8,128)S(1)}, f32[288,128]{1,0:T(8,128)S(1)}, u32[]{:S(2)}, u32[]{:S(2)}) collective-permute-start(f32[288,128]{1,0:T(8,128)S(1)} %get-tuple-element.52), channel_id=1, source_target_pairs={{0,64},{32,96},{64,0},{96,32},{1,65},{33,97},{65,1},{97,33},{2,66}... | collective-permute-start | bytes 442376 | tf_op jit(solution)/shard_map/ppermute | solution.py:522
  29.8 8.8 %collective-permute-start.8 = (f32[288,128]{1,0:T(8,128)S(1)}, f32[288,128]{1,0:T(8,128)S(1)}, u32[]{:S(2)}, u32[]{:S(2)}) collective-permute-start(f32[288,128]{1,0:T(8,128)S(1)} %get-tuple-element.53), channel_id=1, source_target_pairs={{0,96},{32,0},{64,32},{96,64},{1,97},{33,1},{65,33},{97,65},{2,98}... | collective-permute-start | bytes 442376 | tf_op jit(solution)/shard_map/ppermute | solution.py:522
  38.9 6.7 %collective-permute-start.9 = (f32[256,128]{1,0:T(8,128)S(1)}, f32[256,128]{1,0:T(8,128)S(1)}, u32[]{:S(2)}, u32[]{:S(2)}) collective-permute-start(f32[256,128]{1,0:T(8,128)S(1)} %get-tuple-element.55), channel_id=1, source_target_pairs={{0,32},{32,64},{64,96},{96,0},{1,33},{33,65},{65,97},{97,1},{2,34}... | collective-permute-start | bytes 393224 | tf_op jit(solution)/shard_map/ppermute | solution.py:522
  39.8 9.5 %collective-permute-start.10 = (f32[256,128]{1,0:T(8,128)S(1)}, f32[256,128]{1,0:T(8,128)S(1)}, u32[]{:S(2)}, u32[]{:S(2)}) collective-permute-start(f32[256,128]{1,0:T(8,128)S(1)} %get-tuple-element.56), channel_id=1, source_target_pairs={{0,64},{32,96},{64,0},{96,32},{1,65},{33,97},{65,1},{97,33},{2,66}... | collective-permute-start | bytes 393224 | tf_op jit(solution)/shard_map/ppermute | solution.py:522
  43.0 6.3 %collective-permute-start.11 = (f32[256,128]{1,0:T(8,128)S(1)}, f32[256,128]{1,0:T(8,128)S(1)}, u32[]{:S(2)}, u32[]{:S(2)}) collective-permute-start(f32[256,128]{1,0:T(8,128)S(1)} %get-tuple-element.57), channel_id=1, source_target_pairs={{0,96},{32,0},{64,32},{96,64},{1,97},{33,1},{65,33},{97,65},{2,98}... | collective-permute-start | bytes 393224 | tf_op jit(solution)/shard_map/ppermute | solution.py:522

commit v5 on v4

--- a/solution.py
+++ b/solution.py
@@ -14,6 +14,7 @@
 LONS = 24
 LATS = 128
 BLOCKS = 4
+PARTNERS = (0, 3, 2, 1)
 RECORD = 72
 STATES = 64
 GROUP = 4
@@ -21,7 +22,7 @@
 INNER = (1, 2, 3, 4)
 SLAB = 8
 SLABS = LEVELS // SLAB
-PAD = LATS + 16
+PAD = LATS + 24
 HALO = GROUP * SLABS * LATS
 
 OFF_CHIP = pl.BlockSpec(memory_space=pltpu.HBM)
@@ -63,8 +64,8 @@
 
 def in_order(pieces, target, rows):
     here = lax.axis_index("lev")
-    for shift, piece in enumerate(pieces):
-        source = lax.rem(here - shift + BLOCKS, BLOCKS)
+    for mask, piece in zip(PARTNERS, pieces):
+        source = jnp.bitwise_xor(here, mask)
         target[pl.ds(pl.multiple_of(source * rows, 8), rows), :] = piece[...]
 
 
@@ -140,8 +141,8 @@
 
 def share_out(exits, pieces, rows):
     here = lax.axis_index("lev")
-    for shift, piece in enumerate(pieces):
-        target = lax.rem(here + shift, BLOCKS)
+    for mask, piece in zip(PARTNERS, pieces):
+        target = jnp.bitwise_xor(here, mask)
         piece[...] = exits[pl.ds(pl.multiple_of(target * rows, 8), rows), :]
 
 
@@ -274,11 +275,17 @@
 
 
 def entering_of(states, start):
-    return [[states[start + 16 * n + 8 * half : start + 16 * n + 8 * half + 8, :] for n in range(4)] for half in range(2)]
+    return [[states[pl.ds(start + 16 * n + 8 * half, 8), :] for n in range(4)] for half in range(2)]
 
 
 def spread(kappa_row):
     return jnp.transpose(jnp.broadcast_to(kappa_row, (LATS, LATS)))
+
+
+def by_core(act, mate, other):
+    odd = lax.rem(lax.axis_index("col"), 2)
+    pl.when(odd == 0)(lambda: act(other, mate))
+    pl.when(odd == 1)(lambda: act(mate, other))
 
 
 def stepped(here, around, k):
@@ -289,24 +296,25 @@
     zero = jnp.zeros((8, LATS), F32)
     for block in range(blocks):
         rows[block * PAD : block * PAD + 8, :] = zero
-        rows[block * PAD + LATS + 8 : (block + 1) * PAD, :] = zero
-
-
-def edge_kernel(local, profiles, kappa, s0, s1, s2, s3, to_low, to_high, states):
+        rows[block * PAD + LATS + 8 : block * PAD + LATS + 16, :] = zero
+
+
+def edge_kernel(local, profiles, kappa, s0, s1, s2, s3, to_mate, to_other, states):
+    odd = lax.rem(lax.axis_index("col"), 2)
     in_order((s0, s1, s2, s3), states, len(EDGE) * STATES)
     profile_rows = profiles.reshape(4 * LEVELS * LONS, LATS)
-    for index, out in enumerate((to_low, to_high)):
-        lon = GROUP * EDGE[index]
-        out[HALO : HALO + 8, :] = kappa[8 * (lon // 8) : 8 * (lon // 8) + 8, :]
+    sides = ((to_mate, 1 - odd), (to_other, odd))
+    for out, index in sides:
+        out[HALO : HALO + 8, :] = kappa[pl.ds(pl.multiple_of(16 * index, 8), 8), :]
 
     def run(slab, carry):
-        for index, out in enumerate((to_low, to_high)):
+        for out, index in sides:
             for j in range(GROUP):
-                lon = GROUP * EDGE[index] + j
+                lon = GROUP * (EDGE[1] - EDGE[0]) * index + j
                 block = corrected_block(
                     lambda level, half: local[slab * SLAB + level, GROUP * index + j, 8 * half : 8 * half + 8, :],
                     lambda n, level: row(profile_rows, (n * LEVELS + slab * SLAB + level) * LONS + lon),
-                    entering_of(states, slot(EDGE, index, j) * STATES),
+                    entering_of(states, pl.multiple_of(slot(EDGE, index, j) * STATES, 8)),
                 )
                 out[pl.ds(pl.multiple_of((j * SLABS + slab) * LATS, 8), LATS), :] = jnp.transpose(block)
         return carry
@@ -327,7 +335,7 @@
     )(local, profiles, diffusivity, *pieces)
 
 
-def inner_kernel(local, profiles, kappa, to_low, to_high, s0, s1, s2, s3, out, begun, kept, spread_rows, states, buffers, made, sems):
+def inner_kernel(local, profiles, kappa, to_mate, to_other, s0, s1, s2, s3, out, begun, kept, spread_rows, states, buffers, made, sems):
     def save(slab):
         part = pl.ds(slab * SLAB * MEMBERS, SLAB * MEMBERS)
         return pltpu.make_async_copy(made.at[part], out.at[part, pl.ds(8, 8), :], sems.at[slab])
@@ -350,22 +358,25 @@
                     return ((slab * 2 + side) * 2 * SMOOTH + 2 * step + m - step) * PAD + 8
             return None
 
-        for lon in range(LONS):
-            if GROUP <= lon < LONS - GROUP:
-                block = jnp.transpose(
-                    corrected_block(
-                        lambda level, half: local[slab * SLAB + level, lon - GROUP, 8 * half : 8 * half + 8, :],
-                        lambda n, level: row(profile_rows, (n * LEVELS + slab * SLAB + level) * LONS + lon),
-                        entering_of(states, (lon - GROUP) * STATES),
-                    )
-                )
-            else:
-                sent, j = (to_low, lon) if lon < GROUP else (to_high, lon - LONS + GROUP)
-                block = sent[pl.ds(pl.multiple_of((j * SLABS + slab) * LATS, 8), LATS), :]
-            buffers[0, lon, 8 : 8 + LATS, :] = block
-            start = keep(0, lon)
-            if start is not None:
-                kept_rows[pl.ds(pl.multiple_of(start, 8), LATS), :] = block
+        for lon in range(GROUP, LONS - GROUP):
+            block = corrected_block(
+                lambda level, half: local[slab * SLAB + level, lon - GROUP, 8 * half : 8 * half + 8, :],
+                lambda n, level: row(profile_rows, (n * LEVELS + slab * SLAB + level) * LONS + lon),
+                entering_of(states, (lon - GROUP) * STATES),
+            )
+            buffers[0, lon, 8 : 8 + LATS, :] = jnp.transpose(block)
+
+        def edges(to_low, to_high):
+            for index, sent in enumerate((to_low, to_high)):
+                for j in range(GROUP):
+                    lon = GROUP * EDGE[index] + j
+                    block = sent[pl.ds(pl.multiple_of((j * SLABS + slab) * LATS, 8), LATS), :]
+                    buffers[0, lon, 8 : 8 + LATS, :] = block
+                    start = keep(0, lon)
+                    if start is not None:
+                        kept_rows[pl.ds(pl.multiple_of(start, 8), LATS), :] = block
+
+        by_core(edges, to_mate, to_other)
         for step in range(SMOOTH):
 
             def at(which, lon, offset):
@@ -389,7 +400,7 @@
                     west, here = here, east
                 return carry
 
-            lax.fori_loop(0, LATS // 8, tile, 0, unroll=2)
+            lax.fori_loop(0, LATS // 8, tile, 0, unroll=4)
         for lon in range(GROUP, LONS - GROUP):
             block = jnp.transpose(buffers[0, lon, 8 : 8 + LATS, :])
             for part in range(2 * SLAB):
@@ -407,7 +418,7 @@
     wait_all([save(slab) for slab in range(SLABS)])
 
 
-def inner_call(local, profiles, diffusivity, to_low, to_high, pieces):
+def inner_call(local, profiles, diffusivity, to_mate, to_other, pieces):
     return pl.pallas_call(
         inner_kernel,
         out_shape=[
@@ -427,10 +438,10 @@
         compiler_params=ROOM,
         cost_estimate=cost(2 * 10**8),
         name="inner",
-    )(local, profiles, diffusivity, to_low, to_high, *pieces)
-
-
-def outer_kernel(whole, begun, kept, spread_rows, low, high, out, filled, buffers, halo_spread, sems):
+    )(local, profiles, diffusivity, to_mate, to_other, *pieces)
+
+
+def outer_kernel(whole, begun, kept, spread_rows, mate, other, out, filled, buffers, halo_spread, sems):
     places = 2 * SMOOTH
 
     def saves(slab):
@@ -443,19 +454,26 @@
     rows = buffers.reshape(2 * 2 * places * PAD, LATS)
     kept_rows = kept.reshape(SLABS * 2 * 2 * SMOOTH * PAD, LATS)
     clear_pads(rows, 2 * 2 * places)
-    for side, halo in enumerate((low, high)):
-        for j in range(GROUP):
-            place = j if side == 0 else GROUP - 1 - j
-            at = HALO + (GROUP + j if side == 0 else j)
-            halo_spread[side, place] = spread(halo[at : at + 1, :])
-    filled_rows = filled.reshape(2 * LEVELS * MEMBERS * 8, LATS)
-
-    def run(slab, carry):
+
+    def spreads(low, high):
         for side, halo in enumerate((low, high)):
             for j in range(GROUP):
                 place = j if side == 0 else GROUP - 1 - j
-                block = halo[pl.ds(pl.multiple_of((j * SLABS + slab) * LATS, 8), LATS), :]
-                buffers[0, side, place, 8 : 8 + LATS, :] = block
+                at = HALO + (GROUP + j if side == 0 else j)
+                halo_spread[side, place] = spread(halo[at : at + 1, :])
+
+    by_core(spreads, mate, other)
+    filled_rows = filled.reshape(2 * LEVELS * MEMBERS * 8, LATS)
+
+    def run(slab, carry):
+        def halos(low, high):
+            for side, halo in enumerate((low, high)):
+                for j in range(GROUP):
+                    place = j if side == 0 else GROUP - 1 - j
+                    block = halo[pl.ds(pl.multiple_of((j * SLABS + slab) * LATS, 8), LATS), :]
+                    buffers[0, side, place, 8 : 8 + LATS, :] = block
+
+        by_core(halos, mate, other)
         for step in range(SMOOTH):
 
             def tile(t, carry):
@@ -483,7 +501,7 @@
                         west, here = here, east
                 return carry
 
-            lax.fori_loop(0, LATS // 8, tile, 0, unroll=2)
+            lax.fori_loop(0, LATS // 8, tile, 0, unroll=4)
         for side in range(2):
             for m in range(GROUP):
                 block = jnp.transpose(buffers[0, side, GROUP + m, 8 : 8 + LATS, :])
@@ -499,7 +517,7 @@
         wait_all(saves(slab))
 
 
-def outer_call(whole, begun, kept, spread_rows, low, high):
+def outer_call(whole, begun, kept, spread_rows, mate, other):
     return pl.pallas_call(
         outer_kernel,
         out_shape=[shape(LEVELS * MEMBERS, LONS, LATS), resident(2, LEVELS * MEMBERS, 8, LATS)],
@@ -513,23 +531,22 @@
         ],
         compiler_params=ROOM,
         name="outer",
-    )(whole, begun, kept, spread_rows, low, high)
+    )(whole, begun, kept, spread_rows, mate, other)
 
 
 def shifted(pieces):
     moved = [pieces[0]]
-    for shift in (1, 2, 3):
-        moved.append(lax.ppermute(pieces[shift], "lev", [(i, (i + shift) % BLOCKS) for i in range(BLOCKS)]))
+    for at in (1, 2, 3):
+        moved.append(lax.ppermute(pieces[at], "lev", [(i, i ^ PARTNERS[at]) for i in range(BLOCKS)]))
     return moved
 
 
-def exchanged(to_low, to_high):
+def exchanged(to_mate, to_other):
     count = lax.axis_size("col")
-    forward = [(i, i + 1) for i in range(count - 1)]
-    backward = [(b, a) for a, b in forward]
-    low = lax.ppermute(to_high, "col", forward)
-    high = lax.ppermute(to_low, "col", backward)
-    return low, high
+    both_ways = lambda first: [pair for i in range(first, count - 1, 2) for pair in ((i, i + 1), (i + 1, i))]
+    mate = lax.ppermute(to_mate, "col", both_ways(0))
+    other = lax.ppermute(to_other, "col", both_ways(1))
+    return mate, other
 
 
 def per_device(control_field, decay_rate, diffusivity):
@@ -538,10 +555,10 @@
     inner_local, *inner_pieces = inner_sweep_call(xs, rates, table)
     edge_states = shifted(solve_call(shifted(edge_pieces)))
     inner_states = shifted(solve_call(shifted(inner_pieces)))
-    to_low, to_high = edge_call(edge_local, profiles, diffusivity, edge_states)
-    low, high = exchanged(to_low, to_high)
-    whole, begun, kept, spread_rows = inner_call(inner_local, profiles, diffusivity, to_low, to_high, inner_states)
-    out, _ = outer_call(whole, begun, kept, spread_rows, low, high)
+    to_mate, to_other = edge_call(edge_local, profiles, diffusivity, edge_states)
+    mate, other = exchanged(to_mate, to_other)
+    whole, begun, kept, spread_rows = inner_call(inner_local, profiles, diffusivity, to_mate, to_other, inner_states)
+    out, _ = outer_call(whole, begun, kept, spread_rows, mate, other)
     return out.reshape(control_field.shape)
 
 

time: 63 us -> 59.1 us (0.938)
  the two profiles are of different devices: /device:TPU:64 before, /device:TPU:38 now
where the time goes in v5:
time: 59.1 us; the launch traced here: 59 us
  waiting for transfers between devices  21.5 us (36%)
  starting transfers between devices  19.6 us (33%)
  Pallas kernels  17.8 us (30%)
    ppermute x12, waiting for transfers between devices, shifted(): lax.ppermute(pieces[at], 'lev', [(i, i ^ PARTNERS[at]) for i in range(BLO...  21.5 us
    ppermute x12, starting transfers between devices, shifted(): lax.ppermute(pieces[at], 'lev', [(i, i ^ PARTNERS[at]) for i in range(BLO...  16.7 us
    pallas_call x1, Pallas kernels, inner_call(): pl.pallas_call(inner_kernel, out_shape=[shape(LEVELS * MEMBERS, LONS, LAT...  8.22 us
    pallas_call x1, Pallas kernels, outer_call(): pl.pallas_call(outer_kernel, out_shape=[shape(LEVELS * MEMBERS, LONS, LAT...  4.25 us
    ppermute x1, starting transfers between devices, exchanged(): other = lax.ppermute(to_other, 'col', both_ways(1))  2.83 us
    pallas_call x1, Pallas kernels, edge_sweep_call(): pl.pallas_call(edge_sweep_kernel, out_shape=outs, in_specs=[OFF_CHIP] * 2...  2.53 us
    pallas_call x1, Pallas kernels, inner_sweep_call(): pl.pallas_call(inner_sweep_kernel, out_shape=outs, in_specs=[ON_CHIP] * 3...  1.75 us
  transfers between devices with their start and end apart: 14, of which 9 were waited for; matrix products, arithmetic and copies ran while one was open for 0% of the time, Pallas kernels for 17%

profile of v5, /device:TPU:38, one launch (start us, length us, event | category | flops | bytes accessed | tf_op | source)
XLA Modules:
  0.0 59.0 jit_solution(6847561300807583910)
XLA Ops:
  0.0 0.0 copy-start
  0.0 2.5 %edge_sweeps.1 = (f32[24,8,16,128]{3,2,1,0:T(8,128)S(1)}, f32[144,128]{1,0:T(8,128)S(1)}, f32[144,128]{1,0:T(8,128)S(1)}, f32[144,128]{1,0:T(8,128)S(1)}, f32[14...) custom-call(f32[384,24,128]{2,1,0:T(8,128)} %bitcast.2, ...), custom_call_target="tpu_custom_call" | custom-call | flops 30000000 | bytes 1000000 | tf_op jit(solution)/shard_map/edge_sweeps/pallas_call | solution.py:170
  2.5 3.1 %collective-permute-start = (f32[144,128]{1,0:T(8,128)S(1)}, f32[144,128]{1,0:T(8,128)S(1)}, u32[]{:S(2)}, u32[]{:S(2)}) collective-permute-start(f32[144,128]{1,0:T(8,128)S(1)} %get-tuple-element.41), channel_id=1, source_target_pairs={{0,96},{32,64},{64,32},{96,0},{1,97},{33,65},{65,33},{97,1},{2,98}... | collective-permute-start | bytes 221192 | tf_op jit(solution)/shard_map/ppermute | solution.py:540
  5.6 0.6 %collective-permute-start.1 = (f32[144,128]{1,0:T(8,128)S(1)}, f32[144,128]{1,0:T(8,128)S(1)}, u32[]{:S(2)}, u32[]{:S(2)}) collective-permute-start(f32[144,128]{1,0:T(8,128)S(1)} %get-tuple-element.42), channel_id=1, source_target_pairs={{0,64},{32,96},{64,0},{96,32},{1,65},{33,97},{65,1},{97,33},{2,66}... | collective-permute-start | bytes 221192 | tf_op jit(solution)/shard_map/ppermute | solution.py:540
  6.3 0.5 collective-permute-start.2
  6.7 1.8 %collective-permute-done.refs_1_ = f32[144,128]{1,0:T(8,128)S(1)} collective-permute-done((f32[144,128]{1,0:T(8,128)S(1)}, f32[144,128]{1,0:T(8,128)S(1)}, u32[]{:S(2)}, u32[]{:S(2)}) %collective-permute-start) | collective-permute-done | bytes 73760 | tf_op jit(solution)/shard_map/ppermute | solution.py:540
  8.5 3.1 %collective-permute-done.1.refs_2_ = f32[144,128]{1,0:T(8,128)S(1)} collective-permute-done((f32[144,128]{1,0:T(8,128)S(1)}, f32[144,128]{1,0:T(8,128)S(1)}, u32[]{:S(2)}, u32[]{:S(2)}) %collective-permute-start.1) | collective-permute-done | bytes 73760 | tf_op jit(solution)/shard_map/ppermute | solution.py:540
  11.7 0.0 collective-permute-done.2.refs_3_
  11.7 0.1 shard_map.37
  11.8 1.4 %collective-permute-start.3 = (f32[128,128]{1,0:T(8,128)S(1)}, f32[128,128]{1,0:T(8,128)S(1)}, u32[]{:S(2)}, u32[]{:S(2)}) collective-permute-start(f32[128,128]{1,0:T(8,128)S(1)} %get-tuple-element.45), channel_id=1, source_target_pairs={{0,96},{32,64},{64,32},{96,0},{1,97},{33,65},{65,33},{97,1},{2,98}... | collective-permute-start | bytes 196616 | tf_op jit(solution)/shard_map/ppermute | solution.py:540
  13.2 1.1 %collective-permute-start.4 = (f32[128,128]{1,0:T(8,128)S(1)}, f32[128,128]{1,0:T(8,128)S(1)}, u32[]{:S(2)}, u32[]{:S(2)}) collective-permute-start(f32[128,128]{1,0:T(8,128)S(1)} %get-tuple-element.46), channel_id=1, source_target_pairs={{0,64},{32,96},{64,0},{96,32},{1,65},{33,97},{65,1},{97,33},{2,66}... | collective-permute-start | bytes 196616 | tf_op jit(solution)/shard_map/ppermute | solution.py:540
  14.3 1.7 %collective-permute-start.5 = (f32[128,128]{1,0:T(8,128)S(1)}, f32[128,128]{1,0:T(8,128)S(1)}, u32[]{:S(2)}, u32[]{:S(2)}) collective-permute-start(f32[128,128]{1,0:T(8,128)S(1)} %get-tuple-element.47), channel_id=1, source_target_pairs={{0,32},{32,0},{64,96},{96,64},{1,33},{33,1},{65,97},{97,65},{2,34}... | collective-permute-start | bytes 196616 | tf_op jit(solution)/shard_map/ppermute | solution.py:540
  16.0 1.4 %collective-permute-done.3.s1 = f32[128,128]{1,0:T(8,128)S(1)} collective-permute-done((f32[128,128]{1,0:T(8,128)S(1)}, f32[128,128]{1,0:T(8,128)S(1)}, u32[]{:S(2)}, u32[]{:S(2)}) %collective-permute-start.3) | collective-permute-done | bytes 65568 | tf_op jit(solution)/shard_map/ppermute | solution.py:540
  17.3 1.6 %collective-permute-done.4.s2 = f32[128,128]{1,0:T(8,128)S(1)} collective-permute-done((f32[128,128]{1,0:T(8,128)S(1)}, f32[128,128]{1,0:T(8,128)S(1)}, u32[]{:S(2)}, u32[]{:S(2)}) %collective-permute-start.4) | collective-permute-done | bytes 65568 | tf_op jit(solution)/shard_map/ppermute | solution.py:540
  19.0 0.0 collective-permute-done.5.s3
  19.0 0.0 copy-done
  19.0 0.7 %edges.1 = (f32[1544,128]{1,0:T(8,128)S(1)}, f32[1544,128]{1,0:T(8,128)S(1)}) custom-call(f32[24,8,16,128]{3,2,1,0:T(8,128)S(1)} %get-tuple-element.39.local, f32[4,24,24,128]{3,2,1,0:T(8,128)S(1)} %get-tuple-element.38.profiles, f32[24,128]{1,0:T(8,128)S(1)} %copy-done, f32[128,128]{1,0:T(8,128)S(1)} %get-tuple-element.44.s0, ...), custom_call_target="tpu_custom_call" | custom-call | flops 10000000 | bytes 1000000 | tf_op jit(solution)/shard_map/edges/pallas_call | solution.py:326
  19.7 0.1 collective-permute-start.12
  19.8 2.8 %collective-permute-start.13 = (f32[1544,128]{1,0:T(8,128)S(1)}, f32[1544,128]{1,0:T(8,128)S(1)}, u32[]{:S(2)}, u32[]{:S(2)}) collective-permute-start(f32[1544,128]{1,0:T(8,128)S(1)} %get-tuple-element.49.to_other), channel_id=1, source_target_pairs={{1,2},{2,1},{3,4},{4,3},{5,6},{6,5},{7,8},{8,7},{9,10},{10,9},{11,... | collective-permute-start | bytes 2371592 | tf_op jit(solution)/shard_map/ppermute | solution.py:548
  22.6 1.8 %inner_sweeps.1 = (f32[24,16,16,128]{3,2,1,0:T(8,128)S(1)}, f32[288,128]{1,0:T(8,128)S(1)}, f32[288,128]{1,0:T(8,128)S(1)}, f32[288,128]{1,0:T(8,128)S(1)}, f32[288,128]{1,0:T(8,128)S(1)}) custom-call(f32[384,24,128]{2,1,0:T(8,128)S(1)} %get-tuple-element.34.xs, f32[24,24,128]{2,1,0:T(8,128)S(1)} %get-tuple-element.35.rates, ...), custom_call_target="tpu_custom_call" | custom-call | flops 50000000 | bytes 1000000 | tf_op jit(solution)/shard_map/inner_sweeps/pallas_call | solution.py:194
  24.4 2.0 %collective-permute-start.6 = (f32[288,128]{1,0:T(8,128)S(1)}, f32[288,128]{1,0:T(8,128)S(1)}, u32[]{:S(2)}, u32[]{:S(2)}) collective-permute-start(f32[288,128]{1,0:T(8,128)S(1)} %get-tuple-element.51), channel_id=1, source_target_pairs={{0,96},{32,64},{64,32},{96,0},{1,97},{33,65},{65,33},{97,1},{2,98}... | collective-permute-start | bytes 442376 | tf_op jit(solution)/shard_map/ppermute | solution.py:540
  26.3 1.4 %collective-permute-start.7 = (f32[288,128]{1,0:T(8,128)S(1)}, f32[288,128]{1,0:T(8,128)S(1)}, u32[]{:S(2)}, u32[]{:S(2)}) collective-permute-start(f32[288,128]{1,0:T(8,128)S(1)} %get-tuple-element.52), channel_id=1, source_target_pairs={{0,64},{32,96},{64,0},{96,32},{1,65},{33,97},{65,1},{97,33},{2,66}... | collective-permute-start | bytes 442376 | tf_op jit(solution)/shard_map/ppermute | solution.py:540
  27.8 0.8 %collective-permute-start.8 = (f32[288,128]{1,0:T(8,128)S(1)}, f32[288,128]{1,0:T(8,128)S(1)}, u32[]{:S(2)}, u32[]{:S(2)}) collective-permute-start(f32[288,128]{1,0:T(8,128)S(1)} %get-tuple-element.53), channel_id=1, source_target_pairs={{0,32},{32,0},{64,96},{96,64},{1,33},{33,1},{65,97},{97,65},{2,34}... | collective-permute-start | bytes 442376 | tf_op jit(solution)/shard_map/ppermute | solution.py:540
  28.6 6.9 %collective-permute-done.6.refs_1_ = f32[288,128]{1,0:T(8,128)S(1)} collective-permute-done((f32[288,128]{1,0:T(8,128)S(1)}, f32[288,128]{1,0:T(8,128)S(1)}, u32[]{:S(2)}, u32[]{:S(2)}) %collective-permute-start.6) | collective-permute-done | bytes 147488 | tf_op jit(solution)/shard_map/ppermute | solution.py:540
  35.5 0.0 collective-permute-done.7.refs_2_
  35.5 0.7 %collective-permute-done.8.refs_3_ = f32[288,128]{1,0:T(8,128)S(1)} collective-permute-done((f32[288,128]{1,0:T(8,128)S(1)}, f32[288,128]{1,0:T(8,128)S(1)}, u32[]{:S(2)}, u32[]{:S(2)}) %collective-permute-start.8) | collective-permute-done | bytes 147488 | tf_op jit(solution)/shard_map/ppermute | solution.py:540
  36.2 0.2 shard_map.38
  36.5 2.0 %collective-permute-start.9 = (f32[256,128]{1,0:T(8,128)S(1)}, f32[256,128]{1,0:T(8,128)S(1)}, u32[]{:S(2)}, u32[]{:S(2)}) collective-permute-start(f32[256,128]{1,0:T(8,128)S(1)} %get-tuple-element.55), channel_id=1, source_target_pairs={{0,96},{32,64},{64,32},{96,0},{1,97},{33,65},{65,33},{97,1},{2,98}... | collective-permute-start | bytes 393224 | tf_op jit(solution)/shard_map/ppermute | solution.py:540
  38.4 1.4 %collective-permute-start.10 = (f32[256,128]{1,0:T(8,128)S(1)}, f32[256,128]{1,0:T(8,128)S(1)}, u32[]{:S(2)}, u32[]{:S(2)}) collective-permute-start(f32[256,128]{1,0:T(8,128)S(1)} %get-tuple-element.56), channel_id=1, source_target_pairs={{0,64},{32,96},{64,0},{96,32},{1,65},{33,97},{65,1},{97,33},{2,66}... | collective-permute-start | bytes 393224 | tf_op jit(solution)/shard_map/ppermute | solution.py:540
  39.8 0.8 %collective-permute-start.11 = (f32[256,128]{1,0:T(8,128)S(1)}, f32[256,128]{1,0:T(8,128)S(1)}, u32[]{:S(2)}, u32[]{:S(2)}) collective-permute-start(f32[256,128]{1,0:T(8,128)S(1)} %get-tuple-element.57), channel_id=1, source_target_pairs={{0,32},{32,0},{64,96},{96,64},{1,33},{33,1},{65,97},{97,65},{2,34}... | collective-permute-start | bytes 393224 | tf_op jit(solution)/shard_map/ppermute | solution.py:540
  40.6 4.8 %collective-permute-done.9.s1 = f32[256,128]{1,0:T(8,128)S(1)} collective-permute-done((f32[256,128]{1,0:T(8,128)S(1)}, f32[256,128]{1,0:T(8,128)S(1)}, u32[]{:S(2)}, u32[]{:S(2)}) %collective-permute-start.9) | collective-permute-done | bytes 131104 | tf_op jit(solution)/shard_map/ppermute | solution.py:540
  45.4 0.9 %collective-permute-done.10.s2 = f32[256,128]{1,0:T(8,128)S(1)} collective-permute-done((f32[256,128]{1,0:T(8,128)S(1)}, f32[256,128]{1,0:T(8,128)S(1)}, u32[]{:S(2)}, u32[]{:S(2)}) %collective-permute-start.10) | collective-permute-done | bytes 131104 | tf_op jit(solution)/shard_map/ppermute | solution.py:540
  46.3 0.2 collective-permute-done.11.s3
  46.5 8.2 %inner.1 = (f32[384,24,128]{2,1,0:T(8,128)}, f32[2,384,8,128]{3,2,1,0:T(8,128)S(1)}, f32[3,2,8,152,128]{4,3,2,1,0:T(8,128)S(1)}, f32[24,128,128]{2,1,0:T(8,128)S(1)}) custom-call(f32[24,16,16,128]{3,2,1,0:T(8,128)S(1)} %get-tuple-element.37.local, f32[4,24,24,128]{3,2,1,0:T(8,128)S(1)} %get-tuple-element.38.profiles, f32[24,128]{1,0:T(8,128)S(1)} %copy-done, ...), custom_call_target="tpu_custom_call" | custom-call | flops 200000000 | bytes 1000000 | tf_op jit(solution)/shard_map/inner/pallas_call | solution.py:422
  54.7 0.0 collective-permute-done.12.mate
  54.7 0.0 collective-permute-done.13.other
  54.7 4.2 %outer.1 = (f32[384,24,128]{2,1,0:T(8,128)}, f32[2,384,8,128]{3,2,1,0:T(8,128)S(1)}) custom-call(f32[384,24,128]{2,1,0:T(8,128)} %get-tuple-element.58.whole, f32[2,384,8,128]{3,2,1,0:T(8,128)S(1)} %get-tuple-element.59.begun, f32[3,2,8,152,128]{4,3,2,1,0:T(8,128)S(1)} %get-tuple-element.60.kept, ...), custom_call_target="tpu_custom_call", output_to_operand_aliasing={{0}: (0, {}), {1}: (1, {})} | custom-call | tf_op jit(solution)/shard_map/outer/pallas_call | solution.py:521
Async XLA Ops:
  0.0 19.0 %copy-start = (f32[24,128]{1,0:T(8,128)S(1)}, f32[24,128]{1,0:T(8,128)}, u32[]{:S(2)}) copy-start(f32[24,128]{1,0:T(8,128)} %kappa.3) | copy-start | bytes 36868
  2.5 6.0 %collective-permute-start = (f32[144,128]{1,0:T(8,128)S(1)}, f32[144,128]{1,0:T(8,128)S(1)}, u32[]{:S(2)}, u32[]{:S(2)}) collective-permute-start(f32[144,128]{1,0:T(8,128)S(1)} %get-tuple-element.41), channel_id=1, source_target_pairs={{0,96},{32,64},{64,32},{96,0},{1,97},{33,65},{65,33},{97,1},{2,98}... | collective-permute-start | bytes 221192 | tf_op jit(solution)/shard_map/ppermute | solution.py:540
  5.6 6.0 %collective-permute-start.1 = (f32[144,128]{1,0:T(8,128)S(1)}, f32[144,128]{1,0:T(8,128)S(1)}, u32[]{:S(2)}, u32[]{:S(2)}) collective-permute-start(f32[144,128]{1,0:T(8,128)S(1)} %get-tuple-element.42), channel_id=1, source_target_pairs={{0,64},{32,96},{64,0},{96,32},{1,65},{33,97},{65,1},{97,33},{2,66}... | collective-permute-start | bytes 221192 | tf_op jit(solution)/shard_map/ppermute | solution.py:540
  6.3 5.4 %collective-permute-start.2 = (f32[144,128]{1,0:T(8,128)S(1)}, f32[144,128]{1,0:T(8,128)S(1)}, u32[]{:S(2)}, u32[]{:S(2)}) collective-permute-start(f32[144,128]{1,0:T(8,128)S(1)} %get-tuple-element.43), channel_id=1, source_target_pairs={{0,32},{32,0},{64,96},{96,64},{1,33},{33,1},{65,97},{97,65},{2,34}... | collective-permute-start | bytes 221192 | tf_op jit(solution)/shard_map/ppermute | solution.py:540
  11.8 5.6 %collective-permute-start.3 = (f32[128,128]{1,0:T(8,128)S(1)}, f32[128,128]{1,0:T(8,128)S(1)}, u32[]{:S(2)}, u32[]{:S(2)}) collective-permute-start(f32[128,128]{1,0:T(8,128)S(1)} %get-tuple-element.45), channel_id=1, source_target_pairs={{0,96},{32,64},{64,32},{96,0},{1,97},{33,65},{65,33},{97,1},{2,98}... | collective-permute-start | bytes 196616 | tf_op jit(solution)/shard_map/ppermute | solution.py:540
  13.2 5.8 %collective-permute-start.4 = (f32[128,128]{1,0:T(8,128)S(1)}, f32[128,128]{1,0:T(8,128)S(1)}, u32[]{:S(2)}, u32[]{:S(2)}) collective-permute-start(f32[128,128]{1,0:T(8,128)S(1)} %get-tuple-element.46), channel_id=1, source_target_pairs={{0,64},{32,96},{64,0},{96,32},{1,65},{33,97},{65,1},{97,33},{2,66}... | collective-permute-start | bytes 196616 | tf_op jit(solution)/shard_map/ppermute | solution.py:540
  14.3 4.7 %collective-permute-start.5 = (f32[128,128]{1,0:T(8,128)S(1)}, f32[128,128]{1,0:T(8,128)S(1)}, u32[]{:S(2)}, u32[]{:S(2)}) collective-permute-start(f32[128,128]{1,0:T(8,128)S(1)} %get-tuple-element.47), channel_id=1, source_target_pairs={{0,32},{32,0},{64,96},{96,64},{1,33},{33,1},{65,97},{97,65},{2,34}... | collective-permute-start | bytes 196616 | tf_op jit(solution)/shard_map/ppermute | solution.py:540
  19.7 35.0 %collective-permute-start.12 = (f32[1544,128]{1,0:T(8,128)S(1)}, f32[1544,128]{1,0:T(8,128)S(1)}, u32[]{:S(2)}, u32[]{:S(2)}) collective-permute-start(f32[1544,128]{1,0:T(8,128)S(1)} %get-tuple-element.48.to_mate), channel_id=1, source_target_pairs={{0,1},{1,0},{2,3},{3,2},{4,5},{5,4},{6,7},{7,6},{8,9},{9,8},{10,11... | collective-permute-start | bytes 2371592 | tf_op jit(solution)/shard_map/ppermute | solution.py:547
  19.8 34.9 %collective-permute-start.13 = (f32[1544,128]{1,0:T(8,128)S(1)}, f32[1544,128]{1,0:T(8,128)S(1)}, u32[]{:S(2)}, u32[]{:S(2)}) collective-permute-start(f32[1544,128]{1,0:T(8,128)S(1)} %get-tuple-element.49.to_other), channel_id=1, source_target_pairs={{1,2},{2,1},{3,4},{4,3},{5,6},{6,5},{7,8},{8,7},{9,10},{10,9},{11,... | collective-permute-start | bytes 2371592 | tf_op jit(solution)/shard_map/ppermute | solution.py:548
  24.4 11.1 %collective-permute-start.6 = (f32[288,128]{1,0:T(8,128)S(1)}, f32[288,128]{1,0:T(8,128)S(1)}, u32[]{:S(2)}, u32[]{:S(2)}) collective-permute-start(f32[288,128]{1,0:T(8,128)S(1)} %get-tuple-element.51), channel_id=1, source_target_pairs={{0,96},{32,64},{64,32},{96,0},{1,97},{33,65},{65,33},{97,1},{2,98}... | collective-permute-start | bytes 442376 | tf_op jit(solution)/shard_map/ppermute | solution.py:540
  26.3 9.1 %collective-permute-start.7 = (f32[288,128]{1,0:T(8,128)S(1)}, f32[288,128]{1,0:T(8,128)S(1)}, u32[]{:S(2)}, u32[]{:S(2)}) collective-permute-start(f32[288,128]{1,0:T(8,128)S(1)} %get-tuple-element.52), channel_id=1, source_target_pairs={{0,64},{32,96},{64,0},{96,32},{1,65},{33,97},{65,1},{97,33},{2,66}... | collective-permute-start | bytes 442376 | tf_op jit(solution)/shard_map/ppermute | solution.py:540
  27.8 8.5 %collective-permute-start.8 = (f32[288,128]{1,0:T(8,128)S(1)}, f32[288,128]{1,0:T(8,128)S(1)}, u32[]{:S(2)}, u32[]{:S(2)}) collective-permute-start(f32[288,128]{1,0:T(8,128)S(1)} %get-tuple-element.53), channel_id=1, source_target_pairs={{0,32},{32,0},{64,96},{96,64},{1,33},{33,1},{65,97},{97,65},{2,34}... | collective-permute-start | bytes 442376 | tf_op jit(solution)/shard_map/ppermute | solution.py:540
  36.5 8.9 %collective-permute-start.9 = (f32[256,128]{1,0:T(8,128)S(1)}, f32[256,128]{1,0:T(8,128)S(1)}, u32[]{:S(2)}, u32[]{:S(2)}) collective-permute-start(f32[256,128]{1,0:T(8,128)S(1)} %get-tuple-element.55), channel_id=1, source_target_pairs={{0,96},{32,64},{64,32},{96,0},{1,97},{33,65},{65,33},{97,1},{2,98}... | collective-permute-start | bytes 393224 | tf_op jit(solution)/shard_map/ppermute | solution.py:540
  38.4 7.9 %collective-permute-start.10 = (f32[256,128]{1,0:T(8,128)S(1)}, f32[256,128]{1,0:T(8,128)S(1)}, u32[]{:S(2)}, u32[]{:S(2)}) collective-permute-start(f32[256,128]{1,0:T(8,128)S(1)} %get-tuple-element.56), channel_id=1, source_target_pairs={{0,64},{32,96},{64,0},{96,32},{1,65},{33,97},{65,1},{97,33},{2,66}... | collective-permute-start | bytes 393224 | tf_op jit(solution)/shard_map/ppermute | solution.py:540
  39.8 6.6 %collective-permute-start.11 = (f32[256,128]{1,0:T(8,128)S(1)}, f32[256,128]{1,0:T(8,128)S(1)}, u32[]{:S(2)}, u32[]{:S(2)}) collective-permute-start(f32[256,128]{1,0:T(8,128)S(1)} %get-tuple-element.57), channel_id=1, source_target_pairs={{0,32},{32,0},{64,96},{96,64},{1,33},{33,1},{65,97},{97,65},{2,34}... | collective-permute-start | bytes 393224 | tf_op jit(solution)/shard_map/ppermute | solution.py:540

commit v6 on v5

--- a/solution.py
+++ b/solution.py
@@ -18,8 +18,9 @@
 RECORD = 72
 STATES = 64
 GROUP = 4
-EDGE = (0, 5)
-INNER = (1, 2, 3, 4)
+EDGE = ((0, 1, 2, 3), (20, 21, 22, 23), (4, 5, 18, 19))
+INNER = ((6, 7, 8, 9), (10, 11, 12, 13), (14, 15, 16, 17))
+SENT = 2
 SLAB = 8
 SLABS = LEVELS // SLAB
 PAD = LATS + 24
@@ -48,7 +49,7 @@
 
 
 def slot(groups, index, j):
-    return 2 * j + index if groups == EDGE else GROUP * index + j
+    return len(groups) * j + index if groups == EDGE else GROUP * index + j
 
 
 def start_all(copies):
@@ -101,17 +102,17 @@
     weights = rates.reshape(LEVELS * LONS, LATS)
 
     def run(index, carry):
-        lon = GROUP * (groups[0] + index * (groups[1] - groups[0]))
+        lons = groups[index] if isinstance(index, int) else [groups[0][0] + GROUP * index + j for j in range(GROUP)]
         for number in range(4):
             order = range(LEVELS) if number % 2 == 0 else range(LEVELS - 1, -1, -1)
             state = {}
             for level in order:
                 for j in range(GROUP):
-                    weight = row(weights, level * LONS + lon + j)
+                    weight = row(weights, level * LONS + lons[j])
                     rest = 1.0 - weight
                     for half in range(2):
                         if number == 0:
-                            start = (level * MEMBERS + 8 * half) * LONS + lon + j
+                            start = (level * MEMBERS + 8 * half) * LONS + lons[j]
                             value = values[pl.ds(start, 8, stride=LONS), :]
                         else:
                             value = local[level, GROUP * index + j, 8 * half : 8 * half + 8, :]
@@ -127,7 +128,7 @@
 
     for index, group in enumerate(groups):
         for j in range(GROUP):
-            lon = GROUP * group + j
+            lon = group[j]
             for which in range(6):
                 record = slot(groups, index, j) * RECORD + STATES + which
                 exits[record : record + 1, :] = table[which, lon : lon + 1, :]
@@ -158,7 +159,7 @@
     for which, tiles in enumerate(responses(rates, profiles, scratch)):
         for tile, value in enumerate(tiles):
             table[which, 8 * tile : 8 * tile + 8, :] = value
-    sweep_groups(EDGE, xs, rates, table, local, exits, [loads[0].wait, loads[2].wait])
+    sweep_groups(EDGE, xs, rates, table, local, exits, [loads[0].wait, loads[2].wait, lambda: None])
     share_out(exits, (p0, p1, p2, p3), len(EDGE) * RECORD)
     loads[1].wait()
 
@@ -310,7 +311,7 @@
     def run(slab, carry):
         for out, index in sides:
             for j in range(GROUP):
-                lon = GROUP * (EDGE[1] - EDGE[0]) * index + j
+                lon = (LONS - GROUP) * index + j
                 block = corrected_block(
                     lambda level, half: local[slab * SLAB + level, GROUP * index + j, 8 * half : 8 * half + 8, :],
                     lambda n, level: row(profile_rows, (n * LEVELS + slab * SLAB + level) * LONS + lon),
@@ -335,12 +336,16 @@
     )(local, profiles, diffusivity, *pieces)
 
 
-def inner_kernel(local, profiles, kappa, to_mate, to_other, s0, s1, s2, s3, out, begun, kept, spread_rows, states, buffers, made, sems):
+def inner_kernel(local, edge_local, profiles, kappa, to_mate, to_other, *refs):
+    pieces, edge_pieces, refs = refs[:4], refs[4:8], refs[8:]
+    out, begun, kept, spread_rows, states, edge_states, buffers, made, sems = refs
+
     def save(slab):
         part = pl.ds(slab * SLAB * MEMBERS, SLAB * MEMBERS)
         return pltpu.make_async_copy(made.at[part], out.at[part, pl.ds(8, 8), :], sems.at[slab])
 
-    in_order((s0, s1, s2, s3), states, len(INNER) * STATES)
+    in_order(pieces, states, len(INNER) * STATES)
+    in_order(edge_pieces, edge_states, len(EDGE) * STATES)
     rows = buffers.reshape(2 * LONS * PAD, LATS)
     kept_rows = kept.reshape(SLABS * 2 * 2 * SMOOTH * PAD, LATS)
     clear_pads(rows, 2 * LONS)
@@ -359,17 +364,23 @@
             return None
 
         for lon in range(GROUP, LONS - GROUP):
+            if lon in EDGE[SENT]:
+                j = EDGE[SENT].index(lon)
+                source, at, entering = edge_local, SENT * GROUP + j, entering_of(edge_states, slot(EDGE, SENT, j) * STATES)
+            else:
+                at = lon - INNER[0][0]
+                source, entering = local, entering_of(states, at * STATES)
             block = corrected_block(
-                lambda level, half: local[slab * SLAB + level, lon - GROUP, 8 * half : 8 * half + 8, :],
+                lambda level, half: source[slab * SLAB + level, at, 8 * half : 8 * half + 8, :],
                 lambda n, level: row(profile_rows, (n * LEVELS + slab * SLAB + level) * LONS + lon),
-                entering_of(states, (lon - GROUP) * STATES),
+                entering,
             )
             buffers[0, lon, 8 : 8 + LATS, :] = jnp.transpose(block)
 
         def edges(to_low, to_high):
             for index, sent in enumerate((to_low, to_high)):
                 for j in range(GROUP):
-                    lon = GROUP * EDGE[index] + j
+                    lon = EDGE[index][j]
                     block = sent[pl.ds(pl.multiple_of((j * SLABS + slab) * LATS, 8), LATS), :]
                     buffers[0, lon, 8 : 8 + LATS, :] = block
                     start = keep(0, lon)
@@ -418,7 +429,7 @@
     wait_all([save(slab) for slab in range(SLABS)])
 
 
-def inner_call(local, profiles, diffusivity, to_mate, to_other, pieces):
+def inner_call(local, edge_local, profiles, diffusivity, to_mate, to_other, pieces, edge_pieces):
     return pl.pallas_call(
         inner_kernel,
         out_shape=[
@@ -427,10 +438,11 @@
             resident(SLABS, 2, 2 * SMOOTH, PAD, LATS),
             resident(LONS, LATS, LATS),
         ],
-        in_specs=[ON_CHIP] * 9,
+        in_specs=[ON_CHIP] * 14,
         out_specs=[OFF_CHIP, ON_CHIP, ON_CHIP, ON_CHIP],
         scratch_shapes=[
             pltpu.VMEM((GROUP * len(INNER) * STATES, LATS), F32),
+            pltpu.VMEM((GROUP * len(EDGE) * STATES, LATS), F32),
             pltpu.VMEM((2, LONS, PAD, LATS), F32),
             pltpu.VMEM((LEVELS * MEMBERS, 8, LATS), F32),
             pltpu.SemaphoreType.DMA((SLABS,)),
@@ -438,7 +450,7 @@
         compiler_params=ROOM,
         cost_estimate=cost(2 * 10**8),
         name="inner",
-    )(local, profiles, diffusivity, to_mate, to_other, *pieces)
+    )(local, edge_local, profiles, diffusivity, to_mate, to_other, *pieces, *edge_pieces)
 
 
 def outer_kernel(whole, begun, kept, spread_rows, mate, other, out, filled, buffers, halo_spread, sems):
@@ -544,8 +556,8 @@
 def exchanged(to_mate, to_other):
     count = lax.axis_size("col")
     both_ways = lambda first: [pair for i in range(first, count - 1, 2) for pair in ((i, i + 1), (i + 1, i))]
+    other = lax.ppermute(to_other, "col", both_ways(1))
     mate = lax.ppermute(to_mate, "col", both_ways(0))
-    other = lax.ppermute(to_other, "col", both_ways(1))
     return mate, other
 
 
@@ -557,7 +569,7 @@
     inner_states = shifted(solve_call(shifted(inner_pieces)))
     to_mate, to_other = edge_call(edge_local, profiles, diffusivity, edge_states)
     mate, other = exchanged(to_mate, to_other)
-    whole, begun, kept, spread_rows = inner_call(inner_local, profiles, diffusivity, to_mate, to_other, inner_states)
+    whole, begun, kept, spread_rows = inner_call(inner_local, edge_local, profiles, diffusivity, to_mate, to_other, inner_states, edge_states)
     out, _ = outer_call(whole, begun, kept, spread_rows, mate, other)
     return out.reshape(control_field.shape)
 

time: 59.1 us -> 57.6 us (0.975)
  the two profiles are of different devices: /device:TPU:38 before, /device:TPU:64 now
where the time goes in v6:
time: 57.6 us; the launch traced here: 56.9 us
  starting transfers between devices  21.1 us (37%)
  waiting for transfers between devices  18.4 us (32%)
  Pallas kernels  17.4 us (30%)
    ppermute x12, waiting for transfers between devices, shifted(): lax.ppermute(pieces[at], 'lev', [(i, i ^ PARTNERS[at]) for i in range(BLO...  18.3 us
    ppermute x12, starting transfers between devices, shifted(): lax.ppermute(pieces[at], 'lev', [(i, i ^ PARTNERS[at]) for i in range(BLO...  16.7 us
    pallas_call x1, Pallas kernels, inner_call(): pl.pallas_call(inner_kernel, out_shape=[shape(LEVELS * MEMBERS, LONS, LAT...  7.91 us
    ppermute x1, starting transfers between devices, exchanged(): other = lax.ppermute(to_other, 'col', both_ways(1))  4.3 us
    pallas_call x1, Pallas kernels, outer_call(): pl.pallas_call(outer_kernel, out_shape=[shape(LEVELS * MEMBERS, LONS, LAT...  4.23 us
    pallas_call x1, Pallas kernels, edge_sweep_call(): pl.pallas_call(edge_sweep_kernel, out_shape=outs, in_specs=[OFF_CHIP] * 2...  2.91 us
    pallas_call x1, Pallas kernels, inner_sweep_call(): pl.pallas_call(inner_sweep_kernel, out_shape=outs, in_specs=[ON_CHIP] * 3...  1.33 us
  transfers between devices with their start and end apart: 14, of which 10 were waited for; matrix products, arithmetic and copies ran while one was open for 0% of the time, Pallas kernels for 17%

profile of v6, /device:TPU:64, one launch (start us, length us, event | category | flops | bytes accessed | tf_op | source)
XLA Modules:
  0.0 56.9 jit_solution(17252112539599894579)
XLA Ops:
  0.0 0.0 copy-start
  0.0 2.9 %edge_sweeps.1 = (f32[24,12,16,128]{3,2,1,0:T(8,128)S(1)}, f32[216,128]{1,0:T(8,128)S(1)}, f32[216,128]{1,0:T(8,128)S(1)}, f32[216,128]{1,0:T(8,128)S(1)}, f32[2...) custom-call(f32[384,24,128]{2,1,0:T(8,128)} %bitcast.2, ...), custom_call_target="tpu_custom_call" | custom-call | flops 30000000 | bytes 1000000 | tf_op jit(solution)/shard_map/edge_sweeps/pallas_call | solution.py:171
  2.9 3.1 %collective-permute-start = (f32[216,128]{1,0:T(8,128)S(1)}, f32[216,128]{1,0:T(8,128)S(1)}, u32[]{:S(2)}, u32[]{:S(2)}) collective-permute-start(f32[216,128]{1,0:T(8,128)S(1)} %get-tuple-element.41), channel_id=1, source_target_pairs={{0,96},{32,64},{64,32},{96,0},{1,97},{33,65},{65,33},{97,1},{2,98}... | collective-permute-start | bytes 331784 | tf_op jit(solution)/shard_map/ppermute | solution.py:552
  6.0 0.6 %collective-permute-start.1 = (f32[216,128]{1,0:T(8,128)S(1)}, f32[216,128]{1,0:T(8,128)S(1)}, u32[]{:S(2)}, u32[]{:S(2)}) collective-permute-start(f32[216,128]{1,0:T(8,128)S(1)} %get-tuple-element.42), channel_id=1, source_target_pairs={{0,64},{32,96},{64,0},{96,32},{1,65},{33,97},{65,1},{97,33},{2,66}... | collective-permute-start | bytes 331784 | tf_op jit(solution)/shard_map/ppermute | solution.py:552
  6.6 0.4 collective-permute-start.2
  7.1 3.6 %collective-permute-done.refs_1_ = f32[216,128]{1,0:T(8,128)S(1)} collective-permute-done((f32[216,128]{1,0:T(8,128)S(1)}, f32[216,128]{1,0:T(8,128)S(1)}, u32[]{:S(2)}, u32[]{:S(2)}) %collective-permute-start) | collective-permute-done | bytes 110624 | tf_op jit(solution)/shard_map/ppermute | solution.py:552
  10.7 2.5 %collective-permute-done.1.refs_2_ = f32[216,128]{1,0:T(8,128)S(1)} collective-permute-done((f32[216,128]{1,0:T(8,128)S(1)}, f32[216,128]{1,0:T(8,128)S(1)}, u32[]{:S(2)}, u32[]{:S(2)}) %collective-permute-start.1) | collective-permute-done | bytes 110624 | tf_op jit(solution)/shard_map/ppermute | solution.py:552
  13.2 0.0 collective-permute-done.2.refs_3_
  13.2 0.2 shard_map.37
  13.4 1.8 %collective-permute-start.3 = (f32[192,128]{1,0:T(8,128)S(1)}, f32[192,128]{1,0:T(8,128)S(1)}, u32[]{:S(2)}, u32[]{:S(2)}) collective-permute-start(f32[192,128]{1,0:T(8,128)S(1)} %get-tuple-element.45), channel_id=1, source_target_pairs={{0,96},{32,64},{64,32},{96,0},{1,97},{33,65},{65,33},{97,1},{2,98}... | collective-permute-start | bytes 294920 | tf_op jit(solution)/shard_map/ppermute | solution.py:552
  15.2 0.7 %collective-permute-start.4 = (f32[192,128]{1,0:T(8,128)S(1)}, f32[192,128]{1,0:T(8,128)S(1)}, u32[]{:S(2)}, u32[]{:S(2)}) collective-permute-start(f32[192,128]{1,0:T(8,128)S(1)} %get-tuple-element.46), channel_id=1, source_target_pairs={{0,64},{32,96},{64,0},{96,32},{1,65},{33,97},{65,1},{97,33},{2,66}... | collective-permute-start | bytes 294920 | tf_op jit(solution)/shard_map/ppermute | solution.py:552
  15.9 1.7 %collective-permute-start.5 = (f32[192,128]{1,0:T(8,128)S(1)}, f32[192,128]{1,0:T(8,128)S(1)}, u32[]{:S(2)}, u32[]{:S(2)}) collective-permute-start(f32[192,128]{1,0:T(8,128)S(1)} %get-tuple-element.47), channel_id=1, source_target_pairs={{0,32},{32,0},{64,96},{96,64},{1,33},{33,1},{65,97},{97,65},{2,34}... | collective-permute-start | bytes 294920 | tf_op jit(solution)/shard_map/ppermute | solution.py:552
  17.6 2.6 %collective-permute-done.3.s1.refs_5_ = f32[192,128]{1,0:T(8,128)S(1)} collective-permute-done((f32[192,128]{1,0:T(8,128)S(1)}, f32[192,128]{1,0:T(8,128)S(1)}, u32[]{:S(2)}, u32[]{:S(2)}) %collective-permute-start.3) | collective-permute-done | bytes 98336 | tf_op jit(solution)/shard_map/ppermute | solution.py:552
  20.2 1.1 %collective-permute-done.4.s2.refs_6_ = f32[192,128]{1,0:T(8,128)S(1)} collective-permute-done((f32[192,128]{1,0:T(8,128)S(1)}, f32[192,128]{1,0:T(8,128)S(1)}, u32[]{:S(2)}, u32[]{:S(2)}) %collective-permute-start.4) | collective-permute-done | bytes 98336 | tf_op jit(solution)/shard_map/ppermute | solution.py:552
  21.3 0.0 collective-permute-done.5.s3.refs_7_
  21.4 0.0 copy-done
  21.4 0.7 %edges.1 = (f32[1544,128]{1,0:T(8,128)S(1)}, f32[1544,128]{1,0:T(8,128)S(1)}) custom-call(f32[24,12,16,128]{3,2,1,0:T(8,128)S(1)} %get-tuple-element.38.local.edge_local, f32[4,24,24,128]{3,2,1,0:T(8,128)S(1)} %get-tuple-element.39.profiles, f32[24,128]{1,0:T(8,128)S(1)} %copy-done, f32[192,128]{1,0:T(8,128)S(1)} %get-tuple-element.44.s0.refs_4_, ...), custom_call_target="tpu_custom_call" | custom-call | flops 10000000 | bytes 1000000 | tf_op jit(solution)/shard_map/edges/pallas_call | solution.py:327
  22.1 0.1 collective-permute-start.12
  22.2 4.3 %collective-permute-start.13 = (f32[1544,128]{1,0:T(8,128)S(1)}, f32[1544,128]{1,0:T(8,128)S(1)}, u32[]{:S(2)}, u32[]{:S(2)}) collective-permute-start(f32[1544,128]{1,0:T(8,128)S(1)} %get-tuple-element.49.to_other), channel_id=1, source_target_pairs={{1,2},{2,1},{3,4},{4,3},{5,6},{6,5},{7,8},{8,7},{9,10},{10,9},{11,... | collective-permute-start | bytes 2371592 | tf_op jit(solution)/shard_map/ppermute | solution.py:559
  26.5 1.3 %inner_sweeps.1 = (f32[24,12,16,128]{3,2,1,0:T(8,128)S(1)}, f32[216,128]{1,0:T(8,128)S(1)}, f32[216,128]{1,0:T(8,128)S(1)}, f32[216,128]{1,0:T(8,128)S(1)}, f32[216,128]{1,0:T(8,128)S(1)}) custom-call(f32[384,24,128]{2,1,0:T(8,128)S(1)} %get-tuple-element.34.xs, f32[24,24,128]{2,1,0:T(8,128)S(1)} %get-tuple-element.35.rates, ...), custom_call_target="tpu_custom_call" | custom-call | flops 50000000 | bytes 1000000 | tf_op jit(solution)/shard_map/inner_sweeps/pallas_call | solution.py:195
  27.8 1.7 %collective-permute-start.6 = (f32[216,128]{1,0:T(8,128)S(1)}, f32[216,128]{1,0:T(8,128)S(1)}, u32[]{:S(2)}, u32[]{:S(2)}) collective-permute-start(f32[216,128]{1,0:T(8,128)S(1)} %get-tuple-element.51), channel_id=1, source_target_pairs={{0,96},{32,64},{64,32},{96,0},{1,97},{33,65},{65,33},{97,1},{2,98}... | collective-permute-start | bytes 331784 | tf_op jit(solution)/shard_map/ppermute | solution.py:552
  29.5 1.3 %collective-permute-start.7 = (f32[216,128]{1,0:T(8,128)S(1)}, f32[216,128]{1,0:T(8,128)S(1)}, u32[]{:S(2)}, u32[]{:S(2)}) collective-permute-start(f32[216,128]{1,0:T(8,128)S(1)} %get-tuple-element.52), channel_id=1, source_target_pairs={{0,64},{32,96},{64,0},{96,32},{1,65},{33,97},{65,1},{97,33},{2,66}... | collective-permute-start | bytes 331784 | tf_op jit(solution)/shard_map/ppermute | solution.py:552
  30.8 1.2 %collective-permute-start.8 = (f32[216,128]{1,0:T(8,128)S(1)}, f32[216,128]{1,0:T(8,128)S(1)}, u32[]{:S(2)}, u32[]{:S(2)}) collective-permute-start(f32[216,128]{1,0:T(8,128)S(1)} %get-tuple-element.53), channel_id=1, source_target_pairs={{0,32},{32,0},{64,96},{96,64},{1,33},{33,1},{65,97},{97,65},{2,34}... | collective-permute-start | bytes 331784 | tf_op jit(solution)/shard_map/ppermute | solution.py:552
  32.0 3.3 %collective-permute-done.6.refs_1_ = f32[216,128]{1,0:T(8,128)S(1)} collective-permute-done((f32[216,128]{1,0:T(8,128)S(1)}, f32[216,128]{1,0:T(8,128)S(1)}, u32[]{:S(2)}, u32[]{:S(2)}) %collective-permute-start.6) | collective-permute-done | bytes 110624 | tf_op jit(solution)/shard_map/ppermute | solution.py:552
  35.2 0.8 %collective-permute-done.7.refs_2_ = f32[216,128]{1,0:T(8,128)S(1)} collective-permute-done((f32[216,128]{1,0:T(8,128)S(1)}, f32[216,128]{1,0:T(8,128)S(1)}, u32[]{:S(2)}, u32[]{:S(2)}) %collective-permute-start.7) | collective-permute-done | bytes 110624 | tf_op jit(solution)/shard_map/ppermute | solution.py:552
  36.1 0.1 collective-permute-done.8.refs_3_
  36.2 0.2 shard_map.38
  36.4 2.1 %collective-permute-start.10 = (f32[192,128]{1,0:T(8,128)S(1)}, f32[192,128]{1,0:T(8,128)S(1)}, u32[]{:S(2)}, u32[]{:S(2)}) collective-permute-start(f32[192,128]{1,0:T(8,128)S(1)} %get-tuple-element.56), channel_id=1, source_target_pairs={{0,64},{32,96},{64,0},{96,32},{1,65},{33,97},{65,1},{97,33},{2,66}... | collective-permute-start | bytes 294920 | tf_op jit(solution)/shard_map/ppermute | solution.py:552
  38.5 0.4 collective-permute-start.11
  38.9 1.6 %collective-permute-start.9 = (f32[192,128]{1,0:T(8,128)S(1)}, f32[192,128]{1,0:T(8,128)S(1)}, u32[]{:S(2)}, u32[]{:S(2)}) collective-permute-start(f32[192,128]{1,0:T(8,128)S(1)} %get-tuple-element.55), channel_id=1, source_target_pairs={{0,96},{32,64},{64,32},{96,0},{1,97},{33,65},{65,33},{97,1},{2,98}... | collective-permute-start | bytes 294920 | tf_op jit(solution)/shard_map/ppermute | solution.py:552
  40.6 2.0 %collective-permute-done.10.refs_2_ = f32[192,128]{1,0:T(8,128)S(1)} collective-permute-done((f32[192,128]{1,0:T(8,128)S(1)}, f32[192,128]{1,0:T(8,128)S(1)}, u32[]{:S(2)}, u32[]{:S(2)}) %collective-permute-start.10) | collective-permute-done | bytes 98336 | tf_op jit(solution)/shard_map/ppermute | solution.py:552
  42.6 0.6 collective-permute-done.11.refs_3_
  43.2 1.6 %collective-permute-done.9.refs_1_ = f32[192,128]{1,0:T(8,128)S(1)} collective-permute-done((f32[192,128]{1,0:T(8,128)S(1)}, f32[192,128]{1,0:T(8,128)S(1)}, u32[]{:S(2)}, u32[]{:S(2)}) %collective-permute-start.9) | collective-permute-done | bytes 98336 | tf_op jit(solution)/shard_map/ppermute | solution.py:552
  44.8 7.9 %inner.1 = (f32[384,24,128]{2,1,0:T(8,128)}, f32[2,384,8,128]{3,2,1,0:T(8,128)S(1)}, f32[3,2,8,152,128]{4,3,2,1,0:T(8,128)S(1)}, f32[24,128,128]{2,1,0:T(8,128)S(1)}) custom-call(f32[24,12,16,128]{3,2,1,0:T(8,128)S(1)} %get-tuple-element.37.local, f32[24,12,16,128]{3,2,1,0:T(8,128)S(1)} %get-tuple-element.38.local.edge_local, ...), custom_call_target="tpu_custom_call" | custom-call | flops 200000000 | bytes 1000000 | tf_op jit(solution)/shard_map/inner/pallas_call | solution.py:433
  52.7 0.0 collective-permute-done.12.mate
  52.7 0.0 collective-permute-done.13.other
  52.7 4.2 %outer.1 = (f32[384,24,128]{2,1,0:T(8,128)}, f32[2,384,8,128]{3,2,1,0:T(8,128)S(1)}) custom-call(f32[384,24,128]{2,1,0:T(8,128)} %get-tuple-element.58.whole, f32[2,384,8,128]{3,2,1,0:T(8,128)S(1)} %get-tuple-element.59.begun, f32[3,2,8,152,128]{4,3,2,1,0:T(8,128)S(1)} %get-tuple-element.60.kept, ...), custom_call_target="tpu_custom_call", output_to_operand_aliasing={{0}: (0, {}), {1}: (1, {})} | custom-call | tf_op jit(solution)/shard_map/outer/pallas_call | solution.py:533
Async XLA Ops:
  0.0 21.4 %copy-start = (f32[24,128]{1,0:T(8,128)S(1)}, f32[24,128]{1,0:T(8,128)}, u32[]{:S(2)}) copy-start(f32[24,128]{1,0:T(8,128)} %kappa.3) | copy-start | bytes 36868
  2.9 7.8 %collective-permute-start = (f32[216,128]{1,0:T(8,128)S(1)}, f32[216,128]{1,0:T(8,128)S(1)}, u32[]{:S(2)}, u32[]{:S(2)}) collective-permute-start(f32[216,128]{1,0:T(8,128)S(1)} %get-tuple-element.41), channel_id=1, source_target_pairs={{0,96},{32,64},{64,32},{96,0},{1,97},{33,65},{65,33},{97,1},{2,98}... | collective-permute-start | bytes 331784 | tf_op jit(solution)/shard_map/ppermute | solution.py:552
  6.0 7.2 %collective-permute-start.1 = (f32[216,128]{1,0:T(8,128)S(1)}, f32[216,128]{1,0:T(8,128)S(1)}, u32[]{:S(2)}, u32[]{:S(2)}) collective-permute-start(f32[216,128]{1,0:T(8,128)S(1)} %get-tuple-element.42), channel_id=1, source_target_pairs={{0,64},{32,96},{64,0},{96,32},{1,65},{33,97},{65,1},{97,33},{2,66}... | collective-permute-start | bytes 331784 | tf_op jit(solution)/shard_map/ppermute | solution.py:552
  6.6 6.6 %collective-permute-start.2 = (f32[216,128]{1,0:T(8,128)S(1)}, f32[216,128]{1,0:T(8,128)S(1)}, u32[]{:S(2)}, u32[]{:S(2)}) collective-permute-start(f32[216,128]{1,0:T(8,128)S(1)} %get-tuple-element.43), channel_id=1, source_target_pairs={{0,32},{32,0},{64,96},{96,64},{1,33},{33,1},{65,97},{97,65},{2,34}... | collective-permute-start | bytes 331784 | tf_op jit(solution)/shard_map/ppermute | solution.py:552
  13.4 6.8 %collective-permute-start.3 = (f32[192,128]{1,0:T(8,128)S(1)}, f32[192,128]{1,0:T(8,128)S(1)}, u32[]{:S(2)}, u32[]{:S(2)}) collective-permute-start(f32[192,128]{1,0:T(8,128)S(1)} %get-tuple-element.45), channel_id=1, source_target_pairs={{0,96},{32,64},{64,32},{96,0},{1,97},{33,65},{65,33},{97,1},{2,98}... | collective-permute-start | bytes 294920 | tf_op jit(solution)/shard_map/ppermute | solution.py:552
  15.2 6.1 %collective-permute-start.4 = (f32[192,128]{1,0:T(8,128)S(1)}, f32[192,128]{1,0:T(8,128)S(1)}, u32[]{:S(2)}, u32[]{:S(2)}) collective-permute-start(f32[192,128]{1,0:T(8,128)S(1)} %get-tuple-element.46), channel_id=1, source_target_pairs={{0,64},{32,96},{64,0},{96,32},{1,65},{33,97},{65,1},{97,33},{2,66}... | collective-permute-start | bytes 294920 | tf_op jit(solution)/shard_map/ppermute | solution.py:552
  15.9 5.5 %collective-permute-start.5 = (f32[192,128]{1,0:T(8,128)S(1)}, f32[192,128]{1,0:T(8,128)S(1)}, u32[]{:S(2)}, u32[]{:S(2)}) collective-permute-start(f32[192,128]{1,0:T(8,128)S(1)} %get-tuple-element.47), channel_id=1, source_target_pairs={{0,32},{32,0},{64,96},{96,64},{1,33},{33,1},{65,97},{97,65},{2,34}... | collective-permute-start | bytes 294920 | tf_op jit(solution)/shard_map/ppermute | solution.py:552
  22.1 30.6 %collective-permute-start.12 = (f32[1544,128]{1,0:T(8,128)S(1)}, f32[1544,128]{1,0:T(8,128)S(1)}, u32[]{:S(2)}, u32[]{:S(2)}) collective-permute-start(f32[1544,128]{1,0:T(8,128)S(1)} %get-tuple-element.48.to_mate), channel_id=1, source_target_pairs={{0,1},{1,0},{2,3},{3,2},{4,5},{5,4},{6,7},{7,6},{8,9},{9,8},{10,11... | collective-permute-start | bytes 2371592 | tf_op jit(solution)/shard_map/ppermute | solution.py:560
  22.2 30.5 %collective-permute-start.13 = (f32[1544,128]{1,0:T(8,128)S(1)}, f32[1544,128]{1,0:T(8,128)S(1)}, u32[]{:S(2)}, u32[]{:S(2)}) collective-permute-start(f32[1544,128]{1,0:T(8,128)S(1)} %get-tuple-element.49.to_other), channel_id=1, source_target_pairs={{1,2},{2,1},{3,4},{4,3},{5,6},{6,5},{7,8},{8,7},{9,10},{10,9},{11,... | collective-permute-start | bytes 2371592 | tf_op jit(solution)/shard_map/ppermute | solution.py:559
  27.8 7.4 %collective-permute-start.6 = (f32[216,128]{1,0:T(8,128)S(1)}, f32[216,128]{1,0:T(8,128)S(1)}, u32[]{:S(2)}, u32[]{:S(2)}) collective-permute-start(f32[216,128]{1,0:T(8,128)S(1)} %get-tuple-element.51), channel_id=1, source_target_pairs={{0,96},{32,64},{64,32},{96,0},{1,97},{33,65},{65,33},{97,1},{2,98}... | collective-permute-start | bytes 331784 | tf_op jit(solution)/shard_map/ppermute | solution.py:552
  29.5 6.6 %collective-permute-start.7 = (f32[216,128]{1,0:T(8,128)S(1)}, f32[216,128]{1,0:T(8,128)S(1)}, u32[]{:S(2)}, u32[]{:S(2)}) collective-permute-start(f32[216,128]{1,0:T(8,128)S(1)} %get-tuple-element.52), channel_id=1, source_target_pairs={{0,64},{32,96},{64,0},{96,32},{1,65},{33,97},{65,1},{97,33},{2,66}... | collective-permute-start | bytes 331784 | tf_op jit(solution)/shard_map/ppermute | solution.py:552
  30.8 5.4 %collective-permute-start.8 = (f32[216,128]{1,0:T(8,128)S(1)}, f32[216,128]{1,0:T(8,128)S(1)}, u32[]{:S(2)}, u32[]{:S(2)}) collective-permute-start(f32[216,128]{1,0:T(8,128)S(1)} %get-tuple-element.53), channel_id=1, source_target_pairs={{0,32},{32,0},{64,96},{96,64},{1,33},{33,1},{65,97},{97,65},{2,34}... | collective-permute-start | bytes 331784 | tf_op jit(solution)/shard_map/ppermute | solution.py:552
  36.4 6.2 %collective-permute-start.10 = (f32[192,128]{1,0:T(8,128)S(1)}, f32[192,128]{1,0:T(8,128)S(1)}, u32[]{:S(2)}, u32[]{:S(2)}) collective-permute-start(f32[192,128]{1,0:T(8,128)S(1)} %get-tuple-element.56), channel_id=1, source_target_pairs={{0,64},{32,96},{64,0},{96,32},{1,65},{33,97},{65,1},{97,33},{2,66}... | collective-permute-start | bytes 294920 | tf_op jit(solution)/shard_map/ppermute | solution.py:552
  38.5 4.6 %collective-permute-start.11 = (f32[192,128]{1,0:T(8,128)S(1)}, f32[192,128]{1,0:T(8,128)S(1)}, u32[]{:S(2)}, u32[]{:S(2)}) collective-permute-start(f32[192,128]{1,0:T(8,128)S(1)} %get-tuple-element.57), channel_id=1, source_target_pairs={{0,32},{32,0},{64,96},{96,64},{1,33},{33,1},{65,97},{97,65},{2,34}... | collective-permute-start | bytes 294920 | tf_op jit(solution)/shard_map/ppermute | solution.py:552
  38.9 5.8 %collective-permute-start.9 = (f32[192,128]{1,0:T(8,128)S(1)}, f32[192,128]{1,0:T(8,128)S(1)}, u32[]{:S(2)}, u32[]{:S(2)}) collective-permute-start(f32[192,128]{1,0:T(8,128)S(1)} %get-tuple-element.55), channel_id=1, source_target_pairs={{0,96},{32,64},{64,32},{96,0},{1,97},{33,65},{65,33},{97,1},{2,98}... | collective-permute-start | bytes 294920 | tf_op jit(solution)/shard_map/ppermute | solution.py:552
